TPU v7x, 8 devices: a whole 2x2x1 slice. The times are simulated.
8 devices in a mesh: data: 1 (over z), dap: 8 (over y, x, core).
Axes of the slice: x: 2, y: 2, z: 1, core: 2. Of those that a mesh axis runs over, the one named last changes fastest.
Arguments:
- extra_msa: bfloat16 [3072, 256, 64], P('data', 'dap')
- extra_mask: int32 [3072, 256], P('data')
- main_msa: bfloat16 [512, 256, 256], P('data', 'dap')
- main_mask: int32 [512, 256], P('data')
- pair_act: float32 [256, 256, 128], P(('data', 'dap'))
- extra_ln_gamma: bfloat16 [64], replicated
- extra_ln_beta: bfloat16 [64], replicated
- extra_w_left: bfloat16 [64, 32], replicated
- extra_b_left: bfloat16 [32], replicated
- extra_w_right: bfloat16 [64, 32], replicated
- extra_b_right: bfloat16 [32], replicated
- extra_w_out: bfloat16 [1024, 128], replicated
- extra_b_out: bfloat16 [128], replicated
- main_ln_gamma: bfloat16 [256], replicated
- main_ln_beta: bfloat16 [256], replicated
- main_w_left: bfloat16 [256, 32], replicated
- main_b_left: bfloat16 [32], replicated
- main_w_right: bfloat16 [256, 32], replicated
- main_b_right: bfloat16 [32], replicated
- main_w_out: bfloat16 [1024, 128], replicated
- main_b_out: bfloat16 [128], replicated
Outputs:
- output 1: float32 [256, 256, 128], P(('data', 'dap'))
- output 2: bfloat16 [3072, 256, 64], P(('data', 'dap'))
- output 3: bfloat16 [512, 256, 256], P(('data', 'dap'))
All inputs are finite; a program needn't handle non-finite values.
Results may differ from a plain program's by a relative error of at most 0.00472692.
Values are sent between devices in bfloat16 or wider.
A program may use at most 1 GiB of HBM per device.

v0:
```python
import jax
import jax.numpy as jnp
from jax import lax
from jax.sharding import PartitionSpec as P

LN_EPS = 1e-5
NORM_EPS = 1e-3


def layer_norm(value_a10, ln_gamma, ln_beta):
    as_float = value_a10.astype(jnp.float32)
    row_mean = jnp.mean(as_float, axis=-1, keepdims=True)
    centered = as_float - row_mean
    row_var = jnp.mean(centered * centered, axis=-1, keepdims=True)
    scaled = centered * lax.rsqrt(row_var + LN_EPS)
    return (scaled * ln_gamma.astype(jnp.float32) + ln_beta.astype(jnp.float32)).astype(jnp.bfloat16)


def project_pair(normed, mask_float, w_left, b_left, w_right, b_right):
    hidden = w_left.shape[1]
    w_both = jnp.concatenate([w_left, w_right], axis=1)
    b_both = jnp.concatenate([b_left, b_right]).astype(jnp.float32)
    both_proj = jnp.einsum('...m,mc->...c', normed, w_both, preferred_element_type=jnp.float32)
    both_proj = ((both_proj + b_both) * mask_float[..., None]).astype(jnp.bfloat16)
    return both_proj[..., :hidden], both_proj[..., hidden:]


def pair_counts(mask_rows, mask_full):
    return jnp.einsum('si,sj->ij', mask_rows.astype(jnp.bfloat16), mask_full.astype(jnp.bfloat16), preferred_element_type=jnp.float32)


def gathered_term(value_a9, mask_full, ln_gamma, ln_beta, w_left, b_left, w_right, b_right, w_out, b_out):
    row_count = value_a9.shape[1]
    hidden = w_left.shape[1]
    row_start = lax.axis_index('dap') * row_count
    mask_rows = lax.dynamic_slice_in_dim(mask_full, row_start, row_count, axis=1)
    normed = layer_norm(value_a9, ln_gamma, ln_beta)
    left_proj, right_proj = project_pair(normed, mask_rows.astype(jnp.float32), w_left, b_left, w_right, b_right)
    right_all = lax.all_gather(right_proj, 'dap', axis=1, tiled=True)
    outer_prod = jnp.einsum('sic,sjd->ijcd', left_proj, right_all, preferred_element_type=jnp.float32).astype(jnp.bfloat16)
    pair_sum = jnp.einsum('ijcd,cdk->ijk', outer_prod, w_out.reshape(hidden, hidden, -1), preferred_element_type=jnp.float32)
    counts = pair_counts(mask_rows, mask_full)
    return (pair_sum + b_out.astype(jnp.float32)) / (NORM_EPS + counts)[:, :, None]


def reduced_term(relaid, mask_full, dap_size, ln_gamma, ln_beta, w_left, b_left, w_right, b_right, w_out, b_out):
    seq_local, res_count, array_b9 = relaid.shape
    hidden = w_left.shape[1]
    row_count = res_count // dap_size
    dap_index = lax.axis_index('dap')
    mask_local = lax.dynamic_slice_in_dim(mask_full, dap_index * seq_local, seq_local, axis=0)
    normed = layer_norm(relaid, ln_gamma, ln_beta)
    left_proj, right_proj = project_pair(normed, mask_local.astype(jnp.float32), w_left, b_left, w_right, b_right)
    left_blocks = jnp.moveaxis(left_proj.reshape(seq_local, dap_size, row_count, hidden), 1, 0)
    w_grid = w_out.reshape(hidden, hidden, -1)

    def block_partial(left_block):
        outer_prod = jnp.einsum('sic,sjd->ijcd', left_block, right_proj, preferred_element_type=jnp.float32).astype(jnp.bfloat16)
        return jnp.einsum('ijcd,cdk->ijk', outer_prod, w_grid, preferred_element_type=jnp.float32).astype(jnp.bfloat16)

    partial_sums = lax.map(block_partial, left_blocks).reshape(res_count, res_count, -1)
    reduced = lax.psum_scatter(partial_sums, 'dap', scatter_dimension=0, tiled=True)
    mask_rows = lax.dynamic_slice_in_dim(mask_full, dap_index * row_count, row_count, axis=1)
    counts = pair_counts(mask_rows, mask_full)
    return (reduced.astype(jnp.float32) + b_out.astype(jnp.float32)) / (NORM_EPS + counts)[:, :, None]


def solution(mesh):
    dap_size = mesh.shape['dap']
    value_a8 = P('data', 'dap', None)
    mask_spec = P('data', None)
    row_spec = P(('data', 'dap'), None, None)

    def local_program(extra_block, extra_mask, main_block, main_mask, pair_rows, extra_ln_gamma, extra_ln_beta, extra_w_left, extra_b_left, extra_w_right, extra_b_right, extra_w_out, extra_b_out, main_ln_gamma, main_ln_beta, main_w_left, main_b_left, main_w_right, main_b_right, main_w_out, main_b_out):
        extra_relaid = lax.all_to_all(extra_block, 'dap', 0, 1, tiled=True)
        extra_term = reduced_term(extra_relaid, extra_mask, dap_size, extra_ln_gamma, extra_ln_beta, extra_w_left, extra_b_left, extra_w_right, extra_b_right, extra_w_out, extra_b_out)
        main_term = gathered_term(main_block, main_mask, main_ln_gamma, main_ln_beta, main_w_left, main_b_left, main_w_right, main_b_right, main_w_out, main_b_out)
        main_relaid = lax.all_to_all(main_block, 'dap', 0, 1, tiled=True)
        return pair_rows + extra_term + main_term, extra_relaid, main_relaid

    in_specs = (value_a8, mask_spec, value_a8, mask_spec, row_spec) + (P(),) * 16
    sharded = jax.shard_map(local_program, mesh=mesh, in_specs=in_specs, out_specs=(row_spec, row_spec, row_spec), check_vma=False)
    return sharded
```

profile of v0, /device:TPU:0, one launch (start us, length us, event | category | flops | bytes accessed | tf_op | source)
XLA Modules:
  0.0 906.9 jit_solution(15611151170931850994)
XLA Ops:
  7.2 35.0 %copy.76 = bf16[3072,32,64]{2,1,0:T(8,128)(2,1)} copy(bf16[3072,32,64]{0,2,1:T(8,128)(2,1)} %param.23) | data formatting | bytes 25165824 | tf_op args[0]
  42.2 22.7 %reshape.113 = bf16[8,2,393216]{2,1,0:T(2,128)(2,1)} reshape(bf16[3072,32,64]{2,1,0:T(8,128)(2,1)} %copy.76) | data formatting | bytes 25165824
  100.0 142.9 %all-to-all-done = bf16[8,2,393216]{2,1,0:T(2,128)(2,1)} async-done(((bf16[8,2,393216]{2,1,0:T(2,128)(2,1)}), bf16[8,2,393216]{2,1,0:T(2,128)(2,1)}, u32[]{:S(2)}, u32[]{:S(2)}) %all-to-all-start) | async-done | bytes 12582944 | tf_op jit(solution)/shard_map/all_to_all | solution.py:75
  242.9 23.0 %reshape.114 = bf16[3072,32,64]{2,1,0:T(8,128)(2,1)} reshape(bf16[8,2,393216]{2,1,0:T(2,128)(2,1)} %all-to-all-done) | data formatting | bytes 25165824
  265.9 23.9 %copy.94 = bf16[8,384,32,64]{1,0,3,2:T(8,128)(2,1)} copy(bf16[8,384,32,64]{3,2,1,0:T(8,128)(2,1)} %bitcast.91) | data formatting | bytes 25165824 | tf_op jit(solution)/shard_map/all_to_all | solution.py:75
  305.2 31.2 %copy.78 = bf16[384,8,32,64]{0,3,2,1:T(8,128)(2,1)} copy(bf16[384,8,32,64]{3,2,0,1:T(8,128)(2,1)} %bitcast.92) | data formatting | bytes 25165824 | tf_op jit(solution)/shard_map/all_to_all | solution.py:75
  336.4 12.9 %add_convert_fusion = bf16[384,256,64]{0,2,1:T(8,128)(2,1)} fusion(f32[64]{0:T(128)S(1)} %convert_element_type.93, f32[64]{0:T(128)S(1)} %convert_element_type.92, f32[384,256]{0,1:T(8,128)S(1)} %bitcast.98, f32[384,256]{0,1:T(8,128)S(1)} %bitcast.97, bf16[384,8,32,64]{0,3,2,1:T(8,128)(2,1)} %copy.78), kind=kLoop, calls=%fused_computation.17 | loop fusion | flops 37748736 | bytes 25952768 | tf_op jit(solution)/shard_map/convert_element_type | solution.py:16
  349.3 18.1 %copy.81 = bf16[384,256,64]{1,2,0:T(8,128)(2,1)} copy(bf16[384,256,64]{0,2,1:T(8,128)(2,1)} %add_convert_fusion) | data formatting | bytes 25165824 | tf_op jit(solution)/shard_map/convert_element_type | solution.py:16
  379.2 9.8 %copy.82 = bf16[384,256,32]{0,2,1:T(8,128)(2,1)} copy(bf16[384,256,32]{1,2,0:T(8,128)(2,1)} %get-tuple-element.87) | data formatting | bytes 12582912 | tf_op jit(solution)/shard_map/slice | solution.py:25
  398.0 193.2 %while.10 = (s32[]{:T(128)}, bf16[8,32,256,128]{3,2,1,0:T(8,128)(2,1)}, bf16[8,384,32,32]{1,3,2,0:T(8,128)(2,1)}, bf16[384,256,32]{1,0,2:T(8,128)(2,1)}, bf16[32,32,128]{2,0,1:T(8,128)(2,1)S(1)}, /*index=5*/s32[]{:T(128)}) while((s32[]{:T(128)}, bf16[8,32,256,128]{3,2,1,0:T(8,128)(2,1)}, bf16[8,384,32,32]{1,3,2,0:T(8,128)(2,1)}, ...), condition=%wide.region_3.4_spmd, body=%wide.region_2.3_spmd.sunk | while | flops 8590983168 | bytes 42992708 | solution.py:61
  398.0 14.4 %fusion.56 = bf16[32,32,256,32]{2,1,3,0:T(8,128)(2,1)} fusion(bf16[384,256,32]{1,0,2:T(8,128)(2,1)} %get-tuple-element.134, bf16[8,384,32,32]{1,3,2,0:T(8,128)(2,1)} %get-tuple-element.133, s32[]{:T(128)} %get-tuple-element.125), kind=kOutput, calls=%fused_computation.3.clone.1 | convolution fusion | flops 6442450944 | bytes 23855616 | tf_op jit(solution)/shard_map/while/body/eval_jaxpr/sic,sjd->ijcd/dot_general | solution.py:58
  422.2 14.4 %fusion.56 = bf16[32,32,256,32]{2,1,3,0:T(8,128)(2,1)} fusion(bf16[384,256,32]{1,0,2:T(8,128)(2,1)} %get-tuple-element.134, bf16[8,384,32,32]{1,3,2,0:T(8,128)(2,1)} %get-tuple-element.133, s32[]{:T(128)} %get-tuple-element.125), kind=kOutput, calls=%fused_computation.3.clone.1 | convolution fusion | flops 6442450944 | bytes 23855616 | tf_op jit(solution)/shard_map/while/body/eval_jaxpr/sic,sjd->ijcd/dot_general | solution.py:58
  446.3 14.4 %fusion.56 = bf16[32,32,256,32]{2,1,3,0:T(8,128)(2,1)} fusion(bf16[384,256,32]{1,0,2:T(8,128)(2,1)} %get-tuple-element.134, bf16[8,384,32,32]{1,3,2,0:T(8,128)(2,1)} %get-tuple-element.133, s32[]{:T(128)} %get-tuple-element.125), kind=kOutput, calls=%fused_computation.3.clone.1 | convolution fusion | flops 6442450944 | bytes 23855616 | tf_op jit(solution)/shard_map/while/body/eval_jaxpr/sic,sjd->ijcd/dot_general | solution.py:58
  470.5 14.4 %fusion.56 = bf16[32,32,256,32]{2,1,3,0:T(8,128)(2,1)} fusion(bf16[384,256,32]{1,0,2:T(8,128)(2,1)} %get-tuple-element.134, bf16[8,384,32,32]{1,3,2,0:T(8,128)(2,1)} %get-tuple-element.133, s32[]{:T(128)} %get-tuple-element.125), kind=kOutput, calls=%fused_computation.3.clone.1 | convolution fusion | flops 6442450944 | bytes 23855616 | tf_op jit(solution)/shard_map/while/body/eval_jaxpr/sic,sjd->ijcd/dot_general | solution.py:58
  494.6 14.4 %fusion.56 = bf16[32,32,256,32]{2,1,3,0:T(8,128)(2,1)} fusion(bf16[384,256,32]{1,0,2:T(8,128)(2,1)} %get-tuple-element.134, bf16[8,384,32,32]{1,3,2,0:T(8,128)(2,1)} %get-tuple-element.133, s32[]{:T(128)} %get-tuple-element.125), kind=kOutput, calls=%fused_computation.3.clone.1 | convolution fusion | flops 6442450944 | bytes 23855616 | tf_op jit(solution)/shard_map/while/body/eval_jaxpr/sic,sjd->ijcd/dot_general | solution.py:58
  518.8 14.4 %fusion.56 = bf16[32,32,256,32]{2,1,3,0:T(8,128)(2,1)} fusion(bf16[384,256,32]{1,0,2:T(8,128)(2,1)} %get-tuple-element.134, bf16[8,384,32,32]{1,3,2,0:T(8,128)(2,1)} %get-tuple-element.133, s32[]{:T(128)} %get-tuple-element.125), kind=kOutput, calls=%fused_computation.3.clone.1 | convolution fusion | flops 6442450944 | bytes 23855616 | tf_op jit(solution)/shard_map/while/body/eval_jaxpr/sic,sjd->ijcd/dot_general | solution.py:58
  542.9 14.4 %fusion.56 = bf16[32,32,256,32]{2,1,3,0:T(8,128)(2,1)} fusion(bf16[384,256,32]{1,0,2:T(8,128)(2,1)} %get-tuple-element.134, bf16[8,384,32,32]{1,3,2,0:T(8,128)(2,1)} %get-tuple-element.133, s32[]{:T(128)} %get-tuple-element.125), kind=kOutput, calls=%fused_computation.3.clone.1 | convolution fusion | flops 6442450944 | bytes 23855616 | tf_op jit(solution)/shard_map/while/body/eval_jaxpr/sic,sjd->ijcd/dot_general | solution.py:58
  557.3 9.8 %bitcast_dynamic-update-slice_fusion.2 = bf16[8,32,256,128]{3,2,1,0:T(8,128)(2,1)} fusion(bf16[8,32,256,128]{3,2,1,0:T(8,128)(2,1)} %get-tuple-element.126, s32[]{:T(128)} %get-tuple-element.125, bf16[32,32,256,32]{2,1,3,0:T(8,128)(2,1)} %fusion.56, bf16[32,32,128]{2,0,1:T(8,128)(2,1)S(1)} %get-tuple-element.135), kind=kOutput, calls=%fused_computation.6.clone.1 | convolution fusion | flops 2148532224 | bytes 19137024 | tf_op jit(solution)/shard_map/while/body/eval_jaxpr/ijcd,cdk->ijk/dot_general | solution.py:59
  567.1 14.4 %fusion.56 = bf16[32,32,256,32]{2,1,3,0:T(8,128)(2,1)} fusion(bf16[384,256,32]{1,0,2:T(8,128)(2,1)} %get-tuple-element.134, bf16[8,384,32,32]{1,3,2,0:T(8,128)(2,1)} %get-tuple-element.133, s32[]{:T(128)} %get-tuple-element.125), kind=kOutput, calls=%fused_computation.3.clone.1 | convolution fusion | flops 6442450944 | bytes 23855616 | tf_op jit(solution)/shard_map/while/body/eval_jaxpr/sic,sjd->ijcd/dot_general | solution.py:58
  597.6 136.7 %all-to-all-done.1 = bf16[512,32,256]{2,1,0:T(8,128)(2,1)} async-done(((bf16[512,32,256]{2,1,0:T(8,128)(2,1)}), bf16[512,32,256]{2,1,0:T(8,128)(2,1)}, u32[]{:S(2)}, u32[]{:S(2)}) %all-to-all-start.1) | async-done | bytes 8388640 | tf_op jit(solution)/shard_map/all_to_all | solution.py:78
  742.5 18.1 %copy.89 = bf16[384,256,64]{1,2,0:T(8,128)(2,1)} copy(bf16[384,256,64]{0,2,1:T(8,128)(2,1)} %bitcast.93) | data formatting | bytes 25165824
  760.7 41.8 %convert_bitcast_fusion = bf16[32,256,32,32]{2,3,0,1:T(8,128)(2,1)} fusion(bf16[512,256,32]{0,2,1:T(8,128)(2,1)} %all-gather.2.cloned.1.call-done, bf16[512,32,64]{0,2,1:T(8,128)(2,1)S(1)} %copy-done.6), kind=kOutput, calls=%fused_computation.11 | convolution fusion | flops 8598323200 | bytes 26214400 | tf_op jit(solution)/shard_map/sic,sjd->ijcd/dot_general | solution.py:40
  802.5 84.7 %copy.87 = bf16[32,256,32,32]{1,3,2,0:T(8,128)(2,1)} copy(bf16[32,256,32,32]{2,3,0,1:T(8,128)(2,1)} %convert_bitcast_fusion) | data formatting | bytes 33554432 | tf_op jit(solution)/shard_map/convert_element_type | solution.py:40
  887.1 12.5 %fusion.25 = f32[32,256,128]{2,1,0:T(8,128)} fusion(f32[32,256,128]{2,1,0:T(8,128)} %param.27, bf16[32,256,128]{2,1,0:T(8,128)(2,1)} %reduce-scatter.2.cloned.1.call-done, bf16[32,256,32,32]{1,3,2,0:T(8,128)(2,1)} %copy.87, bf16[32,32,128,1]{2,1,0,3:T(8,128)(2,1)S(1)} %bitcast.90, f32[32,256]{1,0:T(8,128)S(1)} %convolution_add_fusion, ...), kind=kOutput, calls=%fused_computation.31 | convolution fusion | flops 2154823680 | bytes 27591680 | tf_op jit(solution)/shard_map/ijcd,cdk->ijk/dot_general | solution.py:41
  (92 shorter events, 153.6 us)
Async XLA Ops:
  7.2 880.0 %copy-start = (bf16[1024,128]{1,0:T(8,128)(2,1)S(1)}, bf16[1024,128]{1,0:T(8,128)(2,1)}, u32[]{:S(2)}) copy-start(bf16[1024,128]{1,0:T(8,128)(2,1)} %param.42) | copy-start | bytes 786436
  64.8 4.4 copy-start.2
  64.9 4.7 copy-start.12
  64.9 4.7 copy-start.13
  64.9 4.7 copy-start.14
  64.9 4.7 copy-start.15
  64.9 178.0 %all-to-all-start = ((bf16[8,2,393216]{2,1,0:T(2,128)(2,1)}), bf16[8,2,393216]{2,1,0:T(2,128)(2,1)}, u32[]{:S(2)}, u32[]{:S(2)}) async-start(bf16[8,2,393216]{2,1,0:T(2,128)(2,1)} %reshape.113), calls=%async_computation | async-start | bytes 25165824 | tf_op jit(solution)/shard_map/all_to_all | solution.py:75
  69.2 691.5 %all-gather.2.cloned.1.call-start = ((), (), s32[]{:S(2)}) async-start(), calls=%async_computation.4 | async-start | bytes 9437184 | tf_op jit(solution)/shard_map/all_gather | solution.py:39
  69.5 21.3 %copy-start.3 = (s32[512,32]{0,1:T(8,128)}, s32[512,32]{0,1:T(8,128)S(1)}, u32[]{:S(2)}) copy-start(s32[512,32]{0,1:T(8,128)S(1)} %copy.96) | copy-start | bytes 196612
  75.3 15.5 %copy-start.10 = (bf16[256,32]{0,1:T(8,128)(2,1)S(1)}, bf16[256,32]{0,1:T(8,128)(2,1)}, u32[]{:S(2)}) copy-start(bf16[256,32]{0,1:T(8,128)(2,1)} %param.40) | copy-start | bytes 49156
  75.3 15.5 %copy-start.11 = (bf16[256,32]{0,1:T(8,128)(2,1)S(1)}, bf16[256,32]{0,1:T(8,128)(2,1)}, u32[]{:S(2)}) copy-start(bf16[256,32]{0,1:T(8,128)(2,1)} %param.38) | copy-start | bytes 49156
  90.8 7.9 copy-start.16
  90.8 7.9 copy-start.17
  90.9 7.9 copy-start.7
  90.9 8.0 copy-start.18
  90.9 8.0 copy-start.19
  98.7 788.5 %reduce-scatter.2.cloned.1.call-start = ((), (), s32[]{:S(2)}) async-start(), calls=%async_computation.3 | async-start | bytes 18874368 | tf_op jit(solution)/shard_map/reduce_scatter | solution.py:62
  349.3 18.1 %copy-start.8 = (bf16[64,32]{0,1:T(8,128)(2,1)S(1)}, bf16[64,32]{0,1:T(8,128)(2,1)}, u32[]{:S(2)}) copy-start(bf16[64,32]{0,1:T(8,128)(2,1)} %param.32) | copy-start | bytes 12292
  349.3 18.1 %copy-start.9 = (bf16[64,32]{0,1:T(8,128)(2,1)S(1)}, bf16[64,32]{0,1:T(8,128)(2,1)}, u32[]{:S(2)}) copy-start(bf16[64,32]{0,1:T(8,128)(2,1)} %param.30) | copy-start | bytes 12292
  591.3 4.3 copy-start.21
  591.3 4.3 copy-start.4
  591.3 5.5 copy-start.1
  591.3 143.0 %all-to-all-start.1 = ((bf16[512,32,256]{2,1,0:T(8,128)(2,1)}), bf16[512,32,256]{2,1,0:T(8,128)(2,1)}, u32[]{:S(2)}, u32[]{:S(2)}) async-start(bf16[512,32,256]{2,1,0:T(8,128)(2,1)} %param.25), calls=%async_computation.2 | async-start | bytes 16777216 | tf_op jit(solution)/shard_map/all_to_all | solution.py:78
  742.5 18.1 %copy-start.6 = (bf16[512,32,64]{0,2,1:T(8,128)(2,1)S(1)}, bf16[512,32,64]{0,2,1:T(8,128)(2,1)}, u32[]{:S(2)}) copy-start(bf16[512,32,64]{0,2,1:T(8,128)(2,1)} %copy-done.5) | copy-start | bytes 6291460
  (2 other events, 5.6 us)
Sparse Core Ops, SparseCore 0:
  98.8 115.4 all-gather.1
  591.4 171.4 reduce-scatter.1
where the time goes:
time: 921 us; the launch traced here: 907 us
  local copies, waits for them, and re-layouts  292 us (32%)
  waiting for transfers between devices  280 us (30%)
  matrix products  261 us (28%)
  other arithmetic  50.3 us (5%)
  between operations  14.9 us (2%)
    all_to_all x1, waiting for transfers between devices, local_program(): extra_relaid = lax.all_to_all(extra_block, 'dap', 0, 1, tiled=True)  143 us
    all_to_all x1, waiting for transfers between devices, local_program(): main_relaid = lax.all_to_all(main_block, 'dap', 0, 1, tiled=True)  137 us
    dot_general x8, matrix products, block_partial(): jnp.einsum('sic,sjd->ijcd', left_block, right_proj, preferred_element_typ...  115 us
    unnamed x49, local copies, waits for them, and re-layouts  100 us
    convert_element_type x1, local copies, waits for them, and re-layouts, gathered_term(): jnp.einsum('sic,sjd->ijcd', left_proj, right_all, preferred_element_type=...  84.7 us
    dot_general x8, matrix products, block_partial(): jnp.einsum('ijcd,cdk->ijk', outer_prod, w_grid, preferred_element_type=jn...  77.9 us
    all_to_all x2, local copies, waits for them, and re-layouts, local_program(): extra_relaid = lax.all_to_all(extra_block, 'dap', 0, 1, tiled=True)  55.1 us
    dot_general x1, matrix products, gathered_term(): jnp.einsum('sic,sjd->ijcd', left_proj, right_all, preferred_element_type=...  41.8 us
  transfers between devices with their start and end apart: 4, of which 2 were waited for; matrix products, arithmetic and copies ran while one was open for 59% of the time, Pallas kernels for 0%

commit v1 on v0

v1 whole, which is shorter than its diff:
```python
import functools

import jax
import jax.numpy as jnp
from jax import lax
from jax.experimental import pallas as pl
from jax.experimental.pallas import tpu as pltpu
from jax.sharding import PartitionSpec as P

LN_EPS = 1e-5
NORM_EPS = 1e-3
NT = (((1,), (1,)), ((), ()))
F32 = jnp.float32
BF16 = jnp.bfloat16
ANY = pl.BlockSpec(memory_space=pl.ANY)
CORE, XBIT, YBIT = 1, 2, 4


def swap(value, bit, size):
    return lax.ppermute(value, 'dap', [(d, d ^ bit) for d in range(size)])


def project_kernel(group, x_ref, mask_ref, gamma_ref, beta_ref, w_ref, bias_ref, a_ref, b_ref):
    rows, chans, seqs = x_ref.shape
    hid = b_ref.shape[0]
    half = group * hid

    def body(step, carry):
        pieces = []
        for part in range(2):
            first = pl.multiple_of(step * 2 * group + part * group, group)
            x = x_ref[pl.ds(first, group)].astype(F32)
            centered = x - jnp.mean(x, axis=1, keepdims=True)
            var = jnp.mean(centered * centered, axis=1, keepdims=True)
            y = centered * lax.rsqrt(var + LN_EPS) * gamma_ref[...][None] + beta_ref[...][None]
            y = y.astype(BF16).reshape(group * chans, seqs)
            z = jnp.dot(w_ref[...], y, preferred_element_type=F32) + bias_ref[...]
            mask = mask_ref[pl.ds(first, group), :]
            left = z[:half].reshape(group, hid, seqs) * mask[:, None, :]
            a_ref[0, pl.ds(pl.multiple_of(first * hid, half), half), :] = left.astype(BF16).reshape(half, seqs)
            pieces.append(z[half:].reshape(hid, group, seqs) * mask[None])
        both = jnp.concatenate(pieces, axis=1).astype(BF16)
        b_ref[:, pl.ds(pl.multiple_of(step * 2 * group, 2 * group), 2 * group), :] = both
        return carry

    lax.fori_loop(0, rows // (2 * group), body, 0)


def project(x, mask_t, gamma, beta, w_left, b_left, w_right, b_right, block=32, group=8):
    res, chans, seqs = x.shape
    hid = w_left.shape[1]
    eye = jnp.eye(group, dtype=BF16)
    w_a = jnp.einsum('gh,mp->gphm', eye, w_left).reshape(group * hid, group * chans)
    w_b = jnp.einsum('gh,mq->qghm', eye, w_right).reshape(group * hid, group * chans)
    w_both = jnp.concatenate([w_a, w_b], axis=0)
    bias = jnp.concatenate([jnp.tile(b_left, group), jnp.repeat(b_right, group)]).astype(F32)
    bias = jnp.broadcast_to(bias[:, None], (2 * group * hid, seqs))
    gamma = jnp.broadcast_to(gamma.astype(F32)[:, None], (chans, seqs))
    beta = jnp.broadcast_to(beta.astype(F32)[:, None], (chans, seqs))
    steps = res // block
    whole = lambda shape: pl.BlockSpec(shape, lambda s: (0,) * len(shape))
    return pl.pallas_call(
        functools.partial(project_kernel, group),
        grid=(steps,),
        in_specs=[
            pl.BlockSpec((block, chans, seqs), lambda s: (s, 0, 0)),
            pl.BlockSpec((block, seqs), lambda s: (s, 0)),
            whole((chans, seqs)), whole((chans, seqs)), whole(w_both.shape), whole(bias.shape),
        ],
        out_specs=[
            pl.BlockSpec((1, block * hid, seqs), lambda s: (s, 0, 0)),
            pl.BlockSpec((hid, block, seqs), lambda s: (0, s, 0)),
        ],
        out_shape=[
            jax.ShapeDtypeStruct((steps, block * hid, seqs), BF16),
            jax.ShapeDtypeStruct((hid, res, seqs), BF16),
        ],
        compiler_params=pltpu.CompilerParams(vmem_limit_bytes=48 << 20),
        cost_estimate=pl.CostEstimate(flops=12 << 30, bytes_accessed=26 << 20, transcendentals=0),
        name='project',
    )(x, mask_t, gamma, beta, w_both, bias)


def outer_kernel(nblk, lens, places, qu, iu, idx_ref, *refs):
    na, nb = len(lens[0]), len(lens[1])
    a_refs, b_refs = refs[:na], refs[na:na + nb]
    w_ref, out_ref, a_v, b_v, o_v, sa, sb = refs[na + nb:]
    rows, hid, _, cols = o_v.shape
    step = pl.program_id(0)
    slot = lax.rem(step, 2)

    def a_copies(st, sl):
        off, out = 0, []
        for t, k in enumerate(lens[0]):
            out.append(pltpu.make_async_copy(a_refs[t].at[idx_ref[t, st]], a_v.at[sl, :, pl.ds(off, k)], sa.at[sl, t]))
            off += k
        return out

    def b_copies():
        off, out = 0, []
        for t, k in enumerate(lens[1]):
            if places is None:
                out.append(pltpu.make_async_copy(b_refs[t], b_v.at[:, :, pl.ds(off, k)], sb.at[t]))
                off += k
            else:
                width = cols // nb
                at = pl.multiple_of((idx_ref[na, 0] ^ places[t]) * width, width)
                out.append(pltpu.make_async_copy(b_refs[t], b_v.at[:, pl.ds(at, width), :], sb.at[t]))
        return out

    @pl.when(step == 0)
    def _():
        for c in a_copies(0, 0) + b_copies():
            c.start()
        for c in b_copies():
            c.wait()

    for c in a_copies(step, slot):
        c.wait()

    @pl.when(step + 1 < nblk)
    def _():
        for c in a_copies(step + 1, 1 - slot):
            c.start()

    def q_body(g, carry):
        for u in range(qu):
            q = g * qu + u
            o = lax.dot_general(a_v[slot], b_v[q], NT, preferred_element_type=F32)
            o_v[:, q] = o.astype(BF16).reshape(rows, hid, cols)
        return carry

    lax.fori_loop(0, hid // qu, q_body, 0)

    def i_body(g, carry):
        for u in range(iu):
            i = g * iu + u
            r = jnp.dot(w_ref[...], o_v[i].reshape(hid * hid, cols), preferred_element_type=F32)
            out_ref[i] = r.astype(out_ref.dtype)
        return carry

    lax.fori_loop(0, rows // iu, i_body, 0)


def outer(idx, a_list, b_list, w_out, nblk, cols, out_dtype, places=None, qu=8, iu=8):
    hid = b_list[0].shape[0]
    rows = a_list[0].shape[1] // hid
    depth = sum(a.shape[2] for a in a_list)
    chans = w_out.shape[1]
    w_t = w_out.reshape(hid, hid, chans).transpose(2, 1, 0).reshape(chans, hid * hid)
    lens = (tuple(a.shape[2] for a in a_list), tuple(b.shape[2] for b in b_list))
    flops = 2 * nblk * rows * hid * hid * cols * (depth + chans)
    return pl.pallas_call(
        functools.partial(outer_kernel, nblk, lens, places, qu, iu),
        grid_spec=pltpu.PrefetchScalarGridSpec(
            num_scalar_prefetch=1,
            grid=(nblk,),
            in_specs=[ANY] * (len(a_list) + len(b_list)) + [pl.BlockSpec(w_t.shape, lambda s, i: (0, 0))],
            out_specs=pl.BlockSpec((rows, chans, cols), lambda s, i: (s, 0, 0)),
            scratch_shapes=[
                pltpu.VMEM((2, rows * hid, depth), BF16),
                pltpu.VMEM((hid, cols, depth), BF16),
                pltpu.VMEM((rows, hid, hid, cols), BF16),
                pltpu.SemaphoreType.DMA((2, len(a_list))),
                pltpu.SemaphoreType.DMA((len(b_list),)),
            ],
        ),
        out_shape=jax.ShapeDtypeStruct((nblk * rows, chans, cols), out_dtype),
        compiler_params=pltpu.CompilerParams(vmem_limit_bytes=60 << 20),
        cost_estimate=pl.CostEstimate(flops=flops, bytes_accessed=32 << 20, transcendentals=0),
        name='outer',
    )(idx, *a_list, *b_list, w_t)


def combine_kernel(count, *refs):
    parts = refs[:count]
    main_ref, z_ref, den_e_ref, den_m_ref, bias_e_ref, bias_m_ref, out_ref = refs[count:]
    for i in range(out_ref.shape[0]):
        extra = parts[0][i].astype(F32)
        for part in parts[1:]:
            extra = extra + part[i].astype(F32)
        extra = (extra + bias_e_ref[...]) / den_e_ref[pl.ds(i, 1), :]
        main = (main_ref[i] + bias_m_ref[...]) / den_m_ref[pl.ds(i, 1), :]
        out_ref[i] = z_ref[i] + (extra + main).T


def combine(parts, main, z, den_e, den_m, bias_e, bias_m, block=8):
    rows, cols, chans = z.shape
    t_spec = lambda: pl.BlockSpec((block, chans, cols), lambda s: (s, 0, 0))
    z_spec = lambda: pl.BlockSpec((block, cols, chans), lambda s: (s, 0, 0))
    d_spec = lambda: pl.BlockSpec((block, cols), lambda s: (s, 0))
    c_spec = lambda: pl.BlockSpec((chans, cols), lambda s: (0, 0))
    wide = lambda b: jnp.broadcast_to(b.astype(F32)[:, None], (chans, cols))
    return pl.pallas_call(
        functools.partial(combine_kernel, len(parts)),
        grid=(rows // block,),
        in_specs=[t_spec() for _ in parts] + [t_spec(), z_spec(), d_spec(), d_spec(), c_spec(), c_spec()],
        out_specs=z_spec(),
        out_shape=jax.ShapeDtypeStruct(z.shape, F32),
        cost_estimate=pl.CostEstimate(flops=1 << 24, bytes_accessed=20 << 20, transcendentals=0),
        name='combine',
    )(*parts, main, z, den_e, den_m, wide(bias_e), wide(bias_m))


def layer_norm(value, gamma, beta):
    as_float = value.astype(F32)
    mean = jnp.mean(as_float, axis=-1, keepdims=True)
    centered = as_float - mean
    var = jnp.mean(centered * centered, axis=-1, keepdims=True)
    return (centered * lax.rsqrt(var + LN_EPS) * gamma.astype(F32) + beta.astype(F32)).astype(BF16)


def denominators(mask, mask_rows):
    counts = jnp.einsum('si,sj->ij', mask_rows.astype(BF16), mask.astype(BF16), preferred_element_type=F32)
    return NORM_EPS + counts


def solution(mesh):
    size = mesh.shape['dap']
    value_spec = P('data', 'dap', None)
    mask_spec = P('data', None)
    row_spec = P(('data', 'dap'), None, None)

    def local_program(extra_block, extra_mask, main_block, main_mask, pair_rows, eg, eb, ewl, ebl, ewr, ebr, ewo, ebo, mg, mb, mwl, mbl, mwr, mbr, mwo, mbo):
        me = lax.axis_index('dap')
        core, chip = lax.rem(me, 2), me // 2
        rows = extra_block.shape[1]
        hid = ewl.shape[1]

        seqs = extra_block.shape[0] // size
        chans = extra_block.shape[2]
        turned = extra_block.transpose(1, 2, 0).reshape(rows, chans, size, seqs).transpose(2, 0, 1, 3)
        extra_t = lax.all_to_all(turned, 'dap', 0, 0, tiled=True).reshape(size * rows, chans, seqs)
        extra_out = extra_t.transpose(2, 0, 1)

        mask_rows_m = lax.dynamic_slice_in_dim(main_mask, me * rows, rows, axis=1)
        mask_rows_e = lax.dynamic_slice_in_dim(extra_mask, me * rows, rows, axis=1)
        den_m = denominators(main_mask, mask_rows_m)
        den_e = denominators(extra_mask, mask_rows_e)
        normed = layer_norm(main_block, mg, mb)
        mask_m = mask_rows_m.astype(F32).T
        a_m = jnp.einsum('sim,mp->ips', normed, mwl, preferred_element_type=F32) + mbl.astype(F32)[None, :, None]
        a_m = (a_m * mask_m[:, None, :]).astype(BF16).reshape(1, rows * hid, -1)
        b_m = jnp.einsum('sim,mq->qis', normed, mwr, preferred_element_type=F32) + mbr.astype(F32)[:, None, None]
        b_m = (b_m * mask_m[None]).astype(BF16)

        extra_t, main_block, b_m = lax.optimization_barrier((extra_t, main_block, b_m))
        main_out = lax.all_to_all(main_block, 'dap', 0, 1, tiled=True)
        b_x, b_y = swap(b_m, XBIT, size), swap(b_m, YBIT, size)
        cut = hid // 2
        b_d = jnp.concatenate([swap(b_x[:cut], YBIT, size), swap(b_y[cut:], XBIT, size)], axis=0)
        b_parts = [b_m, b_x, b_y, b_d]
        b_parts = b_parts + [swap(part, CORE, size) for part in b_parts]
        places = (0, XBIT, YBIT, XBIT | YBIT, CORE, CORE | XBIT, CORE | YBIT, CORE | XBIT | YBIT)

        mask_seq = lax.dynamic_slice_in_dim(extra_mask, me * seqs, seqs, axis=0).astype(F32).T
        a_e, b_e = project(extra_t, mask_seq, eg, eb, ewl, ebl, ewr, ebr)
        a_split = a_e.reshape(size // 2, 2, rows * hid, seqs)
        a_give = lax.dynamic_index_in_dim(a_split, 1 - core, axis=1, keepdims=False)
        a_sib, b_sib = swap(a_give, CORE, size), swap(b_e, CORE, size)
        order = chip ^ jnp.array([3, 1, 2, 0], jnp.int32)
        idx = jnp.stack([order * 2 + core, order]).astype(jnp.int32)
        part = outer(idx, [a_e, a_sib], [b_e, b_sib], ewo, size // 2, size * rows, BF16)
        part = part.reshape(size // 2, rows, part.shape[1], part.shape[2])
        got = [swap(part[t], 2 * k, size) for t, k in enumerate((3, 1, 2))]

        idx_m = jnp.stack([jnp.zeros((), jnp.int32), me.astype(jnp.int32)])[:, None]
        main_sum = outer(idx_m, [a_m], b_parts, mwo, 1, size * rows, F32, places=places)
        pair_out = combine([part[3]] + got, main_sum, pair_rows, den_e, den_m, ebo, mbo)
        return pair_out, extra_out, main_out

    in_specs = (value_spec, mask_spec, value_spec, mask_spec, row_spec) + (P(),) * 16
    return jax.shard_map(local_program, mesh=mesh, in_specs=in_specs, out_specs=(row_spec, row_spec, row_spec), check_vma=False)
```

time: 921 us -> 431 us (0.47); the launches traced: 907 us -> 429 us
  matrix products: 261 us -> 21.5 us
  local copies, waits for them, and re-layouts: 292 us -> 76.8 us
  waiting for transfers between devices: 280 us -> 151 us
  Pallas kernels: 0 us -> 123 us
  other arithmetic: 50.3 us -> 20.1 us
  starting transfers between devices: 8.62 us -> 36.5 us
  between operations: 14.9 us -> 1.11 us
    dot_general x22 -> x4, matrix products: 261 us -> 21.5 us  [the longest x1 10.4 us: local_program(): jnp.einsum('sim,mq->qis', normed, mwr, preferred_element_type=F32)]
    all_to_all x2, waiting for transfers between devices: 280 us -> 86 us  [the longest x1 86 us: local_program(): lax.all_to_all(turned, 'dap', 0, 0, tiled=True)]
    pallas_call x0 -> x4, Pallas kernels: none -> 123 us  [the longest x2 94.8 us: outer(): pl.pallas_call(functools.partial(outer_kernel, nblk, lens, places, qu, iu...]
    convert_element_type x2 -> x0, local copies, waits for them, and re-layouts: 103 us -> none  [the longest x1 84.7 us: gathered_term(): jnp.einsum('sic,sjd->ijcd', left_proj, right_all, preferred_element_type=...]
    unnamed x49 -> x41, local copies, waits for them, and re-layouts: 100 us -> 21.9 us
    ppermute x0 -> x13, waiting for transfers between devices: none -> 64.9 us  [swap(): return lax.ppermute(value, 'dap', [(d, d ^ bit) for d in range(size)])]
    all_to_all x3 -> x1, local copies, waits for them, and re-layouts: 63.4 us -> 8.24 us  [local_program(): main_out = lax.all_to_all(main_block, 'dap', 0, 1, tiled=True)]
    ppermute x0 -> x13, starting transfers between devices: none -> 28.3 us  [swap(): return lax.ppermute(value, 'dap', [(d, d ^ bit) for d in range(size)])]
  transfers between devices with their start and end apart: 4 -> 15, of which waited for: 2 -> 5; matrix products, arithmetic and copies ran while one was open for 59% -> 24% of each run, Pallas kernels for 0% -> 22%
where the time goes in v1:
time: 431 us; the launch traced here: 429 us
  waiting for transfers between devices  151 us (35%)
  Pallas kernels  123 us (29%)
  local copies, waits for them, and re-layouts  76.8 us (18%)
  starting transfers between devices  36.5 us (8%)
  matrix products  21.5 us (5%)
  other arithmetic  20.1 us (5%)
    pallas_call x2, Pallas kernels, outer(): pl.pallas_call(functools.partial(outer_kernel, nblk, lens, places, qu, iu...  94.8 us
    all_to_all x1, waiting for transfers between devices, local_program(): lax.all_to_all(turned, 'dap', 0, 0, tiled=True)  86 us
    ppermute x13, waiting for transfers between devices, swap(): return lax.ppermute(value, 'dap', [(d, d ^ bit) for d in range(size)])  64.9 us
    ppermute x13, starting transfers between devices, swap(): return lax.ppermute(value, 'dap', [(d, d ^ bit) for d in range(size)])  28.3 us
    unnamed x41, local copies, waits for them, and re-layouts  21.9 us
    pallas_call x1, Pallas kernels, project(): pl.pallas_call(functools.partial(project_kernel, group), grid=(steps,), i...  18.5 us
    reshape x1, local copies, waits for them, and re-layouts, local_program(): extra_block.transpose(1, 2, 0).reshape(rows, chans, size, seqs)  11.8 us
    dot_general x1, matrix products, local_program(): jnp.einsum('sim,mq->qis', normed, mwr, preferred_element_type=F32)  10.4 us
  transfers between devices with their start and end apart: 15, of which 5 were waited for; matrix products, arithmetic and copies ran while one was open for 24% of the time, Pallas kernels for 22%

profile of v1, /device:TPU:0, one launch (start us, length us, event | category | flops | bytes accessed | tf_op | source)
XLA Modules:
  0.0 429.5 jit_solution(7584226157851558558)
XLA Ops:
  0.6 11.8 %copy.86 = bf16[32,8,8,8,384]{4,3,1,0,2:T(8,128)(2,1)} copy(bf16[32,8,8,8,384]{4,3,2,1,0:T(8,128)(2,1)} %bitcast.65) | data formatting | bytes 25165824 | tf_op jit(solution)/shard_map/reshape | solution.py:232
  12.4 4.3 %all-to-all-start = ((bf16[8,32,64,384]{3,2,1,0:T(8,128)(2,1)}), bf16[8,32,64,384]{3,2,1,0:T(8,128)(2,1)}, u32[]{:S(2)}, u32[]{:S(2)}) async-start(bf16[8,32,64,384]{3,2,1,0:T(8,128)(2,1)} %bitcast.64), calls=%async_computation | async-start | bytes 25165824 | tf_op jit(solution)/shard_map/all_to_all | solution.py:233
  16.8 5.8 %convert_reduce_fusion = f32[512,32]{1,0:T(8,128)S(1)} fusion(bf16[512,32,256]{2,1,0:T(8,128)(2,1)} %param.24), kind=kLoop, calls=%fused_computation.1 | loop fusion | flops 8372224 | bytes 8454144 | tf_op jit(solution)/shard_map/reduce_sum | solution.py:207
  22.6 7.0 %fusion.2 = f32[512,32]{1,0:T(8,128)S(1)} fusion(bf16[512,32,256]{2,1,0:T(8,128)(2,1)} %param.24, f32[512,32]{1,0:T(8,128)S(1)} %broadcast_multiply_fusion), kind=kLoop, calls=%fused_computation.4 | loop fusion | flops 16760832 | bytes 8519680 | tf_op jit(solution)/shard_map/reduce_sum | solution.py:209
  29.7 7.6 %fusion.6 = f32[512,32,32]{2,1,0:T(8,128)} fusion(bf16[512,32,256]{2,1,0:T(8,128)(2,1)S(1)} %bitcast.63, f32[256]{0:T(256)S(1)} %convert_element_type.64, f32[256]{0:T(256)S(1)} %convert_element_type.63, f32[512,32]{1,0:T(8,128)S(1)} %add_rsqrt_fusion, f32[512,32]{1,0:T(8,128)S(1)} %broadcast_multiply_fusion, bf16[256,32]{0,1:T(8,128)(2,1)S(1)} %copy-done), kind=kOutput, calls=%fused_computation.9 | convolution fusion | flops 293601280 | bytes 10635264 | tf_op jit(solution)/shard_map/sim,mp->ips/dot_general | solution.py:242
  37.3 5.2 %copy.75 = f32[512,32,32]{0,2,1:T(8,128)S(1)} copy(f32[512,32,32]{2,1,0:T(8,128)} %fusion.6) | data formatting | bytes 4194304 | tf_op jit(solution)/shard_map/sim,mp->ips/dot_general | solution.py:242
  44.0 10.4 %fusion.8 = f32[512,32,32]{2,1,0:T(8,128)} fusion(bf16[512,32,256]{2,1,0:T(8,128)(2,1)} %param.24, f32[256]{0:T(256)S(1)} %convert_element_type.64, f32[256]{0:T(256)S(1)} %convert_element_type.63, f32[512,32]{1,0:T(8,128)S(1)} %add_rsqrt_fusion, f32[512,32]{1,0:T(8,128)S(1)} %broadcast_multiply_fusion, bf16[256,32]{0,1:T(8,128)(2,1)S(1)} %copy-done.12), kind=kOutput, calls=%fused_computation.10 | convolution fusion | flops 293601280 | bytes 10635264 | tf_op jit(solution)/shard_map/sim,mq->qis/dot_general | solution.py:244
  54.4 6.6 %copy.68 = f32[512,32,32]{0,1,2:T(8,128)} copy(f32[512,32,32]{2,1,0:T(8,128)} %fusion.8) | data formatting | bytes 4194304 | tf_op jit(solution)/shard_map/sim,mq->qis/dot_general | solution.py:244
  67.4 3.3 fusion.10
  70.7 86.0 %all-to-all-done = bf16[8,32,64,384]{3,2,1,0:T(8,128)(2,1)} async-done(((bf16[8,32,64,384]{3,2,1,0:T(8,128)(2,1)}), bf16[8,32,64,384]{3,2,1,0:T(8,128)(2,1)}, u32[]{:S(2)}, u32[]{:S(2)}) %all-to-all-start) | async-done | bytes 12582944 | tf_op jit(solution)/shard_map/all_to_all | solution.py:233
  158.3 18.5 %project.1 = (bf16[8,1024,384]{2,1,0:T(8,128)(2,1)}, bf16[32,256,384]{2,1,0:T(8,128)(2,1)}) custom-call(bf16[256,64,384]{2,1,0:T(8,128)(2,1)} %bitcast.4.x_ref, f32[256,384]{1,0:T(8,128)S(1)} %convert_bitcast_fusion.mask_ref, f32[64,384]{1,0:T(8,128)S(1)} %broadcast_in_dim.14.gamma_ref, f32[64,384]{1,0:T(8,128)S(1)} %broadcast_in_dim.15.beta_ref, ...), custom_call_target="tpu_custom_call" | custom-call | flops 12884901888 | bytes 27262976 | tf_op jit(solution)/shard_map/project/pallas_call | solution.py:62
  176.8 2.2 dynamic-slice_bitcast_fusion
  180.6 24.1 %collective-permute-done.5.refs_2_ = bf16[32,32,512]{2,1,0:T(8,128)(2,1)S(1)} collective-permute-done((bf16[32,32,512]{2,1,0:T(8,128)(2,1)}, bf16[32,32,512]{2,1,0:T(8,128)(2,1)S(1)}, u32[]{:S(2)}, u32[]{:S(2)}) %collective-permute-start.5) | collective-permute-done | bytes 1048608 | tf_op jit(solution)/shard_map/ppermute | solution.py:20
  209.5 3.9 all-to-all-start.1
  217.0 4.3 %collective-permute-done.7 = bf16[16,32,512]{2,1,0:T(8,128)(2,1)} collective-permute-done((bf16[16,32,512]{2,1,0:T(8,128)(2,1)}, bf16[16,32,512]{2,1,0:T(8,128)(2,1)}, u32[]{:S(2)}, u32[]{:S(2)}) %collective-permute-start.7) | collective-permute-done | bytes 524320 | tf_op jit(solution)/shard_map/ppermute | solution.py:20
  223.2 75.0 %outer.2 = bf16[128,128,256]{2,1,0:T(8,128)(2,1)} custom-call(s32[2,4]{1,0:T(2,128)} %pad_add_fusion.idx_ref, bf16[8,1024,384]{2,1,0:T(8,128)(2,1)} %get-tuple-element.9.refs_0_, bf16[4,1024,384]{2,1,0:T(8,128)(2,1)} %collective-permute-done.refs_1_, bf16[32,256,384]{2,1,0:T(8,128)(2,1)} %get-tuple-element.10.refs_2_, ...), custom_call_target="tpu_custom_call" | custom-call | flops 60129542144 | bytes 33554432 | tf_op jit(solution)/shard_map/outer/pallas_call | solution.py:153
  298.2 6.3 %fusion.25 = (bf16[32,128,256]{2,1,0:T(8,128)(2,1)}, bf16[32,128,256]{2,1,0:T(8,128)(2,1)}, bf16[32,128,256]{2,1,0:T(8,128)(2,1)}, bf16[32,128,256]{2,1,0:T(8,128)(2,1)}) fusion(bf16[128,128,256]{2,1,0:T(8,128)(2,1)} %outer.2), kind=kLoop, calls=%fused_computation.46 | loop fusion | bytes 16777216 | tf_op jit(solution)/shard_map/slice | solution.py:265
  304.5 22.8 %collective-permute-start.2 = (bf16[32,128,256]{2,1,0:T(8,128)(2,1)}, bf16[32,128,256]{2,1,0:T(8,128)(2,1)}, u32[]{:S(2)}, u32[]{:S(2)}) collective-permute-start(bf16[32,128,256]{2,1,0:T(8,128)(2,1)} %get-tuple-element.27), channel_id=1, source_target_pairs={{0,6},{1,7},{2,4},{3,5},{4,2},{5,3},{6,0},{7,1}} | collective-permute-start | bytes 6291464 | tf_op jit(solution)/shard_map/ppermute | solution.py:20
  332.5 2.0 convolution_add_fusion.refs_7_
  336.0 18.0 %copy.81 = bf16[384,256,64]{1,2,0:T(8,128)(2,1)} copy(bf16[384,256,64]{0,2,1:T(8,128)(2,1)} %bitcast.24) | data formatting | bytes 25165824
  354.0 19.8 %outer.3.refs_4_ = f32[32,128,256]{2,1,0:T(8,128)} custom-call(s32[2,1]{1,0:T(2,128)} %copy.78.idx_ref, bf16[1,1024,512]{2,1,0:T(8,128)(2,1)} %bitcast.70, bf16[32,32,512]{2,1,0:T(8,128)(2,1)} %get-tuple-element.11.refs_1_, bf16[32,32,512]{2,1,0:T(8,128)(2,1)} %copy-done.4, bf16[32,32,512]{2,1,0:T(8,128)(2,1)} %collective-permute-done.6.refs_3_, ...), custom_call_target="tpu_custom_call" | custom-call | flops 10737418240 | bytes 33554432 | tf_op jit(solution)/shard_map/outer/pallas_call | solution.py:153
  373.8 8.2 %copy.80 = bf16[8,64,32,256]{3,2,0,1:T(8,128)(2,1)} copy(bf16[8,64,32,256]{3,2,1,0:T(8,128)(2,1)} %bitcast.25) | data formatting | bytes 16777216 | tf_op jit(solution)/shard_map/all_to_all | solution.py:248
  382.0 36.4 %collective-permute-done.3.refs_2_ = bf16[32,128,256]{2,1,0:T(8,128)(2,1)} collective-permute-done((bf16[32,128,256]{2,1,0:T(8,128)(2,1)}, bf16[32,128,256]{2,1,0:T(8,128)(2,1)}, u32[]{:S(2)}, u32[]{:S(2)}) %collective-permute-start.3) | collective-permute-done | bytes 2097184 | tf_op jit(solution)/shard_map/ppermute | solution.py:20
  420.1 9.2 %combine.1 = f32[32,256,128]{2,1,0:T(8,128)} custom-call(bf16[32,128,256]{2,1,0:T(8,128)(2,1)} %get-tuple-element.28.refs_0_, bf16[32,128,256]{2,1,0:T(8,128)(2,1)} %collective-permute-done.2.refs_1_, bf16[32,128,256]{2,1,0:T(8,128)(2,1)} %collective-permute-done.3.refs_2_, bf16[32,128,256]{2,1,0:T(8,128)(2,1)} %collective-permute-done.4.refs_3_, ...), custom_call_target="tpu_custom_call" | custom-call | flops 16777216 | bytes 20971520 | tf_op jit(solution)/shard_map/combine/pallas_call | solution.py:194
  (102 shorter events, 29.6 us)
Async XLA Ops:
  0.6 29.0 %copy-start = (bf16[256,32]{0,1:T(8,128)(2,1)S(1)}, bf16[256,32]{0,1:T(8,128)(2,1)}, u32[]{:S(2)}) copy-start(bf16[256,32]{0,1:T(8,128)(2,1)} %param.37) | copy-start | bytes 49156
  12.4 144.3 %all-to-all-start = ((bf16[8,32,64,384]{3,2,1,0:T(8,128)(2,1)}), bf16[8,32,64,384]{3,2,1,0:T(8,128)(2,1)}, u32[]{:S(2)}, u32[]{:S(2)}) async-start(bf16[8,32,64,384]{3,2,1,0:T(8,128)(2,1)} %bitcast.64), calls=%async_computation | async-start | bytes 25165824 | tf_op jit(solution)/shard_map/all_to_all | solution.py:233
  16.8 12.9 %slice-start = ((s8[8388608]{0:T(1024)(128)(4,1)}), s8[4194304]{0:T(1024)(128)(4,1)S(1)}, s32[]{:S(2)}) async-start(s8[8388608]{0:T(1024)(128)(4,1)} %bitcast.62), calls=%async_computation.2 | async-start | bytes 8388608
  54.4 10.7 %copy-start.9 = (bf16[32]{0:T(256)(128)(2,1)S(1)}, bf16[32]{0:T(256)(128)(2,1)}, u32[]{:S(2)}) copy-start(bf16[32]{0:T(256)(128)(2,1)} %param.32) | copy-start | bytes 196
  54.4 10.9 %copy-start.10 = (bf16[32]{0:T(256)(128)(2,1)S(1)}, bf16[32]{0:T(256)(128)(2,1)}, u32[]{:S(2)}) copy-start(bf16[32]{0:T(256)(128)(2,1)} %param.30) | copy-start | bytes 196
  176.8 32.1 %copy-start.11 = (s32[4]{0:T(128)S(1)}, s32[4]{0:T(128)}, u32[]{:S(2)}) copy-start(s32[4]{0:T(128)} %constant.50.clone) | copy-start | bytes 52
  176.8 46.4 %collective-permute-start.1 = (bf16[32,256,384]{2,1,0:T(8,128)(2,1)}, bf16[32,256,384]{2,1,0:T(8,128)(2,1)}, u32[]{:S(2)}, u32[]{:S(2)}) collective-permute-start(bf16[32,256,384]{2,1,0:T(8,128)(2,1)} %get-tuple-element.10.refs_2_), channel_id=1, source_target_pairs={{0,1},{1,0},{2,3},{3,2},{4,5},{5,4},{6,7},{7,6}} | collective-permute-start | bytes 18874376 | tf_op jit(solution)/shard_map/ppermute | solution.py:20
  179.1 44.1 %collective-permute-start = (bf16[4,1024,384]{2,1,0:T(8,128)(2,1)S(1)}, bf16[4,1024,384]{2,1,0:T(8,128)(2,1)}, u32[]{:S(2)}, u32[]{:S(2)}) collective-permute-start(bf16[4,1024,384]{2,1,0:T(8,128)(2,1)S(1)} %dynamic-slice_bitcast_fusion), channel_id=1, source_target_pairs={{0,1},{1,0},{2,3},{3,2},{4,5},{5,4},{6,7},{7,6}} | collective-permute-start | bytes 9437192 | tf_op jit(solution)/shard_map/ppermute | solution.py:20
  179.6 25.1 %collective-permute-start.5 = (bf16[32,32,512]{2,1,0:T(8,128)(2,1)}, bf16[32,32,512]{2,1,0:T(8,128)(2,1)S(1)}, u32[]{:S(2)}, u32[]{:S(2)}) collective-permute-start(bf16[32,32,512]{2,1,0:T(8,128)(2,1)} %get-tuple-element.11.refs_1_), channel_id=1, source_target_pairs={{0,2},{1,3},{2,0},{3,1},{4,6},{5,7},{6,4},{7,5}} | collective-permute-start | bytes 3145736 | tf_op jit(solution)/shard_map/ppermute | solution.py:20
  179.6 33.8 %collective-permute-start.6 = (bf16[32,32,512]{2,1,0:T(8,128)(2,1)}, bf16[32,32,512]{2,1,0:T(8,128)(2,1)}, u32[]{:S(2)}, u32[]{:S(2)}) collective-permute-start(bf16[32,32,512]{2,1,0:T(8,128)(2,1)} %get-tuple-element.11.refs_1_), channel_id=1, source_target_pairs={{0,4},{1,5},{2,6},{3,7},{4,0},{5,1},{6,2},{7,3}} | collective-permute-start | bytes 3145736 | tf_op jit(solution)/shard_map/ppermute | solution.py:20
  206.5 14.8 %collective-permute-start.7 = (bf16[16,32,512]{2,1,0:T(8,128)(2,1)}, bf16[16,32,512]{2,1,0:T(8,128)(2,1)}, u32[]{:S(2)}, u32[]{:S(2)}) collective-permute-start(bf16[16,32,512]{2,1,0:T(8,128)(2,1)} %slice.32), channel_id=1, source_target_pairs={{0,4},{1,5},{2,6},{3,7},{4,0},{5,1},{6,2},{7,3}} | collective-permute-start | bytes 1572872 | tf_op jit(solution)/shard_map/ppermute | solution.py:20
  209.5 119.8 %collective-permute-start.9 = (bf16[32,32,512]{2,1,0:T(8,128)(2,1)}, bf16[32,32,512]{2,1,0:T(8,128)(2,1)}, u32[]{:S(2)}, u32[]{:S(2)}) collective-permute-start(bf16[32,32,512]{2,1,0:T(8,128)(2,1)} %get-tuple-element.11.refs_1_), channel_id=1, source_target_pairs={{0,1},{1,0},{2,3},{3,2},{4,5},{5,4},{6,7},{7,6}} | collective-permute-start | bytes 3145736 | tf_op jit(solution)/shard_map/ppermute | solution.py:20
  209.5 164.2 %all-to-all-start.1 = ((bf16[512,32,256]{2,1,0:T(8,128)(2,1)}), bf16[512,32,256]{2,1,0:T(8,128)(2,1)}, u32[]{:S(2)}, u32[]{:S(2)}) async-start(bf16[512,32,256]{2,1,0:T(8,128)(2,1)} %param.24), calls=%async_computation.1 | async-start | bytes 16777216 | tf_op jit(solution)/shard_map/all_to_all | solution.py:248
  215.3 112.1 %collective-permute-start.8 = (bf16[16,32,512]{2,1,0:T(8,128)(2,1)}, bf16[16,32,512]{2,1,0:T(8,128)(2,1)S(1)}, u32[]{:S(2)}, u32[]{:S(2)}) collective-permute-start(bf16[16,32,512]{2,1,0:T(8,128)(2,1)} %slice.33), channel_id=1, source_target_pairs={{0,2},{1,3},{2,0},{3,1},{4,6},{5,7},{6,4},{7,5}} | collective-permute-start | bytes 1572872 | tf_op jit(solution)/shard_map/ppermute | solution.py:20
  221.3 108.1 %collective-permute-start.10 = (bf16[32,32,512]{2,1,0:T(8,128)(2,1)}, bf16[32,32,512]{2,1,0:T(8,128)(2,1)}, u32[]{:S(2)}, u32[]{:S(2)}) collective-permute-start(bf16[32,32,512]{2,1,0:T(8,128)(2,1)} %copy-done.4), channel_id=1, source_target_pairs={{0,1},{1,0},{2,3},{3,2},{4,5},{5,4},{6,7},{7,6}} | collective-permute-start | bytes 3145736 | tf_op jit(solution)/shard_map/ppermute | solution.py:20
  298.2 36.3 %copy-start.2 = (s32[3072,256]{1,0:T(8,128)S(1)}, s32[3072,256]{1,0:T(8,128)}, u32[]{:S(2)}) copy-start(s32[3072,256]{1,0:T(8,128)} %param.23) | copy-start | bytes 9437188
  304.5 77.5 %collective-permute-start.2 = (bf16[32,128,256]{2,1,0:T(8,128)(2,1)}, bf16[32,128,256]{2,1,0:T(8,128)(2,1)}, u32[]{:S(2)}, u32[]{:S(2)}) collective-permute-start(bf16[32,128,256]{2,1,0:T(8,128)(2,1)} %get-tuple-element.27), channel_id=1, source_target_pairs={{0,6},{1,7},{2,4},{3,5},{4,2},{5,3},{6,0},{7,1}} | collective-permute-start | bytes 6291464 | tf_op jit(solution)/shard_map/ppermute | solution.py:20
  327.4 91.1 %collective-permute-start.3 = (bf16[32,128,256]{2,1,0:T(8,128)(2,1)}, bf16[32,128,256]{2,1,0:T(8,128)(2,1)}, u32[]{:S(2)}, u32[]{:S(2)}) collective-permute-start(bf16[32,128,256]{2,1,0:T(8,128)(2,1)} %get-tuple-element.26), channel_id=1, source_target_pairs={{0,2},{1,3},{2,0},{3,1},{4,6},{5,7},{6,4},{7,5}} | collective-permute-start | bytes 6291464 | tf_op jit(solution)/shard_map/ppermute | solution.py:20
  327.4 91.2 %collective-permute-start.4 = (bf16[32,128,256]{2,1,0:T(8,128)(2,1)}, bf16[32,128,256]{2,1,0:T(8,128)(2,1)}, u32[]{:S(2)}, u32[]{:S(2)}) collective-permute-start(bf16[32,128,256]{2,1,0:T(8,128)(2,1)} %get-tuple-element.25), channel_id=1, source_target_pairs={{0,4},{1,5},{2,6},{3,7},{4,0},{5,1},{6,2},{7,3}} | collective-permute-start | bytes 6291464 | tf_op jit(solution)/shard_map/ppermute | solution.py:20
  329.4 24.6 %collective-permute-start.11 = (bf16[32,32,512]{2,1,0:T(8,128)(2,1)}, bf16[32,32,512]{2,1,0:T(8,128)(2,1)}, u32[]{:S(2)}, u32[]{:S(2)}) collective-permute-start(bf16[32,32,512]{2,1,0:T(8,128)(2,1)} %collective-permute-done.6.refs_3_), channel_id=1, source_target_pairs={{0,1},{1,0},{2,3},{3,2},{4,5},{5,4},{6,7},{7,6}} | collective-permute-start | bytes 3145736 | tf_op jit(solution)/shard_map/ppermute | solution.py:20
  329.4 24.6 %collective-permute-start.12 = (bf16[32,32,512]{2,1,0:T(8,128)(2,1)}, bf16[32,32,512]{2,1,0:T(8,128)(2,1)}, u32[]{:S(2)}, u32[]{:S(2)}) collective-permute-start(bf16[32,32,512]{2,1,0:T(8,128)(2,1)} %constant_dynamic-update-slice_fusion.refs_4_), channel_id=1, source_target_pairs={{0,1},{1,0},{2,3},{3,2},{4,5},{5,4},{6,7},{7,6}} | collective-permute-start | bytes 3145736 | tf_op jit(solution)/shard_map/ppermute | solution.py:20
  373.8 44.8 %copy-start.7 = (bf16[128]{0:T(256)(128)(2,1)S(1)}, bf16[128]{0:T(256)(128)(2,1)}, u32[]{:S(2)}) copy-start(bf16[128]{0:T(256)(128)(2,1)} %param.34) | copy-start | bytes 772
  373.8 45.5 %copy-start.8 = (bf16[128]{0:T(256)(128)(2,1)S(1)}, bf16[128]{0:T(256)(128)(2,1)}, u32[]{:S(2)}) copy-start(bf16[128]{0:T(256)(128)(2,1)} %param.42) | copy-start | bytes 772
  419.3 10.0 %copy-start.1 = (bf16[256,32]{0,1:T(8,128)(2,1)S(1)}, bf16[256,32]{0,1:T(8,128)(2,1)}, u32[]{:S(2)}) copy-start(bf16[256,32]{0,1:T(8,128)(2,1)} %param.37) | copy-start | bytes 49156
  (10 other events, 59.6 us)

commit v2 on v1

v2 whole, which is shorter than its diff:
```python
import functools

import jax
import jax.numpy as jnp
from jax import lax
from jax.experimental import pallas as pl
from jax.experimental.pallas import tpu as pltpu
from jax.sharding import PartitionSpec as P


LN_EPS = 1e-5
NORM_EPS = 1e-3
NT = (((1,), (1,)), ((), ()))
F32 = jnp.float32
BF16 = jnp.bfloat16
ANY = pl.BlockSpec(memory_space=pl.ANY)
CORE, XBIT, YBIT = 1, 2, 4
LANES = 128
NEAR, REST = (2, 4, 3, 5), (6, 7, 1, 0)


def swap(value, bit, size):
    return lax.ppermute(value, 'dap', [(d, d ^ bit) for d in range(size)])


def turn_kernel(ks, me_ref, x_ref, *refs):
    outs, (v, s_in, s_out) = refs[:len(ks)], refs[len(ks):]
    seqs = v.shape[3]
    loads = [
        pltpu.make_async_copy(x_ref.at[:, :, pl.ds(pl.multiple_of((me_ref[0] ^ k) * seqs, LANES), seqs)], v.at[t], s_in.at[t])
        for t, k in enumerate(ks)
    ]
    stores = [pltpu.make_async_copy(v.at[t], out, s_out.at[t]) for t, out in enumerate(outs)]
    for c in loads:
        c.start()
    for load, save in zip(loads, stores):
        load.wait()
        save.start()
    for c in stores:
        c.wait()


def turn(me, x, ks, size):
    rows, chans, total = x.shape
    seqs = total // size
    return pl.pallas_call(
        functools.partial(turn_kernel, ks),
        grid_spec=pltpu.PrefetchScalarGridSpec(
            num_scalar_prefetch=1,
            grid=(1,),
            in_specs=[ANY],
            out_specs=[ANY] * len(ks),
            scratch_shapes=[
                pltpu.VMEM((len(ks), rows, chans, seqs), x.dtype),
                pltpu.SemaphoreType.DMA((len(ks),)),
                pltpu.SemaphoreType.DMA((len(ks),)),
            ],
        ),
        out_shape=[jax.ShapeDtypeStruct((rows, chans, seqs), x.dtype) for _ in ks],
        cost_estimate=pl.CostEstimate(flops=1 << 24, bytes_accessed=4 << 20, transcendentals=0),
        name='turn',
    )(me, x)


def turn_out_kernel(ks, me_ref, *refs):
    x_refs, (out_ref, in_v, out_v) = refs[:len(ks)], refs[len(ks):]
    rows, lead = x_refs[0].shape[:2]
    for k, ref in zip(ks, x_refs):
        in_v[pl.ds(pl.multiple_of((me_ref[0] ^ k) * rows, rows), rows)] = ref[...].astype(F32)
    for c in range(lead):
        out_v[:, c, :] = in_v[:, c, :].T
    out_ref[...] = out_v[...].astype(BF16)


def turn_out(me, blocks, lead=8):
    ks = tuple(sorted(blocks))
    rows, chans, seqs = blocks[ks[0]].shape
    res = rows * len(ks)
    return pl.pallas_call(
        functools.partial(turn_out_kernel, ks),
        grid_spec=pltpu.PrefetchScalarGridSpec(
            num_scalar_prefetch=1,
            grid=(seqs // LANES, chans // lead),
            in_specs=[pl.BlockSpec((rows, lead, LANES), lambda k, c, i: (0, c, k)) for _ in ks],
            out_specs=pl.BlockSpec((LANES, lead, res), lambda k, c, i: (k, c, 0)),
            scratch_shapes=[pltpu.VMEM((res, lead, LANES), F32), pltpu.VMEM((LANES, lead, res), F32)],
        ),
        out_shape=jax.ShapeDtypeStruct((seqs, chans, res), BF16),
        cost_estimate=pl.CostEstimate(flops=1 << 24, bytes_accessed=25 << 20, transcendentals=0),
        name='turn_out',
    )(me, *[blocks[k] for k in ks])


def project_kernel(group, idx_ref, *refs):
    count = len(refs) - 12
    x_refs = refs[:count]
    mask_ref, gamma_ref, beta_ref, w_ref, bias_ref, own_ref, sib_ref, b_ref, x_v, a_v, s_in, s_out = refs[count:]
    rows, chans, seqs = x_v.shape[1:]
    hid = b_ref.shape[1]
    half = group * hid
    block = pl.program_id(0)
    slot = lax.rem(block, 2)
    loads = [pltpu.make_async_copy(ref, x_v.at[t], s_in.at[t]) for t, ref in enumerate(x_refs)]
    targets = [own_ref.at[t] for t in range(count // 2)] + [sib_ref.at[t] for t in range(count // 2)]
    saves = [pltpu.make_async_copy(a_v.at[t % 2], target, s_out.at[t % 2]) for t, target in enumerate(targets)]

    @pl.when(block == 0)
    def _():
        for c in loads:
            c.start()

    for t in range(count):
        @pl.when(block == t)
        def _(t=t):
            loads[t].wait()
            if t >= 2:
                saves[t - 2].wait()

    def body(step, carry):
        pieces = []
        for part in range(2):
            first = pl.multiple_of(step * 2 * group + part * group, group)
            x = x_v[block, pl.ds(first, group)].astype(F32)
            centered = x - jnp.mean(x, axis=1, keepdims=True)
            var = jnp.mean(centered * centered, axis=1, keepdims=True)
            y = centered * lax.rsqrt(var + LN_EPS) * gamma_ref[...][None] + beta_ref[...][None]
            y = y.astype(BF16).reshape(group * chans, seqs)
            z = jnp.dot(w_ref[...], y, preferred_element_type=F32) + bias_ref[...]
            mask = mask_ref[pl.ds(first, group), :]
            left = z[:half].reshape(group, hid, seqs) * mask[:, None, :]
            a_v[slot, pl.ds(pl.multiple_of(first * hid, half), half), :] = left.astype(BF16).reshape(half, seqs)
            pieces.append(z[half:].reshape(hid, group, seqs) * mask[None])
        both = jnp.concatenate(pieces, axis=1).astype(BF16)
        b_ref[0, :, pl.ds(pl.multiple_of(step * 2 * group, 2 * group), 2 * group), :] = both
        return carry

    lax.fori_loop(0, rows // (2 * group), body, 0)
    for t in range(count):
        @pl.when(block == t)
        def _(t=t):
            saves[t].start()
            if t == count - 1:
                for c in saves[t - 1:]:
                    c.wait()


def project_weights(w_left, b_left, w_right, b_right, seqs, group=8):
    chans, hid = w_left.shape
    eye = jnp.eye(group, dtype=BF16)
    w_a = jnp.einsum('gh,mp->gphm', eye, w_left).reshape(group * hid, group * chans)
    w_b = jnp.einsum('gh,mq->qghm', eye, w_right).reshape(group * hid, group * chans)
    w_both = jnp.concatenate([w_a, w_b], axis=0)
    bias = jnp.concatenate([jnp.tile(b_left, group), jnp.repeat(b_right, group)]).astype(F32)
    return w_both, jnp.broadcast_to(bias[:, None], (2 * group * hid, seqs))


def project(idx, blocks, mask_t, gamma, beta, w_both, bias, hid, group=8):
    count = len(blocks)
    rows, chans, seqs = blocks[0].shape
    whole = lambda v: pl.BlockSpec(v.shape, lambda s, i: (0,) * v.ndim)
    return pl.pallas_call(
        functools.partial(project_kernel, group),
        grid_spec=pltpu.PrefetchScalarGridSpec(
            num_scalar_prefetch=1,
            grid=(count,),
            in_specs=[ANY] * count + [
                pl.BlockSpec((rows, seqs), lambda s, i: (i[s], 0)),
                whole(gamma), whole(beta), whole(w_both), whole(bias),
            ],
            out_specs=[ANY, ANY, pl.BlockSpec((1, hid, rows, seqs), lambda s, i: (s, 0, 0, 0))],
            scratch_shapes=[
                pltpu.VMEM((count, rows, chans, seqs), BF16),
                pltpu.VMEM((2, rows * hid, seqs), BF16),
                pltpu.SemaphoreType.DMA((count,)),
                pltpu.SemaphoreType.DMA((2,)),
            ],
        ),
        out_shape=[
            jax.ShapeDtypeStruct((count // 2, rows * hid, seqs), BF16),
            jax.ShapeDtypeStruct((count // 2, rows * hid, seqs), BF16),
            jax.ShapeDtypeStruct((count, hid, rows, seqs), BF16),
        ],
        compiler_params=pltpu.CompilerParams(vmem_limit_bytes=48 << 20),
        cost_estimate=pl.CostEstimate(flops=6 << 30, bytes_accessed=13 << 20, transcendentals=0),
        name='project',
    )(idx, *blocks, mask_t, gamma, beta, w_both, bias)


def outer_rows(a, b_v, o_v, qu, ready=None):
    rows, hid, _, cols = o_v.shape

    def q_body(g, carry):
        if ready is not None:
            ready(g)
        for u in range(qu):
            q = g * qu + u
            o = lax.dot_general(a[...], b_v[q], NT, preferred_element_type=F32)
            o_v[:, q] = o.astype(BF16).reshape(rows, hid, cols)
        return carry

    lax.fori_loop(0, hid // qu, q_body, 0)


def weigh_rows(w_ref, o_v, iu, store):
    rows, hid, _, cols = o_v.shape

    def i_body(g, carry):
        for u in range(iu):
            i = g * iu + u
            store(i, jnp.dot(w_ref[...], o_v[i].reshape(hid * hid, cols), preferred_element_type=F32))
        return carry

    lax.fori_loop(0, rows // iu, i_body, 0)


SET_A, SET_B = (0, 2, 4, 1, 3, 5), (6, 7)


def extra_kernel(qu, iu, me_ref, *refs):
    (a_a, a_a_sib, a_b, a_b_sib), b_refs = refs[:4], refs[4:8]
    w_ref, sx, sy, kx, ky, own, a_v, b_v, o_v, r_v, sa, sb, so = refs[8:]
    step = pl.program_id(0)
    slot = lax.rem(step, 2)
    half = kx.shape[0]
    lo, hi = pl.ds(0, half), pl.ds(half, half)
    depth = a_a.shape[2]
    width = b_refs[0].shape[2]

    def a_copies(t):
        pair, at = (((a_b, a_b_sib), 0), ((a_a, a_a_sib), 1), ((a_a, a_a_sib), 2), ((a_a, a_a_sib), 0))[t]
        return [
            pltpu.make_async_copy(ref.at[at], a_v.at[t % 2, :, pl.ds(n * depth, depth)], sa.at[t % 2, n])
            for n, ref in enumerate(pair)
        ]

    def b_copies(g):
        out = []
        qs = pl.ds(g * qu, qu)
        pieces = [(n, ref, t, k) for n, (ref, ks) in enumerate(zip(b_refs, (SET_A, SET_A, SET_B, SET_B))) for t, k in enumerate(ks)]
        for m, (n, ref, t, k) in enumerate(pieces):
            k = k ^ CORE if n % 2 else k
            js = pl.ds(pl.multiple_of((me_ref[0] ^ k) * width, width), width)
            out.append(pltpu.make_async_copy(ref.at[t, qs], b_v.at[qs, js, pl.ds(n % 2 * depth, depth)], sb.at[g, m]))
        return out

    def out_copies(t):
        lower, upper = ((sx.at[0], sy.at[0]), (sx.at[1], kx), (ky, sy.at[1]), (own.at[lo], own.at[hi]))[t]
        sl = t % 2
        return [
            pltpu.make_async_copy(r_v.at[sl, lo], lower, so.at[sl, 0]),
            pltpu.make_async_copy(r_v.at[sl, hi], upper, so.at[sl, 1]),
        ]

    @pl.when(step == 0)
    def _():
        for c in a_copies(0):
            c.start()
        for g in range(b_v.shape[0] // qu):
            for c in b_copies(g):
                c.start()

    for t in range(4):
        @pl.when(step == t)
        def _(t=t):
            for c in a_copies(t):
                c.wait()
            if t < 3:
                for c in a_copies(t + 1):
                    c.start()

    def ready(g):
        @pl.when(step == 0)
        def _():
            for c in b_copies(g):
                c.wait()

    outer_rows(a_v.at[slot], b_v, o_v, qu, ready)
    for t in range(2, 4):
        @pl.when(step == t)
        def _(t=t):
            for c in out_copies(t - 2):
                c.wait()

    def store(i, r):
        r_v[slot, i] = r.astype(BF16)

    weigh_rows(w_ref, o_v, iu, store)
    for t in range(4):
        @pl.when(step == t)
        def _(t=t):
            for c in out_copies(t):
                c.start()
            if t == 3:
                for c in out_copies(2) + out_copies(3):
                    c.wait()


def turn_weights(w_out, hid):
    return w_out.reshape(hid, hid, -1).transpose(2, 1, 0).reshape(-1, hid * hid)


def extra_parts(me, a_parts, b_parts, w_t, cols, qu=8, iu=8):
    hid, depth = b_parts[0].shape[1], 2 * b_parts[0].shape[3]
    rows = a_parts[0].shape[1] // hid
    chans = w_t.shape[0]
    half = rows // 2
    part = lambda *lead: jax.ShapeDtypeStruct(lead + (chans, cols), BF16)
    return pl.pallas_call(
        functools.partial(extra_kernel, qu, iu),
        grid_spec=pltpu.PrefetchScalarGridSpec(
            num_scalar_prefetch=1,
            grid=(4,),
            in_specs=[ANY] * 8 + [pl.BlockSpec(w_t.shape, lambda s, i: (0, 0))],
            out_specs=[ANY] * 5,
            scratch_shapes=[
                pltpu.VMEM((2, rows * hid, depth), BF16),
                pltpu.VMEM((hid, cols, depth), BF16),
                pltpu.VMEM((rows, hid, hid, cols), BF16),
                pltpu.VMEM((2, rows, chans, cols), BF16),
                pltpu.SemaphoreType.DMA((2, 2)),
                pltpu.SemaphoreType.DMA((hid // qu, 16)),
                pltpu.SemaphoreType.DMA((2, 2)),
            ],
        ),
        out_shape=[part(2, half), part(2, half), part(half), part(half), part(rows)],
        compiler_params=pltpu.CompilerParams(vmem_limit_bytes=60 << 20),
        cost_estimate=pl.CostEstimate(flops=60 << 30, bytes_accessed=32 << 20, transcendentals=0),
        name='extra_outer',
    )(me, *a_parts, *b_parts, w_t)


def main_kernel(places, qu, iu, idx_ref, a_ref, *refs):
    b_refs = refs[:len(places)]
    w_ref, bias_ref, den_ref, z_ref, out_ref, b_v, o_v, sb = refs[len(places):]
    copies = []
    for t, (ref, (k, first)) in enumerate(zip(b_refs, places)):
        count, width = ref.shape[:2]
        at = pl.multiple_of((idx_ref[0] ^ k) * width, width)
        copies.append(pltpu.make_async_copy(ref, b_v.at[pl.ds(first, count), pl.ds(at, width), :], sb.at[t]))
    for c in copies:
        c.start()
    for c in copies:
        c.wait()
    outer_rows(a_ref, b_v, o_v, qu)

    def store(i, r):
        out_ref[i] = z_ref[i] + ((r + bias_ref[...]) / den_ref[pl.ds(i, 1), :]).T

    weigh_rows(w_ref, o_v, iu, store)


def main_rows(me, a, b_parts, places, w_t, bias, den, z, qu=8, iu=8):
    hid, _, depth = b_parts[0].shape
    rows, cols, _ = z.shape
    whole = lambda v: pl.BlockSpec(v.shape, lambda s, i: (0,) * v.ndim)
    return pl.pallas_call(
        functools.partial(main_kernel, places, qu, iu),
        grid_spec=pltpu.PrefetchScalarGridSpec(
            num_scalar_prefetch=1,
            grid=(1,),
            in_specs=[whole(a)] + [ANY] * len(b_parts) + [whole(w_t), whole(bias), whole(den), whole(z)],
            out_specs=whole(z),
            scratch_shapes=[
                pltpu.VMEM((hid, cols, depth), BF16),
                pltpu.VMEM((rows, hid, hid, cols), BF16),
                pltpu.SemaphoreType.DMA((len(b_parts),)),
            ],
        ),
        out_shape=jax.ShapeDtypeStruct(z.shape, F32),
        compiler_params=pltpu.CompilerParams(vmem_limit_bytes=60 << 20),
        cost_estimate=pl.CostEstimate(flops=12 << 30, bytes_accessed=20 << 20, transcendentals=0),
        name='main_outer',
    )(me, a, *b_parts, w_t, bias, den, z)


def combine_kernel(own_ref, rx_ref, ry_ref, tx_ref, ty_ref, base_ref, den_ref, bias_ref, out_ref):
    step = pl.program_id(0)

    def add(first, second):
        for i in range(out_ref.shape[0]):
            total = own_ref[i].astype(F32) + first[0, i].astype(F32) + second[i].astype(F32)
            out_ref[i] = base_ref[i] + ((total + bias_ref[...]) / den_ref[pl.ds(i, 1), :]).T

    @pl.when(step < pl.num_programs(0) // 2)
    def _():
        add(rx_ref, ty_ref)

    @pl.when(step >= pl.num_programs(0) // 2)
    def _():
        add(ry_ref, tx_ref)


def combine(own, rx, ry, tx, ty, base, den, bias, block=8):
    rows, cols, chans = base.shape
    mid = rows // block // 2
    lower = lambda s: jnp.minimum(s, mid - 1)
    upper = lambda s: jnp.maximum(s - mid, 0)
    flat = lambda: pl.BlockSpec((block, cols, chans), lambda s: (s, 0, 0))
    return pl.pallas_call(
        combine_kernel,
        grid=(2 * mid,),
        in_specs=[
            pl.BlockSpec((block, chans, cols), lambda s: (s, 0, 0)),
            pl.BlockSpec((1, block, chans, cols), lambda s: (1, lower(s), 0, 0)),
            pl.BlockSpec((1, block, chans, cols), lambda s: (1, upper(s), 0, 0)),
            pl.BlockSpec((block, chans, cols), lambda s: (upper(s), 0, 0)),
            pl.BlockSpec((block, chans, cols), lambda s: (lower(s), 0, 0)),
            flat(),
            pl.BlockSpec((block, cols), lambda s: (s, 0)),
            pl.BlockSpec((chans, cols), lambda s: (0, 0)),
        ],
        out_specs=flat(),
        out_shape=jax.ShapeDtypeStruct(base.shape, F32),
        cost_estimate=pl.CostEstimate(flops=1 << 24, bytes_accessed=15 << 20, transcendentals=0),
        name='combine',
    )(own, rx, ry, tx, ty, base, den, bias)


def assemble_kernel(ref, out_ref):
    width = ref.shape[2]
    for d in range(ref.shape[0]):
        out_ref[:, d * width:(d + 1) * width, :] = ref[d]


def assemble(value, block=8):
    srcs, seqs, width, chans = value.shape
    return pl.pallas_call(
        assemble_kernel,
        grid=(seqs // block,),
        in_specs=[pl.BlockSpec((srcs, block, width, chans), lambda s: (0, s, 0, 0))],
        out_specs=pl.BlockSpec((block, srcs * width, chans), lambda s: (s, 0, 0)),
        out_shape=jax.ShapeDtypeStruct((seqs, srcs * width, chans), value.dtype),
        cost_estimate=pl.CostEstimate(flops=1 << 24, bytes_accessed=16 << 20, transcendentals=0),
        name='assemble',
    )(value)


def layer_norm(value, gamma, beta):
    as_float = value.astype(F32)
    mean = jnp.mean(as_float, axis=-1, keepdims=True)
    centered = as_float - mean
    var = jnp.mean(centered * centered, axis=-1, keepdims=True)
    return (centered * lax.rsqrt(var + LN_EPS) * gamma.astype(F32) + beta.astype(F32)).astype(BF16)


def denominators(mask, mask_rows):
    counts = jnp.einsum('si,sj->ij', mask_rows.astype(BF16), mask.astype(BF16), preferred_element_type=F32)
    return NORM_EPS + counts


def solution(mesh):
    size = mesh.shape['dap']
    value_spec = P('data', 'dap', None)
    mask_spec = P('data', None)
    row_spec = P(('data', 'dap'), None, None)

    def local_program(extra_block, extra_mask, main_block, main_mask, pair_rows, eg, eb, ewl, ebl, ewr, ebr, ewo, ebo, mg, mb, mwl, mbl, mwr, mbr, mwo, mbo):
        me = lax.axis_index('dap')
        rows = extra_block.shape[1]
        hid = ewl.shape[1]

        seqs = extra_block.shape[0] // size
        cols = size * rows
        minor = extra_block.transpose(1, 2, 0)
        me1 = me.astype(jnp.int32)[None]
        turned = dict(zip(NEAR, turn(me1, minor, NEAR, size)))
        turned.update(zip(REST, turn(me1, minor, REST, size)))
        blocks = {0: turned[0]}
        for k in NEAR:
            blocks[k] = swap(turned[k], k, size)
        blocks[1] = swap(turned[1], CORE, size)
        near, far = lax.optimization_barrier(([blocks[k] for k in NEAR], [turned[6], turned[7]]))
        blocks.update(zip(NEAR, near))
        for k, value in zip((6, 7), far):
            blocks[k] = swap(value, k, size)

        mask_rows_m = lax.dynamic_slice_in_dim(main_mask, me * rows, rows, axis=1)
        mask_rows_e = lax.dynamic_slice_in_dim(extra_mask, me * rows, rows, axis=1)
        den_m = denominators(main_mask, mask_rows_m)
        den_e = denominators(extra_mask, mask_rows_e)
        normed = layer_norm(main_block, mg, mb)
        mask_m = mask_rows_m.astype(F32).T
        a_m = jnp.einsum('sim,mp->ips', normed, mwl, preferred_element_type=F32) + mbl.astype(F32)[None, :, None]
        a_m = (a_m * mask_m[:, None, :]).astype(BF16).reshape(rows * hid, -1)
        b_m = jnp.einsum('sim,mq->qis', normed, mwr, preferred_element_type=F32) + mbr.astype(F32)[:, None, None]
        b_m = (b_m * mask_m[None]).astype(BF16)

        wide = lambda v, n: jnp.broadcast_to(v.astype(F32)[:, None], (v.shape[0], n))
        mask_seq = lax.dynamic_slice_in_dim(extra_mask, me * seqs, seqs, axis=0).astype(F32).T
        w_both, bias = project_weights(ewl, ebl, ewr, ebr, seqs)
        gamma, beta = wide(eg, seqs), wide(eb, seqs)
        idx_a, idx_b = [(me ^ jnp.array(ks, jnp.int32)).astype(jnp.int32) for ks in (SET_A, SET_B)]
        w_e, w_m = turn_weights(ewo, hid), turn_weights(mwo, hid)
        bias_e, bias_m = wide(ebo, cols), wide(mbo, cols)

        a_a, a_a_give, b_a = project(idx_a, [blocks[k] for k in SET_A], mask_seq, gamma, beta, w_both, bias, hid)
        a_a_sib, b_a_sib = swap(a_a_give, CORE, size), swap(b_a, CORE, size)

        blocks[6], blocks[7], main_moved, b_m = lax.optimization_barrier((blocks[6], blocks[7], main_block, b_m))
        main_moved = lax.all_to_all(main_moved, 'dap', 0, 0, tiled=True).reshape(size, -1, rows, main_block.shape[2])
        b_x, b_y = swap(b_m, XBIT, size), swap(b_m, YBIT, size)
        mid = hid // 2
        b_d = [swap(b_x[:mid], YBIT, size), swap(b_y[mid:], XBIT, size)]
        b_parts = [b_m, b_x, b_y]
        b_parts = b_parts + [swap(part, CORE, size) for part in b_parts]
        b_parts = b_parts + b_d + [swap(part, CORE, size) for part in b_d]
        places = ((0, 0), (XBIT, 0), (YBIT, 0), (CORE, 0), (CORE | XBIT, 0), (CORE | YBIT, 0))
        places = places + ((XBIT | YBIT, 0), (XBIT | YBIT, mid), (CORE | XBIT | YBIT, 0), (CORE | XBIT | YBIT, mid))

        a_b, a_b_give, b_b = project(idx_b, [blocks[k] for k in SET_B], mask_seq, gamma, beta, w_both, bias, hid)
        a_b_sib, b_b_sib = swap(a_b_give, CORE, size), swap(b_b, CORE, size)
        sx, sy, kx, ky, own = extra_parts(me1, (a_a, a_a_sib, a_b, a_b_sib), (b_a, b_a_sib, b_b, b_b_sib), w_e, cols)
        rx, ry = swap(sx, XBIT, size), swap(sy, YBIT, size)
        kx = (kx.astype(F32) + ry[0].astype(F32)).astype(BF16)
        ky = (ky.astype(F32) + rx[0].astype(F32)).astype(BF16)
        tx, ty = swap(kx, XBIT, size), swap(ky, YBIT, size)

        base = main_rows(me1, a_m, b_parts, places, w_m, bias_m, den_m, pair_rows)
        main_out = assemble(main_moved)
        extra_out = turn_out(me1, blocks).transpose(0, 2, 1)
        pair_out = combine(own, rx, ry, tx, ty, base, den_e, bias_e)
        return pair_out, extra_out, main_out

    in_specs = (value_spec, mask_spec, value_spec, mask_spec, row_spec) + (P(),) * 16
    return jax.shard_map(local_program, mesh=mesh, in_specs=in_specs, out_specs=(row_spec, row_spec, row_spec), check_vma=False)
```

time: 431 us -> 448 us (1.039)
  local copies, waits for them, and re-layouts: 76.8 us -> 28.7 us
  Pallas kernels: 123 us -> 169 us
  waiting for transfers between devices: 151 us -> 177 us
  starting transfers between devices: 36.5 us -> 24.3 us
    ppermute x13 -> x24, waiting for transfers between devices: 64.9 us -> 177 us  [swap(): return lax.ppermute(value, 'dap', [(d, d ^ bit) for d in range(size)])]
    all_to_all x2 -> x1, waiting for transfers between devices: 86 us -> 0.01 us  [local_program(): lax.all_to_all(main_moved, 'dap', 0, 0, tiled=True)]
    pallas_call x4 -> x9, Pallas kernels: 123 us -> 169 us  [the longest x1 72.4 us: extra_parts(): pl.pallas_call(functools.partial(extra_kernel, qu, iu), grid_spec=pltpu.P...]
    unnamed x41 -> x96, local copies, waits for them, and re-layouts: 21.9 us -> 4.19 us
    reshape x5 -> x4, local copies, waits for them, and re-layouts: 14.9 us -> 3.08 us  [the longest x2 1.71 us: turn_weights(): return w_out.reshape(hid, hid, -1).transpose(2, 1, 0).reshape(-1, hid * hid)]
    all_to_all x1 -> x0, local copies, waits for them, and re-layouts: 8.24 us -> none  [local_program(): main_out = lax.all_to_all(main_block, 'dap', 0, 1, tiled=True)]
    ppermute x13 -> x24, starting transfers between devices: 28.3 us -> 20.4 us  [swap(): return lax.ppermute(value, 'dap', [(d, d ^ bit) for d in range(size)])]
    slice x3 -> x2, local copies, waits for them, and re-layouts: 8.98 us -> 2.96 us  [local_program(): b_d = [swap(b_x[:mid], YBIT, size), swap(b_y[mid:], XBIT, size)]]
  transfers between devices with their start and end apart: 15 -> 25, of which waited for: 5 -> 10; matrix products, arithmetic and copies ran while one was open for 24% -> 16% of each run, Pallas kernels for 22% -> 31%
where the time goes in v2:
time: 448 us; the launch traced here: 445 us
  waiting for transfers between devices  177 us (40%)
  Pallas kernels  169 us (38%)
  local copies, waits for them, and re-layouts  28.7 us (6%)
  starting transfers between devices  24.3 us (5%)
  matrix products  22.7 us (5%)
  other arithmetic  22.3 us (5%)
    ppermute x24, waiting for transfers between devices, swap(): return lax.ppermute(value, 'dap', [(d, d ^ bit) for d in range(size)])  177 us
    pallas_call x1, Pallas kernels, extra_parts(): pl.pallas_call(functools.partial(extra_kernel, qu, iu), grid_spec=pltpu.P...  72.4 us
    pallas_call x1, Pallas kernels, turn_out(): pl.pallas_call(functools.partial(turn_out_kernel, ks), grid_spec=pltpu.Pr...  28.3 us
    pallas_call x1, Pallas kernels, main_rows(): pl.pallas_call(functools.partial(main_kernel, places, qu, iu), grid_spec=...  20.9 us
    pallas_call x2, Pallas kernels, project(): pl.pallas_call(functools.partial(project_kernel, group), grid_spec=pltpu....  20.6 us
    ppermute x24, starting transfers between devices, swap(): return lax.ppermute(value, 'dap', [(d, d ^ bit) for d in range(size)])  20.4 us
    pallas_call x2, Pallas kernels, turn(): pl.pallas_call(functools.partial(turn_kernel, ks), grid_spec=pltpu.Prefet...  10.8 us
    dot_general x1, matrix products, local_program(): jnp.einsum('sim,mq->qis', normed, mwr, preferred_element_type=F32)  10.3 us
  transfers between devices with their start and end apart: 25, of which 10 were waited for; matrix products, arithmetic and copies ran while one was open for 16% of the time, Pallas kernels for 31%

profile of v2, /device:TPU:0, one launch (start us, length us, event | category | flops | bytes accessed | tf_op | source)
XLA Modules:
  0.0 445.1 jit_solution(5455969993861193918)
XLA Ops:
  0.7 5.4 %turn.3 = (bf16[32,64,384]{2,1,0:T(8,128)(2,1)}, bf16[32,64,384]{2,1,0:T(8,128)(2,1)}, bf16[32,64,384]{2,1,0:T(8,128)(2,1)}, bf16[32,64,384]{2,1,0:T(8,128)(2,1)}) custom-call(s32[1]{0:T(128)} %bitcast.me_ref.idx_ref, bf16[32,64,3072]{2,1,0:T(8,128)(2,1)} %bitcast.51), custom_call_target="tpu_custom_call" | custom-call | flops 16777216 | bytes 4194304 | tf_op jit(solution)/shard_map/turn/pallas_call | solution.py:46
  11.2 5.4 %turn.2 = (bf16[32,64,384]{2,1,0:T(8,128)(2,1)}, bf16[32,64,384]{2,1,0:T(8,128)(2,1)}, bf16[32,64,384]{2,1,0:T(8,128)(2,1)}, bf16[32,64,384]{2,1,0:T(8,128)(2,1)}) custom-call(s32[1]{0:T(128)} %bitcast.me_ref.idx_ref, bf16[32,64,3072]{2,1,0:T(8,128)(2,1)} %bitcast.52), custom_call_target="tpu_custom_call" | custom-call | flops 16777216 | bytes 4194304 | tf_op jit(solution)/shard_map/turn/pallas_call | solution.py:46
  24.3 5.6 %convert_reduce_fusion = f32[512,32]{1,0:T(8,128)S(1)} fusion(bf16[512,32,256]{2,1,0:T(8,128)(2,1)} %param.25), kind=kLoop, calls=%fused_computation.1 | loop fusion | flops 8372224 | bytes 8454144 | tf_op jit(solution)/shard_map/reduce_sum | solution.py:440
  30.8 7.0 %fusion.2 = f32[512,32]{1,0:T(8,128)S(1)} fusion(bf16[512,32,256]{2,1,0:T(8,128)(2,1)} %param.25, f32[512,32]{1,0:T(8,128)S(1)} %broadcast_multiply_fusion), kind=kLoop, calls=%fused_computation.4 | loop fusion | flops 16760832 | bytes 8519680 | tf_op jit(solution)/shard_map/reduce_sum | solution.py:442
  37.9 6.9 %collective-permute-done.refs_1_.refs_2_ = bf16[32,64,384]{2,1,0:T(8,128)(2,1)S(1)} collective-permute-done((bf16[32,64,384]{2,1,0:T(8,128)(2,1)}, bf16[32,64,384]{2,1,0:T(8,128)(2,1)S(1)}, u32[]{:S(2)}, u32[]{:S(2)}) %collective-permute-start) | collective-permute-done | bytes 1572896 | tf_op jit(solution)/shard_map/ppermute | solution.py:23
  47.0 30.1 %collective-permute-done.2.refs_4_.refs_3_ = bf16[32,64,384]{2,1,0:T(8,128)(2,1)} collective-permute-done((bf16[32,64,384]{2,1,0:T(8,128)(2,1)}, bf16[32,64,384]{2,1,0:T(8,128)(2,1)}, u32[]{:S(2)}, u32[]{:S(2)}) %collective-permute-start.2) | collective-permute-done | bytes 1572896 | tf_op jit(solution)/shard_map/ppermute | solution.py:23
  78.7 14.7 %project.2 = (bf16[3,1024,384]{2,1,0:T(8,128)(2,1)}, bf16[3,1024,384]{2,1,0:T(8,128)(2,1)}, bf16[6,32,32,384]{3,2,1,0:T(8,128)(2,1)}) custom-call(s32[6]{0:T(128)S(1)} %copy-done.14, bf16[32,64,384]{2,1,0:T(8,128)(2,1)S(1)} %copy-done.3, bf16[32,64,384]{2,1,0:T(8,128)(2,1)S(1)} %collective-permute-done.refs_1_.refs_2_, ...), custom_call_target="tpu_custom_call" | custom-call | flops 6442450944 | bytes 13631488 | tf_op jit(solution)/shard_map/project/pallas_call | solution.py:161
  94.3 7.7 %fusion.6 = f32[512,32,32]{2,1,0:T(8,128)} fusion(bf16[512,32,256]{2,1,0:T(8,128)(2,1)S(1)} %bitcast.50, f32[256]{0:T(256)S(1)} %convert_element_type.92, f32[256]{0:T(256)S(1)} %convert_element_type.91, f32[512,32]{1,0:T(8,128)S(1)} %add_rsqrt_fusion, f32[512,32]{1,0:T(8,128)S(1)} %broadcast_multiply_fusion, bf16[256,32]{0,1:T(8,128)(2,1)S(1)} %copy-done), kind=kOutput, calls=%fused_computation.8 | convolution fusion | flops 293601280 | bytes 10635264 | tf_op jit(solution)/shard_map/sim,mp->ips/dot_general | solution.py:483
  102.0 6.3 %copy.59 = f32[512,32,32]{0,2,1:T(8,128)} copy(f32[512,32,32]{2,1,0:T(8,128)} %fusion.6) | data formatting | bytes 4194304 | tf_op jit(solution)/shard_map/sim,mp->ips/dot_general | solution.py:483
  111.5 10.3 %fusion.8 = f32[512,32,32]{2,1,0:T(8,128)} fusion(bf16[512,32,256]{2,1,0:T(8,128)(2,1)} %param.25, f32[256]{0:T(256)S(1)} %copy-done.40, f32[256]{0:T(256)S(1)} %copy-done.42, f32[512,32]{1,0:T(8,128)} %copy-done.28, f32[512,32]{1,0:T(8,128)} %copy-done.25, bf16[256,32]{0,1:T(8,128)(2,1)} %param.40), kind=kOutput, calls=%fused_computation.9 | convolution fusion | flops 293601280 | bytes 10635264 | tf_op jit(solution)/shard_map/sim,mq->qis/dot_general | solution.py:485
  121.8 6.7 %copy.55 = f32[512,32,32]{0,1,2:T(8,128)} copy(f32[512,32,32]{2,1,0:T(8,128)} %fusion.8) | data formatting | bytes 4194304 | tf_op jit(solution)/shard_map/sim,mq->qis/dot_general | solution.py:485
  128.5 4.0 fusion.12
  133.3 14.3 %collective-permute-done.6.refs_0_.refs_6_ = bf16[32,64,384]{2,1,0:T(8,128)(2,1)S(1)} collective-permute-done((bf16[32,64,384]{2,1,0:T(8,128)(2,1)}, bf16[32,64,384]{2,1,0:T(8,128)(2,1)S(1)}, u32[]{:S(2)}, u32[]{:S(2)}) %collective-permute-start.6) | collective-permute-done | bytes 1572896 | tf_op jit(solution)/shard_map/ppermute | solution.py:23
  147.6 31.8 %collective-permute-done.7.refs_1_.refs_7_ = bf16[32,64,384]{2,1,0:T(8,128)(2,1)S(1)} collective-permute-done((bf16[32,64,384]{2,1,0:T(8,128)(2,1)}, bf16[32,64,384]{2,1,0:T(8,128)(2,1)S(1)}, u32[]{:S(2)}, u32[]{:S(2)}) %collective-permute-start.7) | collective-permute-done | bytes 1572896 | tf_op jit(solution)/shard_map/ppermute | solution.py:23
  180.6 5.9 %project.3 = (bf16[1,1024,384]{2,1,0:T(8,128)(2,1)S(1)}, bf16[1,1024,384]{2,1,0:T(8,128)(2,1)S(1)}, bf16[2,32,32,384]{3,2,1,0:T(8,128)(2,1)S(1)}) custom-call(s32[2]{0:T(128)S(1)} %broadcast_xor_fusion.idx_ref, bf16[32,64,384]{2,1,0:T(8,128)(2,1)} %copy-done.17, bf16[32,64,384]{2,1,0:T(8,128)(2,1)} %copy-done.18, ...), custom_call_target="tpu_custom_call" | custom-call | flops 6442450944 | bytes 13631488 | tf_op jit(solution)/shard_map/project/pallas_call | solution.py:161
  188.7 3.9 all-to-all-start
  194.4 72.4 %extra_outer.1 = (bf16[2,16,128,256]{3,2,1,0:T(8,128)(2,1)}, bf16[2,16,128,256]{3,2,1,0:T(8,128)(2,1)}, bf16[16,128,256]{2,1,0:T(8,128)(2,1)}, bf16[16,128,256]{2,1,0:T(8,128)(2,1)}, bf16[32,128,256]{2,1,0:T(8,128)(2,1)}) custom-call(s32[1]{0:T(128)} %bitcast.me_ref.idx_ref, bf16[3,1024,384]{2,1,0:T(8,128)(2,1)} %get-tuple-element.44.refs_0_, ...), custom_call_target="tpu_custom_call" | custom-call | flops 64424509440 | bytes 33554432 | tf_op jit(solution)/shard_map/extra_outer/pallas_call | solution.py:308
  271.5 37.1 %collective-permute-done.16.refs_2_ = bf16[32,32,512]{2,1,0:T(8,128)(2,1)} collective-permute-done((bf16[32,32,512]{2,1,0:T(8,128)(2,1)}, bf16[32,32,512]{2,1,0:T(8,128)(2,1)}, u32[]{:S(2)}, u32[]{:S(2)}) %collective-permute-start.16) | collective-permute-done | bytes 1048608 | tf_op jit(solution)/shard_map/ppermute | solution.py:23
  312.9 51.3 %collective-permute-done.20.refs_6_ = bf16[16,32,512]{2,1,0:T(8,128)(2,1)} collective-permute-done((bf16[16,32,512]{2,1,0:T(8,128)(2,1)S(1)}, bf16[16,32,512]{2,1,0:T(8,128)(2,1)}, u32[]{:S(2)}, u32[]{:S(2)}) %collective-permute-start.20) | collective-permute-done | bytes 524320 | tf_op jit(solution)/shard_map/ppermute | solution.py:23
  365.6 3.8 fusion.16.den_ref
  369.4 28.3 %turn_out.1 = bf16[384,64,256]{2,1,0:T(8,128)(2,1)} custom-call(s32[1]{0:T(128)} %bitcast.me_ref.idx_ref, bf16[32,64,384]{2,1,0:T(8,128)(2,1)} %get-tuple-element.32.refs_0_, bf16[32,64,384]{2,1,0:T(8,128)(2,1)} %collective-permute-done.4.refs_3_.refs_1_, bf16[32,64,384]{2,1,0:T(8,128)(2,1)} %copy-done.2, ...), custom_call_target="tpu_custom_call" | custom-call | flops 16777216 | bytes 26214400 | tf_op jit(solution)/shard_map/turn_out/pallas_call | solution.py:79
  405.2 20.9 %main_outer.1.base_ref = f32[32,256,128]{2,1,0:T(8,128)} custom-call(s32[1]{0:T(128)} %bitcast.me_ref.idx_ref, bf16[1024,512]{1,0:T(8,128)(2,1)} %bitcast.56, bf16[32,32,512]{2,1,0:T(8,128)(2,1)} %get-tuple-element.59.refs_0_, bf16[32,32,512]{2,1,0:T(8,128)(2,1)} %collective-permute-done.15.refs_1_, bf16[32,32,512]{2,1,0:T(8,128)(2,1)} %collective-permute-done.16.refs_2_, ...), custom_call_target="tpu_custom_call" | custom-call | flops 12884901888 | bytes 20971520 | tf_op jit(solution)/shard_map/main_outer/pallas_call | solution.py:356
  429.0 7.2 %combine.1 = f32[32,256,128]{2,1,0:T(8,128)} custom-call(bf16[32,128,256]{2,1,0:T(8,128)(2,1)} %get-tuple-element.54.own_ref, bf16[2,16,128,256]{3,2,1,0:T(8,128)(2,1)} %copy-done.16, bf16[2,16,128,256]{3,2,1,0:T(8,128)(2,1)} %collective-permute-done.12.ry_ref, bf16[16,128,256]{2,1,0:T(8,128)(2,1)} %copy-done.23, bf16[16,128,256]{2,1,0:T(8,128)(2,1)} %copy-done.24, ...), custom_call_target="tpu_custom_call" | custom-call | flops 16777216 | bytes 15728640 | tf_op jit(solution)/shard_map/combine/pallas_call | solution.py:399
  436.1 9.0 %assemble.1 = bf16[64,256,256]{2,1,0:T(8,128)(2,1)} custom-call(bf16[8,64,32,256]{3,2,1,0:T(8,128)(2,1)} %bitcast.20.ref), custom_call_target="tpu_custom_call" | custom-call | flops 16777216 | bytes 16777216 | tf_op jit(solution)/shard_map/assemble/pallas_call | solution.py:427
  (177 shorter events, 47.9 us)
Async XLA Ops:
  6.0 38.8 %collective-permute-start = (bf16[32,64,384]{2,1,0:T(8,128)(2,1)}, bf16[32,64,384]{2,1,0:T(8,128)(2,1)S(1)}, u32[]{:S(2)}, u32[]{:S(2)}) collective-permute-start(bf16[32,64,384]{2,1,0:T(8,128)(2,1)} %get-tuple-element.33), channel_id=1, source_target_pairs={{0,2},{1,3},{2,0},{3,1},{4,6},{5,7},{6,4},{7,5}} | collective-permute-start | bytes 4718600 | tf_op jit(solution)/shard_map/ppermute | solution.py:23
  9.4 37.6 %collective-permute-start.1 = (bf16[32,64,384]{2,1,0:T(8,128)(2,1)}, bf16[32,64,384]{2,1,0:T(8,128)(2,1)}, u32[]{:S(2)}, u32[]{:S(2)}) collective-permute-start(bf16[32,64,384]{2,1,0:T(8,128)(2,1)} %get-tuple-element.34), channel_id=1, source_target_pairs={{0,4},{1,5},{2,6},{3,7},{4,0},{5,1},{6,2},{7,3}} | collective-permute-start | bytes 4718600 | tf_op jit(solution)/shard_map/ppermute | solution.py:23
  10.9 66.2 %collective-permute-start.2 = (bf16[32,64,384]{2,1,0:T(8,128)(2,1)}, bf16[32,64,384]{2,1,0:T(8,128)(2,1)}, u32[]{:S(2)}, u32[]{:S(2)}) collective-permute-start(bf16[32,64,384]{2,1,0:T(8,128)(2,1)} %get-tuple-element.35), channel_id=1, source_target_pairs={{0,3},{1,2},{2,1},{3,0},{4,7},{5,6},{6,5},{7,4}} | collective-permute-start | bytes 4718600 | tf_op jit(solution)/shard_map/ppermute | solution.py:23
  10.9 67.4 %collective-permute-start.3 = (bf16[32,64,384]{2,1,0:T(8,128)(2,1)}, bf16[32,64,384]{2,1,0:T(8,128)(2,1)}, u32[]{:S(2)}, u32[]{:S(2)}) collective-permute-start(bf16[32,64,384]{2,1,0:T(8,128)(2,1)} %get-tuple-element.36), channel_id=1, source_target_pairs={{0,5},{1,4},{2,7},{3,6},{4,1},{5,0},{6,3},{7,2}} | collective-permute-start | bytes 4718600 | tf_op jit(solution)/shard_map/ppermute | solution.py:23
  16.6 61.7 %collective-permute-start.4 = (bf16[32,64,384]{2,1,0:T(8,128)(2,1)}, bf16[32,64,384]{2,1,0:T(8,128)(2,1)}, u32[]{:S(2)}, u32[]{:S(2)}) collective-permute-start(bf16[32,64,384]{2,1,0:T(8,128)(2,1)} %get-tuple-element.41), channel_id=1, source_target_pairs={{0,1},{1,0},{2,3},{3,2},{4,5},{5,4},{6,7},{7,6}} | collective-permute-start | bytes 4718600 | tf_op jit(solution)/shard_map/ppermute | solution.py:23
  93.5 100.9 %collective-permute-start.9 = (bf16[6,32,32,384]{3,2,1,0:T(8,128)(2,1)}, bf16[6,32,32,384]{3,2,1,0:T(8,128)(2,1)}, u32[]{:S(2)}, u32[]{:S(2)}) collective-permute-start(bf16[6,32,32,384]{3,2,1,0:T(8,128)(2,1)} %get-tuple-element.52.refs_4_), channel_id=1, source_target_pairs={{0,1},{1,0},{2,3},{3,2},{4,5},{5,4},{6,7},{7,6}} | collective-permute-start | bytes 14155784 | tf_op jit(solution)/shard_map/ppermute | solution.py:23
  109.2 38.4 %collective-permute-start.6 = (bf16[32,64,384]{2,1,0:T(8,128)(2,1)}, bf16[32,64,384]{2,1,0:T(8,128)(2,1)S(1)}, u32[]{:S(2)}, u32[]{:S(2)}) collective-permute-start(bf16[32,64,384]{2,1,0:T(8,128)(2,1)} %get-tuple-element.46), channel_id=1, source_target_pairs={{0,6},{1,7},{2,4},{3,5},{4,2},{5,3},{6,0},{7,1}} | collective-permute-start | bytes 4718600 | tf_op jit(solution)/shard_map/ppermute | solution.py:23
  110.7 68.7 %collective-permute-start.7 = (bf16[32,64,384]{2,1,0:T(8,128)(2,1)}, bf16[32,64,384]{2,1,0:T(8,128)(2,1)S(1)}, u32[]{:S(2)}, u32[]{:S(2)}) collective-permute-start(bf16[32,64,384]{2,1,0:T(8,128)(2,1)} %get-tuple-element.47), channel_id=1, source_target_pairs={{0,7},{1,6},{2,5},{3,4},{4,3},{5,2},{6,1},{7,0}} | collective-permute-start | bytes 4718600 | tf_op jit(solution)/shard_map/ppermute | solution.py:23
  132.6 60.0 %collective-permute-start.5 = (bf16[3,1024,384]{2,1,0:T(8,128)(2,1)}, bf16[3,1024,384]{2,1,0:T(8,128)(2,1)}, u32[]{:S(2)}, u32[]{:S(2)}) collective-permute-start(bf16[3,1024,384]{2,1,0:T(8,128)(2,1)} %get-tuple-element.45), channel_id=1, source_target_pairs={{0,1},{1,0},{2,3},{3,2},{4,5},{5,4},{6,7},{7,6}} | collective-permute-start | bytes 7077896 | tf_op jit(solution)/shard_map/ppermute | solution.py:23
  186.6 7.8 %collective-permute-start.10 = (bf16[2,32,32,384]{3,2,1,0:T(8,128)(2,1)S(1)}, bf16[2,32,32,384]{3,2,1,0:T(8,128)(2,1)}, u32[]{:S(2)}, u32[]{:S(2)}) collective-permute-start(bf16[2,32,32,384]{3,2,1,0:T(8,128)(2,1)S(1)} %get-tuple-element.53.refs_6_), channel_id=1, source_target_pairs={{0,1},{1,0},{2,3},{3,2},{4,5},{5,4},{6,7},{7,6}} | collective-permute-start | bytes 4718600 | tf_op jit(solution)/shard_map/ppermute | solution.py:23
  187.3 7.0 %collective-permute-start.8 = (bf16[1,1024,384]{2,1,0:T(8,128)(2,1)S(1)}, bf16[1,1024,384]{2,1,0:T(8,128)(2,1)}, u32[]{:S(2)}, u32[]{:S(2)}) collective-permute-start(bf16[1,1024,384]{2,1,0:T(8,128)(2,1)S(1)} %get-tuple-element.51), channel_id=1, source_target_pairs={{0,1},{1,0},{2,3},{3,2},{4,5},{5,4},{6,7},{7,6}} | collective-permute-start | bytes 2359304 | tf_op jit(solution)/shard_map/ppermute | solution.py:23
  188.3 80.5 %collective-permute-start.15 = (bf16[32,32,512]{2,1,0:T(8,128)(2,1)}, bf16[32,32,512]{2,1,0:T(8,128)(2,1)}, u32[]{:S(2)}, u32[]{:S(2)}) collective-permute-start(bf16[32,32,512]{2,1,0:T(8,128)(2,1)} %get-tuple-element.59.refs_0_), channel_id=1, source_target_pairs={{0,2},{1,3},{2,0},{3,1},{4,6},{5,7},{6,4},{7,5}} | collective-permute-start | bytes 3145736 | tf_op jit(solution)/shard_map/ppermute | solution.py:23
  188.7 247.4 %all-to-all-start = ((bf16[512,32,256]{2,1,0:T(8,128)(2,1)}), bf16[512,32,256]{2,1,0:T(8,128)(2,1)}, u32[]{:S(2)}, u32[]{:S(2)}) async-start(bf16[512,32,256]{2,1,0:T(8,128)(2,1)} %param.25), calls=%async_computation | async-start | bytes 16777216 | tf_op jit(solution)/shard_map/all_to_all | solution.py:500
  192.6 115.9 %collective-permute-start.16 = (bf16[32,32,512]{2,1,0:T(8,128)(2,1)}, bf16[32,32,512]{2,1,0:T(8,128)(2,1)}, u32[]{:S(2)}, u32[]{:S(2)}) collective-permute-start(bf16[32,32,512]{2,1,0:T(8,128)(2,1)} %get-tuple-element.59.refs_0_), channel_id=1, source_target_pairs={{0,4},{1,5},{2,6},{3,7},{4,0},{5,1},{6,2},{7,3}} | collective-permute-start | bytes 3145736 | tf_op jit(solution)/shard_map/ppermute | solution.py:23
  266.8 130.9 %collective-permute-start.11 = (bf16[2,16,128,256]{3,2,1,0:T(8,128)(2,1)}, bf16[2,16,128,256]{3,2,1,0:T(8,128)(2,1)S(1)}, u32[]{:S(2)}, u32[]{:S(2)}) collective-permute-start(bf16[2,16,128,256]{3,2,1,0:T(8,128)(2,1)} %get-tuple-element.55), channel_id=1, source_target_pairs={{0,2},{1,3},{2,0},{3,1},{4,6},{5,7},{6,4},{7,5}} | collective-permute-start | bytes 6291464 | tf_op jit(solution)/shard_map/ppermute | solution.py:23
  268.3 129.4 %collective-permute-start.12 = (bf16[2,16,128,256]{3,2,1,0:T(8,128)(2,1)}, bf16[2,16,128,256]{3,2,1,0:T(8,128)(2,1)}, u32[]{:S(2)}, u32[]{:S(2)}) collective-permute-start(bf16[2,16,128,256]{3,2,1,0:T(8,128)(2,1)} %get-tuple-element.56), channel_id=1, source_target_pairs={{0,4},{1,5},{2,6},{3,7},{4,0},{5,1},{6,2},{7,3}} | collective-permute-start | bytes 6291464 | tf_op jit(solution)/shard_map/ppermute | solution.py:23
  269.9 94.2 %collective-permute-start.20 = (bf16[16,32,512]{2,1,0:T(8,128)(2,1)S(1)}, bf16[16,32,512]{2,1,0:T(8,128)(2,1)}, u32[]{:S(2)}, u32[]{:S(2)}) collective-permute-start(bf16[16,32,512]{2,1,0:T(8,128)(2,1)S(1)} %slice.18), channel_id=1, source_target_pairs={{0,4},{1,5},{2,6},{3,7},{4,0},{5,1},{6,2},{7,3}} | collective-permute-start | bytes 1572872 | tf_op jit(solution)/shard_map/ppermute | solution.py:23
  310.4 53.7 %collective-permute-start.21 = (bf16[16,32,512]{2,1,0:T(8,128)(2,1)}, bf16[16,32,512]{2,1,0:T(8,128)(2,1)}, u32[]{:S(2)}, u32[]{:S(2)}) collective-permute-start(bf16[16,32,512]{2,1,0:T(8,128)(2,1)} %slice.19), channel_id=1, source_target_pairs={{0,2},{1,3},{2,0},{3,1},{4,6},{5,7},{6,4},{7,5}} | collective-permute-start | bytes 1572872 | tf_op jit(solution)/shard_map/ppermute | solution.py:23
  312.9 88.8 %collective-permute-start.17 = (bf16[32,32,512]{2,1,0:T(8,128)(2,1)}, bf16[32,32,512]{2,1,0:T(8,128)(2,1)}, u32[]{:S(2)}, u32[]{:S(2)}) collective-permute-start(bf16[32,32,512]{2,1,0:T(8,128)(2,1)} %get-tuple-element.59.refs_0_), channel_id=1, source_target_pairs={{0,1},{1,0},{2,3},{3,2},{4,5},{5,4},{6,7},{7,6}} | collective-permute-start | bytes 3145736 | tf_op jit(solution)/shard_map/ppermute | solution.py:23
  364.1 39.5 %collective-permute-start.18 = (bf16[32,32,512]{2,1,0:T(8,128)(2,1)}, bf16[32,32,512]{2,1,0:T(8,128)(2,1)}, u32[]{:S(2)}, u32[]{:S(2)}) collective-permute-start(bf16[32,32,512]{2,1,0:T(8,128)(2,1)} %collective-permute-done.15.refs_1_), channel_id=1, source_target_pairs={{0,1},{1,0},{2,3},{3,2},{4,5},{5,4},{6,7},{7,6}} | collective-permute-start | bytes 3145736 | tf_op jit(solution)/shard_map/ppermute | solution.py:23
  364.2 39.5 %collective-permute-start.19 = (bf16[32,32,512]{2,1,0:T(8,128)(2,1)}, bf16[32,32,512]{2,1,0:T(8,128)(2,1)}, u32[]{:S(2)}, u32[]{:S(2)}) collective-permute-start(bf16[32,32,512]{2,1,0:T(8,128)(2,1)} %collective-permute-done.16.refs_2_), channel_id=1, source_target_pairs={{0,1},{1,0},{2,3},{3,2},{4,5},{5,4},{6,7},{7,6}} | collective-permute-start | bytes 3145736 | tf_op jit(solution)/shard_map/ppermute | solution.py:23
  397.7 5.9 %collective-permute-start.23 = (bf16[16,32,512]{2,1,0:T(8,128)(2,1)}, bf16[16,32,512]{2,1,0:T(8,128)(2,1)S(1)}, u32[]{:S(2)}, u32[]{:S(2)}) collective-permute-start(bf16[16,32,512]{2,1,0:T(8,128)(2,1)} %collective-permute-done.21.refs_7_), channel_id=1, source_target_pairs={{0,1},{1,0},{2,3},{3,2},{4,5},{5,4},{6,7},{7,6}} | collective-permute-start | bytes 1572872 | tf_op jit(solution)/shard_map/ppermute | solution.py:23
  401.6 25.3 %collective-permute-start.13 = (bf16[16,128,256]{2,1,0:T(8,128)(2,1)}, bf16[16,128,256]{2,1,0:T(8,128)(2,1)S(1)}, u32[]{:S(2)}, u32[]{:S(2)}) collective-permute-start(bf16[16,128,256]{2,1,0:T(8,128)(2,1)} %fusion.11), channel_id=1, source_target_pairs={{0,2},{1,3},{2,0},{3,1},{4,6},{5,7},{6,4},{7,5}} | collective-permute-start | bytes 3145736 | tf_op jit(solution)/shard_map/ppermute | solution.py:23
  403.1 24.8 %collective-permute-start.14 = (bf16[16,128,256]{2,1,0:T(8,128)(2,1)S(1)}, bf16[16,128,256]{2,1,0:T(8,128)(2,1)S(1)}, u32[]{:S(2)}, u32[]{:S(2)}) collective-permute-start(bf16[16,128,256]{2,1,0:T(8,128)(2,1)S(1)} %fusion.10), channel_id=1, source_target_pairs={{0,4},{1,5},{2,6},{3,7},{4,0},{5,1},{6,2},{7,3}} | collective-permute-start | bytes 3145736 | tf_op jit(solution)/shard_map/ppermute | solution.py:23
  (48 other events, 1337.7 us)

commit v3 on v2

--- a/solution.py
+++ b/solution.py
@@ -218,7 +218,7 @@
 
 def extra_kernel(qu, iu, me_ref, *refs):
     (a_a, a_a_sib, a_b, a_b_sib), b_refs = refs[:4], refs[4:8]
-    w_ref, sx, sy, kx, ky, own, a_v, b_v, o_v, r_v, sa, sb, so = refs[8:]
+    w_ref, fx, fy, nx, ny, kx, ky, own, a_v, b_v, o_v, r_v, sa, sb, so = refs[8:]
     step = pl.program_id(0)
     slot = lax.rem(step, 2)
     half = kx.shape[0]
@@ -244,7 +244,7 @@
         return out
 
     def out_copies(t):
-        lower, upper = ((sx.at[0], sy.at[0]), (sx.at[1], kx), (ky, sy.at[1]), (own.at[lo], own.at[hi]))[t]
+        lower, upper = ((fx, fy), (nx, kx), (ky, ny), (own.at[lo], own.at[hi]))[t]
         sl = t % 2
         return [
             pltpu.make_async_copy(r_v.at[sl, lo], lower, so.at[sl, 0]),
@@ -311,7 +311,7 @@
             num_scalar_prefetch=1,
             grid=(4,),
             in_specs=[ANY] * 8 + [pl.BlockSpec(w_t.shape, lambda s, i: (0, 0))],
-            out_specs=[ANY] * 5,
+            out_specs=[ANY] * 7,
             scratch_shapes=[
                 pltpu.VMEM((2, rows * hid, depth), BF16),
                 pltpu.VMEM((hid, cols, depth), BF16),
@@ -322,7 +322,7 @@
                 pltpu.SemaphoreType.DMA((2, 2)),
             ],
         ),
-        out_shape=[part(2, half), part(2, half), part(half), part(half), part(rows)],
+        out_shape=[part(half)] * 6 + [part(rows)],
         compiler_params=pltpu.CompilerParams(vmem_limit_bytes=60 << 20),
         cost_estimate=pl.CostEstimate(flops=60 << 30, bytes_accessed=32 << 20, transcendentals=0),
         name='extra_outer',
@@ -331,7 +331,7 @@
 
 def main_kernel(places, qu, iu, idx_ref, a_ref, *refs):
     b_refs = refs[:len(places)]
-    w_ref, bias_ref, den_ref, z_ref, out_ref, b_v, o_v, sb = refs[len(places):]
+    w_ref, bias_ref, inv_ref, z_ref, out_ref, b_v, o_v, sb = refs[len(places):]
     copies = []
     for t, (ref, (k, first)) in enumerate(zip(b_refs, places)):
         count, width = ref.shape[:2]
@@ -344,12 +344,12 @@
     outer_rows(a_ref, b_v, o_v, qu)
 
     def store(i, r):
-        out_ref[i] = z_ref[i] + ((r + bias_ref[...]) / den_ref[pl.ds(i, 1), :]).T
+        out_ref[i] = z_ref[i] + ((r + bias_ref[...]) * inv_ref[pl.ds(i, 1), :]).T
 
     weigh_rows(w_ref, o_v, iu, store)
 
 
-def main_rows(me, a, b_parts, places, w_t, bias, den, z, qu=8, iu=8):
+def main_rows(me, a, b_parts, places, w_t, bias, inv, z, qu=8, iu=8):
     hid, _, depth = b_parts[0].shape
     rows, cols, _ = z.shape
     whole = lambda v: pl.BlockSpec(v.shape, lambda s, i: (0,) * v.ndim)
@@ -358,7 +358,7 @@
         grid_spec=pltpu.PrefetchScalarGridSpec(
             num_scalar_prefetch=1,
             grid=(1,),
-            in_specs=[whole(a)] + [ANY] * len(b_parts) + [whole(w_t), whole(bias), whole(den), whole(z)],
+            in_specs=[whole(a)] + [ANY] * len(b_parts) + [whole(w_t), whole(bias), whole(inv), whole(z)],
             out_specs=whole(z),
             scratch_shapes=[
                 pltpu.VMEM((hid, cols, depth), BF16),
@@ -370,50 +370,53 @@
         compiler_params=pltpu.CompilerParams(vmem_limit_bytes=60 << 20),
         cost_estimate=pl.CostEstimate(flops=12 << 30, bytes_accessed=20 << 20, transcendentals=0),
         name='main_outer',
-    )(me, a, *b_parts, w_t, bias, den, z)
-
-
-def combine_kernel(own_ref, rx_ref, ry_ref, tx_ref, ty_ref, base_ref, den_ref, bias_ref, out_ref):
+    )(me, a, *b_parts, w_t, bias, inv, z)
+
+
+def combine_kernel(base_ref, inv_ref, lower_ref, upper_ref, *refs):
     step = pl.program_id(0)
-
-    def add(first, second):
+    out_ref = refs[-1]
+
+    def add(ref):
         for i in range(out_ref.shape[0]):
-            total = own_ref[i].astype(F32) + first[0, i].astype(F32) + second[i].astype(F32)
-            out_ref[i] = base_ref[i] + ((total + bias_ref[...]) / den_ref[pl.ds(i, 1), :]).T
+            total = ref[i].astype(F32)
+            if len(refs) > 1:
+                total = total + refs[0][i].astype(F32) + refs[1][...]
+            row = step * out_ref.shape[0] + i
+            out_ref[i] = base_ref[i] + (total * inv_ref[pl.ds(row, 1), :]).T
 
     @pl.when(step < pl.num_programs(0) // 2)
     def _():
-        add(rx_ref, ty_ref)
+        add(lower_ref)
 
     @pl.when(step >= pl.num_programs(0) // 2)
     def _():
-        add(ry_ref, tx_ref)
-
-
-def combine(own, rx, ry, tx, ty, base, den, bias, block=8):
+        add(upper_ref)
+
+
+def combine(base, inv, lower, upper, own=None, bias=None, block=16):
     rows, cols, chans = base.shape
     mid = rows // block // 2
-    lower = lambda s: jnp.minimum(s, mid - 1)
-    upper = lambda s: jnp.maximum(s - mid, 0)
     flat = lambda: pl.BlockSpec((block, cols, chans), lambda s: (s, 0, 0))
+    extra, extra_specs = (), []
+    if own is not None:
+        extra = (own, bias)
+        extra_specs = [pl.BlockSpec((block, chans, cols), lambda s: (s, 0, 0)), pl.BlockSpec((chans, cols), lambda s: (0, 0))]
     return pl.pallas_call(
         combine_kernel,
         grid=(2 * mid,),
         in_specs=[
-            pl.BlockSpec((block, chans, cols), lambda s: (s, 0, 0)),
-            pl.BlockSpec((1, block, chans, cols), lambda s: (1, lower(s), 0, 0)),
-            pl.BlockSpec((1, block, chans, cols), lambda s: (1, upper(s), 0, 0)),
-            pl.BlockSpec((block, chans, cols), lambda s: (upper(s), 0, 0)),
-            pl.BlockSpec((block, chans, cols), lambda s: (lower(s), 0, 0)),
             flat(),
-            pl.BlockSpec((block, cols), lambda s: (s, 0)),
-            pl.BlockSpec((chans, cols), lambda s: (0, 0)),
-        ],
+            pl.BlockSpec((rows, cols), lambda s: (0, 0)),
+            pl.BlockSpec((block, chans, cols), lambda s: (jnp.minimum(s, mid - 1), 0, 0)),
+            pl.BlockSpec((block, chans, cols), lambda s: (jnp.maximum(s - mid, 0), 0, 0)),
+        ] + extra_specs,
         out_specs=flat(),
         out_shape=jax.ShapeDtypeStruct(base.shape, F32),
+        compiler_params=pltpu.CompilerParams(vmem_limit_bytes=24 << 20),
         cost_estimate=pl.CostEstimate(flops=1 << 24, bytes_accessed=15 << 20, transcendentals=0),
         name='combine',
-    )(own, rx, ry, tx, ty, base, den, bias)
+    )(base, inv, lower, upper, *extra)
 
 
 def assemble_kernel(ref, out_ref):
@@ -443,9 +446,9 @@
     return (centered * lax.rsqrt(var + LN_EPS) * gamma.astype(F32) + beta.astype(F32)).astype(BF16)
 
 
-def denominators(mask, mask_rows):
+def inverse_norms(mask, mask_rows):
     counts = jnp.einsum('si,sj->ij', mask_rows.astype(BF16), mask.astype(BF16), preferred_element_type=F32)
-    return NORM_EPS + counts
+    return 1.0 / (NORM_EPS + counts)
 
 
 def solution(mesh):
@@ -463,21 +466,24 @@
         cols = size * rows
         minor = extra_block.transpose(1, 2, 0)
         me1 = me.astype(jnp.int32)[None]
-        turned = dict(zip(NEAR, turn(me1, minor, NEAR, size)))
+        turned = dict(zip(NEAR[:2], turn(me1, minor, NEAR[:2], size)))
+        turned.update(zip(NEAR[2:], turn(me1, minor, NEAR[2:], size)))
         turned.update(zip(REST, turn(me1, minor, REST, size)))
         blocks = {0: turned[0]}
-        for k in NEAR:
+        for k in NEAR[:2]:
+            blocks[k] = swap(turned[k], k, size)
+        for k in NEAR[2:]:
             blocks[k] = swap(turned[k], k, size)
         blocks[1] = swap(turned[1], CORE, size)
-        near, far = lax.optimization_barrier(([blocks[k] for k in NEAR], [turned[6], turned[7]]))
-        blocks.update(zip(NEAR, near))
+        near, far = lax.optimization_barrier(([blocks[k] for k in NEAR[:2]], [turned[6], turned[7]]))
+        blocks.update(zip(NEAR[:2], near))
         for k, value in zip((6, 7), far):
             blocks[k] = swap(value, k, size)
 
         mask_rows_m = lax.dynamic_slice_in_dim(main_mask, me * rows, rows, axis=1)
         mask_rows_e = lax.dynamic_slice_in_dim(extra_mask, me * rows, rows, axis=1)
-        den_m = denominators(main_mask, mask_rows_m)
-        den_e = denominators(extra_mask, mask_rows_e)
+        inv_m = inverse_norms(main_mask, mask_rows_m)
+        inv_e = inverse_norms(extra_mask, mask_rows_e)
         normed = layer_norm(main_block, mg, mb)
         mask_m = mask_rows_m.astype(F32).T
         a_m = jnp.einsum('sim,mp->ips', normed, mwl, preferred_element_type=F32) + mbl.astype(F32)[None, :, None]
@@ -496,7 +502,7 @@
         a_a, a_a_give, b_a = project(idx_a, [blocks[k] for k in SET_A], mask_seq, gamma, beta, w_both, bias, hid)
         a_a_sib, b_a_sib = swap(a_a_give, CORE, size), swap(b_a, CORE, size)
 
-        blocks[6], blocks[7], main_moved, b_m = lax.optimization_barrier((blocks[6], blocks[7], main_block, b_m))
+        blocks[6], blocks[7], main_moved = lax.optimization_barrier((blocks[6], blocks[7], main_block))
         main_moved = lax.all_to_all(main_moved, 'dap', 0, 0, tiled=True).reshape(size, -1, rows, main_block.shape[2])
         b_x, b_y = swap(b_m, XBIT, size), swap(b_m, YBIT, size)
         mid = hid // 2
@@ -509,16 +515,18 @@
 
         a_b, a_b_give, b_b = project(idx_b, [blocks[k] for k in SET_B], mask_seq, gamma, beta, w_both, bias, hid)
         a_b_sib, b_b_sib = swap(a_b_give, CORE, size), swap(b_b, CORE, size)
-        sx, sy, kx, ky, own = extra_parts(me1, (a_a, a_a_sib, a_b, a_b_sib), (b_a, b_a_sib, b_b, b_b_sib), w_e, cols)
-        rx, ry = swap(sx, XBIT, size), swap(sy, YBIT, size)
-        kx = (kx.astype(F32) + ry[0].astype(F32)).astype(BF16)
-        ky = (ky.astype(F32) + rx[0].astype(F32)).astype(BF16)
-        tx, ty = swap(kx, XBIT, size), swap(ky, YBIT, size)
-
-        base = main_rows(me1, a_m, b_parts, places, w_m, bias_m, den_m, pair_rows)
+        fx, fy, nx, ny, kx, ky, own = extra_parts(me1, (a_a, a_a_sib, a_b, a_b_sib), (b_a, b_a_sib, b_b, b_b_sib), w_e, cols)
+        fx, fy = swap(fx, XBIT, size), swap(fy, YBIT, size)
+        nx, ny = swap(nx, XBIT, size), swap(ny, YBIT, size)
+        kx = (kx.astype(F32) + fy.astype(F32)).astype(BF16)
+        ky = (ky.astype(F32) + fx.astype(F32)).astype(BF16)
+        kx, ky = swap(kx, XBIT, size), swap(ky, YBIT, size)
+
+        base = main_rows(me1, a_m, b_parts, places, w_m, bias_m, inv_m, pair_rows)
         main_out = assemble(main_moved)
         extra_out = turn_out(me1, blocks).transpose(0, 2, 1)
-        pair_out = combine(own, rx, ry, tx, ty, base, den_e, bias_e)
+        base = combine(base, inv_e, nx, ny, own, bias_e)
+        pair_out = combine(base, inv_e, ky, kx)
         return pair_out, extra_out, main_out
 
     in_specs = (value_spec, mask_spec, value_spec, mask_spec, row_spec) + (P(),) * 16

time: 448 us -> 423 us (0.944)
  waiting for transfers between devices: 177 us -> 149 us
    ppermute x24 -> x26, waiting for transfers between devices: 177 us -> 149 us  [swap(): return lax.ppermute(value, 'dap', [(d, d ^ bit) for d in range(size)])]
    ppermute x24 -> x26, starting transfers between devices: 20.4 us -> 21.3 us  [swap(): return lax.ppermute(value, 'dap', [(d, d ^ bit) for d in range(size)])]
    pallas_call x2 -> x3, Pallas kernels: 10.8 us -> 11.6 us  [turn(): pl.pallas_call(functools.partial(turn_kernel, ks), grid_spec=pltpu.Prefet...]
  transfers between devices with their start and end apart: 25 -> 27, of which waited for: 10 -> 10; matrix products, arithmetic and copies ran while one was open for 16% -> 16% of each run, Pallas kernels for 31% -> 34%
where the time goes in v3:
time: 423 us; the launch traced here: 420 us
  Pallas kernels  171 us (40%)
  waiting for transfers between devices  149 us (35%)
  local copies, waits for them, and re-layouts  30 us (7%)
  starting transfers between devices  25.2 us (6%)
  other arithmetic  23.5 us (6%)
  matrix products  20.8 us (5%)
    ppermute x26, waiting for transfers between devices, swap(): return lax.ppermute(value, 'dap', [(d, d ^ bit) for d in range(size)])  149 us
    pallas_call x1, Pallas kernels, extra_parts(): pl.pallas_call(functools.partial(extra_kernel, qu, iu), grid_spec=pltpu.P...  72.6 us
    pallas_call x1, Pallas kernels, turn_out(): pl.pallas_call(functools.partial(turn_out_kernel, ks), grid_spec=pltpu.Pr...  28.4 us
    pallas_call x2, Pallas kernels, project(): pl.pallas_call(functools.partial(project_kernel, group), grid_spec=pltpu....  21.6 us
    ppermute x26, starting transfers between devices, swap(): return lax.ppermute(value, 'dap', [(d, d ^ bit) for d in range(size)])  21.3 us
    pallas_call x1, Pallas kernels, main_rows(): pl.pallas_call(functools.partial(main_kernel, places, qu, iu), grid_spec=...  20.9 us
    pallas_call x3, Pallas kernels, turn(): pl.pallas_call(functools.partial(turn_kernel, ks), grid_spec=pltpu.Prefet...  11.6 us
    dot_general x1, matrix products, local_program(): jnp.einsum('sim,mq->qis', normed, mwr, preferred_element_type=F32)  10.3 us
  transfers between devices with their start and end apart: 27, of which 10 were waited for; matrix products, arithmetic and copies ran while one was open for 16% of the time, Pallas kernels for 34%

profile of v3, /device:TPU:0, one launch (start us, length us, event | category | flops | bytes accessed | tf_op | source)
XLA Modules:
  0.0 420.0 jit_solution(15702038818054169710)
XLA Ops:
  8.6 5.4 %turn.3 = (bf16[32,64,384]{2,1,0:T(8,128)(2,1)}, bf16[32,64,384]{2,1,0:T(8,128)(2,1)}, bf16[32,64,384]{2,1,0:T(8,128)(2,1)}, bf16[32,64,384]{2,1,0:T(8,128)(2,1)}) custom-call(s32[1]{0:T(128)} %bitcast.idx_ref.me_ref, bf16[32,64,3072]{2,1,0:T(8,128)(2,1)} %bitcast.40), custom_call_target="tpu_custom_call" | custom-call | flops 16777216 | bytes 4194304 | tf_op jit(solution)/shard_map/turn/pallas_call | solution.py:46
  25.7 5.6 %convert_reduce_fusion = f32[512,32]{1,0:T(8,128)S(1)} fusion(bf16[512,32,256]{2,1,0:T(8,128)(2,1)} %param.25), kind=kLoop, calls=%fused_computation.1 | loop fusion | flops 8372224 | bytes 8454144 | tf_op jit(solution)/shard_map/reduce_sum | solution.py:443
  31.5 6.9 %fusion.2 = f32[512,32]{1,0:T(8,128)S(1)} fusion(bf16[512,32,256]{2,1,0:T(8,128)(2,1)} %param.25, f32[512,32]{1,0:T(8,128)S(1)} %broadcast_multiply_fusion), kind=kLoop, calls=%fused_computation.4 | loop fusion | flops 16760832 | bytes 8519680 | tf_op jit(solution)/shard_map/reduce_sum | solution.py:445
  38.5 4.2 collective-permute-done.10.refs_2_.refs_4_
  44.6 31.4 %collective-permute-done.12.refs_4_.refs_3_ = bf16[32,64,384]{2,1,0:T(8,128)(2,1)} collective-permute-done((bf16[32,64,384]{2,1,0:T(8,128)(2,1)}, bf16[32,64,384]{2,1,0:T(8,128)(2,1)}, u32[]{:S(2)}, u32[]{:S(2)}) %collective-permute-start.12) | collective-permute-done | bytes 1572896 | tf_op jit(solution)/shard_map/ppermute | solution.py:23
  76.3 14.7 %project.2 = (bf16[3,1024,384]{2,1,0:T(8,128)(2,1)}, bf16[3,1024,384]{2,1,0:T(8,128)(2,1)}, bf16[6,32,32,384]{3,2,1,0:T(8,128)(2,1)}) custom-call(s32[6]{0:T(128)S(1)} %broadcast_xor_fusion.1.idx_ref, bf16[32,64,384]{2,1,0:T(8,128)(2,1)S(1)} %copy-done.5, bf16[32,64,384]{2,1,0:T(8,128)(2,1)S(1)} %collective-permute-done.9.refs_1_.refs_2_, ...), custom_call_target="tpu_custom_call" | custom-call | flops 6442450944 | bytes 13631488 | tf_op jit(solution)/shard_map/project/pallas_call | solution.py:161
  91.9 7.6 %fusion.8 = f32[512,32,32]{2,1,0:T(8,128)} fusion(bf16[512,32,256]{2,1,0:T(8,128)(2,1)S(1)} %bitcast.43, f32[256]{0:T(256)S(1)} %convert_element_type.82, f32[256]{0:T(256)S(1)} %convert_element_type.81, f32[512,32]{1,0:T(8,128)S(1)} %add_rsqrt_fusion, f32[512,32]{1,0:T(8,128)S(1)} %broadcast_multiply_fusion, bf16[256,32]{0,1:T(8,128)(2,1)S(1)} %copy-done), kind=kOutput, calls=%fused_computation.9 | convolution fusion | flops 293601280 | bytes 10635264 | tf_op jit(solution)/shard_map/sim,mp->ips/dot_general | solution.py:489
  99.6 6.3 %copy.53 = f32[512,32,32]{0,2,1:T(8,128)} copy(f32[512,32,32]{2,1,0:T(8,128)} %fusion.8) | data formatting | bytes 4194304 | tf_op jit(solution)/shard_map/sim,mp->ips/dot_general | solution.py:489
  108.2 10.3 %fusion.6 = f32[512,32,32]{2,1,0:T(8,128)} fusion(bf16[512,32,256]{2,1,0:T(8,128)(2,1)} %param.25, f32[256]{0:T(256)S(1)} %copy-done.34, f32[256]{0:T(256)S(1)} %copy-done.32, f32[512,32]{1,0:T(8,128)} %copy-done.17, f32[512,32]{1,0:T(8,128)} %copy-done.12, bf16[256,32]{0,1:T(8,128)(2,1)S(1)} %copy-done.26), kind=kOutput, calls=%fused_computation.8 | convolution fusion | flops 293601280 | bytes 10635264 | tf_op jit(solution)/shard_map/sim,mq->qis/dot_general | solution.py:491
  118.5 6.6 %copy.55 = f32[512,32,32]{0,1,2:T(8,128)} copy(f32[512,32,32]{2,1,0:T(8,128)} %fusion.6) | data formatting | bytes 4194304 | tf_op jit(solution)/shard_map/sim,mq->qis/dot_general | solution.py:491
  131.0 13.3 %collective-permute-done.15.refs_0_.refs_6_ = bf16[32,64,384]{2,1,0:T(8,128)(2,1)S(1)} collective-permute-done((bf16[32,64,384]{2,1,0:T(8,128)(2,1)}, bf16[32,64,384]{2,1,0:T(8,128)(2,1)S(1)}, u32[]{:S(2)}, u32[]{:S(2)}) %collective-permute-start.15) | collective-permute-done | bytes 1572896 | tf_op jit(solution)/shard_map/ppermute | solution.py:23
  145.4 30.8 %collective-permute-done.16.refs_1_.refs_7_ = bf16[32,64,384]{2,1,0:T(8,128)(2,1)} collective-permute-done((bf16[32,64,384]{2,1,0:T(8,128)(2,1)}, bf16[32,64,384]{2,1,0:T(8,128)(2,1)}, u32[]{:S(2)}, u32[]{:S(2)}) %collective-permute-start.16) | collective-permute-done | bytes 1572896 | tf_op jit(solution)/shard_map/ppermute | solution.py:23
  176.2 6.9 %project.3 = (bf16[1,1024,384]{2,1,0:T(8,128)(2,1)S(1)}, bf16[1,1024,384]{2,1,0:T(8,128)(2,1)}, bf16[2,32,32,384]{3,2,1,0:T(8,128)(2,1)S(1)}) custom-call(s32[2]{0:T(128)S(1)} %broadcast_xor_fusion.idx_ref, bf16[32,64,384]{2,1,0:T(8,128)(2,1)} %copy-done.9, bf16[32,64,384]{2,1,0:T(8,128)(2,1)} %collective-permute-done.16.refs_1_.refs_7_, ...), custom_call_target="tpu_custom_call" | custom-call | flops 6442450944 | bytes 13631488 | tf_op jit(solution)/shard_map/project/pallas_call | solution.py:161
  186.1 12.3 %collective-permute-done.refs_1_ = bf16[32,32,512]{2,1,0:T(8,128)(2,1)S(1)} collective-permute-done((bf16[32,32,512]{2,1,0:T(8,128)(2,1)}, bf16[32,32,512]{2,1,0:T(8,128)(2,1)S(1)}, u32[]{:S(2)}, u32[]{:S(2)}) %collective-permute-start) | collective-permute-done | bytes 1048608 | tf_op jit(solution)/shard_map/ppermute | solution.py:23
  202.2 8.8 %collective-permute-done.1.refs_2_ = bf16[32,32,512]{2,1,0:T(8,128)(2,1)S(1)} collective-permute-done((bf16[32,32,512]{2,1,0:T(8,128)(2,1)}, bf16[32,32,512]{2,1,0:T(8,128)(2,1)S(1)}, u32[]{:S(2)}, u32[]{:S(2)}) %collective-permute-start.1) | collective-permute-done | bytes 1048608 | tf_op jit(solution)/shard_map/ppermute | solution.py:23
  212.2 3.9 all-to-all-start
  217.9 72.6 %extra_outer.1 = (bf16[16,128,256]{2,1,0:T(8,128)(2,1)}, bf16[16,128,256]{2,1,0:T(8,128)(2,1)}, bf16[16,128,256]{2,1,0:T(8,128)(2,1)}, bf16[16,128,256]{2,1,0:T(...) custom-call(s32[1]{0:T(128)} %bitcast.idx_ref.me_ref, ...), custom_call_target="tpu_custom_call" | custom-call | flops 64424509440 | bytes 33554432 | tf_op jit(solution)/shard_map/extra_outer/pallas_call | solution.py:308
  294.0 26.9 %collective-permute-done.6.refs_7_ = bf16[16,32,512]{2,1,0:T(8,128)(2,1)} collective-permute-done((bf16[16,32,512]{2,1,0:T(8,128)(2,1)}, bf16[16,32,512]{2,1,0:T(8,128)(2,1)}, u32[]{:S(2)}, u32[]{:S(2)}) %collective-permute-start.6) | collective-permute-done | bytes 524320 | tf_op jit(solution)/shard_map/ppermute | solution.py:23
  323.8 12.9 %collective-permute-done.24 = bf16[16,128,256]{2,1,0:T(8,128)(2,1)} collective-permute-done((bf16[16,128,256]{2,1,0:T(8,128)(2,1)}, bf16[16,128,256]{2,1,0:T(8,128)(2,1)}, u32[]{:S(2)}, u32[]{:S(2)}) %collective-permute-start.24) | collective-permute-done | bytes 1048608 | tf_op jit(solution)/shard_map/ppermute | solution.py:23
  336.7 6.1 %collective-permute-done.22 = bf16[16,128,256]{2,1,0:T(8,128)(2,1)} collective-permute-done((bf16[16,128,256]{2,1,0:T(8,128)(2,1)}, bf16[16,128,256]{2,1,0:T(8,128)(2,1)}, u32[]{:S(2)}, u32[]{:S(2)}) %collective-permute-start.22) | collective-permute-done | bytes 1048608 | tf_op jit(solution)/shard_map/ppermute | solution.py:23
  352.7 20.9 %main_outer.1.base_ref = f32[32,256,128]{2,1,0:T(8,128)} custom-call(s32[1]{0:T(128)} %bitcast.idx_ref.me_ref, bf16[1024,512]{1,0:T(8,128)(2,1)} %bitcast.47, bf16[32,32,512]{2,1,0:T(8,128)(2,1)} %get-tuple-element.59.refs_0_, bf16[32,32,512]{2,1,0:T(8,128)(2,1)} %copy-done.13, bf16[32,32,512]{2,1,0:T(8,128)(2,1)} %copy-done.14, ...), custom_call_target="tpu_custom_call" | custom-call | flops 12884901888 | bytes 20971520 | tf_op jit(solution)/shard_map/main_outer/pallas_call | solution.py:356
  373.6 28.4 %turn_out.1 = bf16[384,64,256]{2,1,0:T(8,128)(2,1)} custom-call(s32[1]{0:T(128)} %bitcast.idx_ref.me_ref, bf16[32,64,384]{2,1,0:T(8,128)(2,1)} %get-tuple-element.31.refs_0_, bf16[32,64,384]{2,1,0:T(8,128)(2,1)} %collective-permute-done.11.refs_3_.refs_1_, bf16[32,64,384]{2,1,0:T(8,128)(2,1)} %copy-done.4, ...), custom_call_target="tpu_custom_call" | custom-call | flops 16777216 | bytes 26214400 | tf_op jit(solution)/shard_map/turn_out/pallas_call | solution.py:79
  406.9 4.2 combine.3
  411.0 9.0 %assemble.1 = bf16[64,256,256]{2,1,0:T(8,128)(2,1)} custom-call(bf16[8,64,32,256]{3,2,1,0:T(8,128)(2,1)} %bitcast.18.ref), custom_call_target="tpu_custom_call" | custom-call | flops 16777216 | bytes 16777216 | tf_op jit(solution)/shard_map/assemble/pallas_call | solution.py:430
  (165 shorter events, 62.8 us)
Async XLA Ops:
  3.8 38.9 %collective-permute-start.10 = (bf16[32,64,384]{2,1,0:T(8,128)(2,1)}, bf16[32,64,384]{2,1,0:T(8,128)(2,1)}, u32[]{:S(2)}, u32[]{:S(2)}) collective-permute-start(bf16[32,64,384]{2,1,0:T(8,128)(2,1)} %get-tuple-element.33), channel_id=1, source_target_pairs={{0,4},{1,5},{2,6},{3,7},{4,0},{5,1},{6,2},{7,3}} | collective-permute-start | bytes 4718600 | tf_op jit(solution)/shard_map/ppermute | solution.py:23
  7.1 37.5 %collective-permute-start.9 = (bf16[32,64,384]{2,1,0:T(8,128)(2,1)}, bf16[32,64,384]{2,1,0:T(8,128)(2,1)S(1)}, u32[]{:S(2)}, u32[]{:S(2)}) collective-permute-start(bf16[32,64,384]{2,1,0:T(8,128)(2,1)} %get-tuple-element.32), channel_id=1, source_target_pairs={{0,2},{1,3},{2,0},{3,1},{4,6},{5,7},{6,4},{7,5}} | collective-permute-start | bytes 4718600 | tf_op jit(solution)/shard_map/ppermute | solution.py:23
  14.0 30.6 %collective-permute-start.11 = (bf16[32,64,384]{2,1,0:T(8,128)(2,1)}, bf16[32,64,384]{2,1,0:T(8,128)(2,1)}, u32[]{:S(2)}, u32[]{:S(2)}) collective-permute-start(bf16[32,64,384]{2,1,0:T(8,128)(2,1)} %get-tuple-element.38), channel_id=1, source_target_pairs={{0,1},{1,0},{2,3},{3,2},{4,5},{5,4},{6,7},{7,6}} | collective-permute-start | bytes 4718600 | tf_op jit(solution)/shard_map/ppermute | solution.py:23
  17.1 58.9 %collective-permute-start.12 = (bf16[32,64,384]{2,1,0:T(8,128)(2,1)}, bf16[32,64,384]{2,1,0:T(8,128)(2,1)}, u32[]{:S(2)}, u32[]{:S(2)}) collective-permute-start(bf16[32,64,384]{2,1,0:T(8,128)(2,1)} %get-tuple-element.39), channel_id=1, source_target_pairs={{0,3},{1,2},{2,1},{3,0},{4,7},{5,6},{6,5},{7,4}} | collective-permute-start | bytes 4718600 | tf_op jit(solution)/shard_map/ppermute | solution.py:23
  17.8 58.2 %collective-permute-start.13 = (bf16[32,64,384]{2,1,0:T(8,128)(2,1)}, bf16[32,64,384]{2,1,0:T(8,128)(2,1)}, u32[]{:S(2)}, u32[]{:S(2)}) collective-permute-start(bf16[32,64,384]{2,1,0:T(8,128)(2,1)} %get-tuple-element.40), channel_id=1, source_target_pairs={{0,5},{1,4},{2,7},{3,6},{4,1},{5,0},{6,3},{7,2}} | collective-permute-start | bytes 4718600 | tf_op jit(solution)/shard_map/ppermute | solution.py:23
  91.1 126.8 %collective-permute-start.18 = (bf16[6,32,32,384]{3,2,1,0:T(8,128)(2,1)}, bf16[6,32,32,384]{3,2,1,0:T(8,128)(2,1)}, u32[]{:S(2)}, u32[]{:S(2)}) collective-permute-start(bf16[6,32,32,384]{3,2,1,0:T(8,128)(2,1)} %get-tuple-element.49.refs_4_), channel_id=1, source_target_pairs={{0,1},{1,0},{2,3},{3,2},{4,5},{5,4},{6,7},{7,6}} | collective-permute-start | bytes 14155784 | tf_op jit(solution)/shard_map/ppermute | solution.py:23
  105.9 38.4 %collective-permute-start.15 = (bf16[32,64,384]{2,1,0:T(8,128)(2,1)}, bf16[32,64,384]{2,1,0:T(8,128)(2,1)S(1)}, u32[]{:S(2)}, u32[]{:S(2)}) collective-permute-start(bf16[32,64,384]{2,1,0:T(8,128)(2,1)} %get-tuple-element.43), channel_id=1, source_target_pairs={{0,6},{1,7},{2,4},{3,5},{4,2},{5,3},{6,0},{7,1}} | collective-permute-start | bytes 4718600 | tf_op jit(solution)/shard_map/ppermute | solution.py:23
  107.3 68.9 %collective-permute-start.16 = (bf16[32,64,384]{2,1,0:T(8,128)(2,1)}, bf16[32,64,384]{2,1,0:T(8,128)(2,1)}, u32[]{:S(2)}, u32[]{:S(2)}) collective-permute-start(bf16[32,64,384]{2,1,0:T(8,128)(2,1)} %get-tuple-element.44), channel_id=1, source_target_pairs={{0,7},{1,6},{2,5},{3,4},{4,3},{5,2},{6,1},{7,0}} | collective-permute-start | bytes 4718600 | tf_op jit(solution)/shard_map/ppermute | solution.py:23
  129.0 69.4 %collective-permute-start = (bf16[32,32,512]{2,1,0:T(8,128)(2,1)}, bf16[32,32,512]{2,1,0:T(8,128)(2,1)S(1)}, u32[]{:S(2)}, u32[]{:S(2)}) collective-permute-start(bf16[32,32,512]{2,1,0:T(8,128)(2,1)} %get-tuple-element.59.refs_0_), channel_id=1, source_target_pairs={{0,2},{1,3},{2,0},{3,1},{4,6},{5,7},{6,4},{7,5}} | collective-permute-start | bytes 3145736 | tf_op jit(solution)/shard_map/ppermute | solution.py:23
  130.5 87.4 %collective-permute-start.14 = (bf16[3,1024,384]{2,1,0:T(8,128)(2,1)}, bf16[3,1024,384]{2,1,0:T(8,128)(2,1)}, u32[]{:S(2)}, u32[]{:S(2)}) collective-permute-start(bf16[3,1024,384]{2,1,0:T(8,128)(2,1)} %get-tuple-element.42), channel_id=1, source_target_pairs={{0,1},{1,0},{2,3},{3,2},{4,5},{5,4},{6,7},{7,6}} | collective-permute-start | bytes 7077896 | tf_op jit(solution)/shard_map/ppermute | solution.py:23
  184.1 33.8 %collective-permute-start.19 = (bf16[2,32,32,384]{3,2,1,0:T(8,128)(2,1)S(1)}, bf16[2,32,32,384]{3,2,1,0:T(8,128)(2,1)}, u32[]{:S(2)}, u32[]{:S(2)}) collective-permute-start(bf16[2,32,32,384]{3,2,1,0:T(8,128)(2,1)S(1)} %get-tuple-element.50.refs_6_), channel_id=1, source_target_pairs={{0,1},{1,0},{2,3},{3,2},{4,5},{5,4},{6,7},{7,6}} | collective-permute-start | bytes 4718600 | tf_op jit(solution)/shard_map/ppermute | solution.py:23
  185.7 25.3 %collective-permute-start.1 = (bf16[32,32,512]{2,1,0:T(8,128)(2,1)}, bf16[32,32,512]{2,1,0:T(8,128)(2,1)S(1)}, u32[]{:S(2)}, u32[]{:S(2)}) collective-permute-start(bf16[32,32,512]{2,1,0:T(8,128)(2,1)} %get-tuple-element.59.refs_0_), channel_id=1, source_target_pairs={{0,4},{1,5},{2,6},{3,7},{4,0},{5,1},{6,2},{7,3}} | collective-permute-start | bytes 3145736 | tf_op jit(solution)/shard_map/ppermute | solution.py:23
  211.0 82.5 %collective-permute-start.5 = (bf16[16,32,512]{2,1,0:T(8,128)(2,1)}, bf16[16,32,512]{2,1,0:T(8,128)(2,1)}, u32[]{:S(2)}, u32[]{:S(2)}) collective-permute-start(bf16[16,32,512]{2,1,0:T(8,128)(2,1)} %slice.8), channel_id=1, source_target_pairs={{0,4},{1,5},{2,6},{3,7},{4,0},{5,1},{6,2},{7,3}} | collective-permute-start | bytes 1572872 | tf_op jit(solution)/shard_map/ppermute | solution.py:23
  212.2 198.8 %all-to-all-start = ((bf16[512,32,256]{2,1,0:T(8,128)(2,1)}), bf16[512,32,256]{2,1,0:T(8,128)(2,1)}, u32[]{:S(2)}, u32[]{:S(2)}) async-start(bf16[512,32,256]{2,1,0:T(8,128)(2,1)} %param.25), calls=%async_computation | async-start | bytes 16777216 | tf_op jit(solution)/shard_map/all_to_all | solution.py:506
  216.1 104.8 %collective-permute-start.6 = (bf16[16,32,512]{2,1,0:T(8,128)(2,1)}, bf16[16,32,512]{2,1,0:T(8,128)(2,1)}, u32[]{:S(2)}, u32[]{:S(2)}) collective-permute-start(bf16[16,32,512]{2,1,0:T(8,128)(2,1)} %slice.9), channel_id=1, source_target_pairs={{0,2},{1,3},{2,0},{3,1},{4,6},{5,7},{6,4},{7,5}} | collective-permute-start | bytes 1572872 | tf_op jit(solution)/shard_map/ppermute | solution.py:23
  290.5 46.2 %collective-permute-start.24 = (bf16[16,128,256]{2,1,0:T(8,128)(2,1)}, bf16[16,128,256]{2,1,0:T(8,128)(2,1)}, u32[]{:S(2)}, u32[]{:S(2)}) collective-permute-start(bf16[16,128,256]{2,1,0:T(8,128)(2,1)} %get-tuple-element.57), channel_id=1, source_target_pairs={{0,4},{1,5},{2,6},{3,7},{4,0},{5,1},{6,2},{7,3}} | collective-permute-start | bytes 3145736 | tf_op jit(solution)/shard_map/ppermute | solution.py:23
  292.0 50.8 %collective-permute-start.22 = (bf16[16,128,256]{2,1,0:T(8,128)(2,1)}, bf16[16,128,256]{2,1,0:T(8,128)(2,1)}, u32[]{:S(2)}, u32[]{:S(2)}) collective-permute-start(bf16[16,128,256]{2,1,0:T(8,128)(2,1)} %get-tuple-element.55), channel_id=1, source_target_pairs={{0,2},{1,3},{2,0},{3,1},{4,6},{5,7},{6,4},{7,5}} | collective-permute-start | bytes 3145736 | tf_op jit(solution)/shard_map/ppermute | solution.py:23
  292.5 55.3 %collective-permute-start.2 = (bf16[32,32,512]{2,1,0:T(8,128)(2,1)}, bf16[32,32,512]{2,1,0:T(8,128)(2,1)}, u32[]{:S(2)}, u32[]{:S(2)}) collective-permute-start(bf16[32,32,512]{2,1,0:T(8,128)(2,1)} %get-tuple-element.59.refs_0_), channel_id=1, source_target_pairs={{0,1},{1,0},{2,3},{3,2},{4,5},{5,4},{6,7},{7,6}} | collective-permute-start | bytes 3145736 | tf_op jit(solution)/shard_map/ppermute | solution.py:23
  293.5 57.9 %collective-permute-start.3 = (bf16[32,32,512]{2,1,0:T(8,128)(2,1)}, bf16[32,32,512]{2,1,0:T(8,128)(2,1)}, u32[]{:S(2)}, u32[]{:S(2)}) collective-permute-start(bf16[32,32,512]{2,1,0:T(8,128)(2,1)} %copy-done.13), channel_id=1, source_target_pairs={{0,1},{1,0},{2,3},{3,2},{4,5},{5,4},{6,7},{7,6}} | collective-permute-start | bytes 3145736 | tf_op jit(solution)/shard_map/ppermute | solution.py:23
  320.9 31.0 %collective-permute-start.4 = (bf16[32,32,512]{2,1,0:T(8,128)(2,1)}, bf16[32,32,512]{2,1,0:T(8,128)(2,1)}, u32[]{:S(2)}, u32[]{:S(2)}) collective-permute-start(bf16[32,32,512]{2,1,0:T(8,128)(2,1)} %copy-done.14), channel_id=1, source_target_pairs={{0,1},{1,0},{2,3},{3,2},{4,5},{5,4},{6,7},{7,6}} | collective-permute-start | bytes 3145736 | tf_op jit(solution)/shard_map/ppermute | solution.py:23
  347.9 54.2 %collective-permute-start.20 = (bf16[16,128,256]{2,1,0:T(8,128)(2,1)}, bf16[16,128,256]{2,1,0:T(8,128)(2,1)S(1)}, u32[]{:S(2)}, u32[]{:S(2)}) collective-permute-start(bf16[16,128,256]{2,1,0:T(8,128)(2,1)} %get-tuple-element.51), channel_id=1, source_target_pairs={{0,2},{1,3},{2,0},{3,1},{4,6},{5,7},{6,4},{7,5}} | collective-permute-start | bytes 3145736 | tf_op jit(solution)/shard_map/ppermute | solution.py:23
  348.2 53.8 %collective-permute-start.21 = (bf16[16,128,256]{2,1,0:T(8,128)(2,1)}, bf16[16,128,256]{2,1,0:T(8,128)(2,1)}, u32[]{:S(2)}, u32[]{:S(2)}) collective-permute-start(bf16[16,128,256]{2,1,0:T(8,128)(2,1)} %get-tuple-element.52), channel_id=1, source_target_pairs={{0,4},{1,5},{2,6},{3,7},{4,0},{5,1},{6,2},{7,3}} | collective-permute-start | bytes 3145736 | tf_op jit(solution)/shard_map/ppermute | solution.py:23
  349.9 56.9 %collective-permute-start.25 = (bf16[16,128,256]{2,1,0:T(8,128)(2,1)}, bf16[16,128,256]{2,1,0:T(8,128)(2,1)}, u32[]{:S(2)}, u32[]{:S(2)}) collective-permute-start(bf16[16,128,256]{2,1,0:T(8,128)(2,1)} %add_convert_fusion), channel_id=1, source_target_pairs={{0,2},{1,3},{2,0},{3,1},{4,6},{5,7},{6,4},{7,5}} | collective-permute-start | bytes 3145736 | tf_op jit(solution)/shard_map/ppermute | solution.py:23
  351.4 55.4 %collective-permute-start.23 = (bf16[16,128,256]{2,1,0:T(8,128)(2,1)}, bf16[16,128,256]{2,1,0:T(8,128)(2,1)}, u32[]{:S(2)}, u32[]{:S(2)}) collective-permute-start(bf16[16,128,256]{2,1,0:T(8,128)(2,1)} %add_convert_fusion.1), channel_id=1, source_target_pairs={{0,4},{1,5},{2,6},{3,7},{4,0},{5,1},{6,2},{7,3}} | collective-permute-start | bytes 3145736 | tf_op jit(solution)/shard_map/ppermute | solution.py:23
  (41 other events, 1127.2 us)

commit v4 on v3

--- a/solution.py
+++ b/solution.py
@@ -63,32 +63,35 @@
 
 
 def turn_out_kernel(ks, me_ref, *refs):
-    x_refs, (out_ref, in_v, out_v) = refs[:len(ks)], refs[len(ks):]
+    x_refs, (out_ref, in_v, out_v) = refs[:len(ks)], refs[-3:]
     rows, lead = x_refs[0].shape[:2]
     for k, ref in zip(ks, x_refs):
-        in_v[pl.ds(pl.multiple_of((me_ref[0] ^ k) * rows, rows), rows)] = ref[...].astype(F32)
+        at = lax.rem(me_ref[0] ^ k, len(ks)) * rows
+        in_v[pl.ds(pl.multiple_of(at, rows), rows)] = ref[...].astype(F32)
     for c in range(lead):
         out_v[:, c, :] = in_v[:, c, :].T
     out_ref[...] = out_v[...].astype(BF16)
 
 
-def turn_out(me, blocks, lead=8):
-    ks = tuple(sorted(blocks))
+def turn_out(me, blocks, ks, size, into=None, lead=16):
     rows, chans, seqs = blocks[ks[0]].shape
     res = rows * len(ks)
+    halves = size // len(ks)
+    carried = [] if into is None else [into]
     return pl.pallas_call(
         functools.partial(turn_out_kernel, ks),
         grid_spec=pltpu.PrefetchScalarGridSpec(
             num_scalar_prefetch=1,
             grid=(seqs // LANES, chans // lead),
-            in_specs=[pl.BlockSpec((rows, lead, LANES), lambda k, c, i: (0, c, k)) for _ in ks],
-            out_specs=pl.BlockSpec((LANES, lead, res), lambda k, c, i: (k, c, 0)),
+            in_specs=[pl.BlockSpec((rows, lead, LANES), lambda k, c, i: (0, c, k)) for _ in ks] + [ANY] * len(carried),
+            out_specs=pl.BlockSpec((LANES, lead, res), lambda k, c, i: (k, c, (i[0] ^ ks[0]) // len(ks))),
             scratch_shapes=[pltpu.VMEM((res, lead, LANES), F32), pltpu.VMEM((LANES, lead, res), F32)],
         ),
-        out_shape=jax.ShapeDtypeStruct((seqs, chans, res), BF16),
-        cost_estimate=pl.CostEstimate(flops=1 << 24, bytes_accessed=25 << 20, transcendentals=0),
+        out_shape=jax.ShapeDtypeStruct((seqs, chans, halves * res), BF16),
+        input_output_aliases={len(ks) + 1: 0} if carried else {},
+        cost_estimate=pl.CostEstimate(flops=1 << 24, bytes_accessed=13 << 20, transcendentals=0),
         name='turn_out',
-    )(me, *[blocks[k] for k in ks])
+    )(me, *[blocks[k] for k in ks], *carried)
 
 
 def project_kernel(group, idx_ref, *refs):
@@ -186,7 +189,7 @@
     )(idx, *blocks, mask_t, gamma, beta, w_both, bias)
 
 
-def outer_rows(a, b_v, o_v, qu, ready=None):
+def outer_rows(a, b_v, o_v, qu, ready=None, more=None):
     rows, hid, _, cols = o_v.shape
 
     def q_body(g, carry):
@@ -195,6 +198,8 @@
         for u in range(qu):
             q = g * qu + u
             o = lax.dot_general(a[...], b_v[q], NT, preferred_element_type=F32)
+            if more is not None:
+                o = o + jnp.dot(more[0][...], more[1][q], preferred_element_type=F32)
             o_v[:, q] = o.astype(BF16).reshape(rows, hid, cols)
         return carry
 
@@ -329,19 +334,85 @@
     )(me, *a_parts, *b_parts, w_t)
 
 
-def main_kernel(places, qu, iu, idx_ref, a_ref, *refs):
-    b_refs = refs[:len(places)]
-    w_ref, bias_ref, inv_ref, z_ref, out_ref, b_v, o_v, sb = refs[len(places):]
+def main_late_kernel(x_ref, mask_ref, gamma_ref, beta_ref, w_ref, bias_ref, out_ref, z_v):
+    srcs, seqs, rows, chans = x_ref.shape
+    hid = w_ref.shape[0]
+
+    def body(g, carry):
+        for u in range(4):
+            n = g * 4 + u
+            x = x_ref[:, n].reshape(srcs * rows, chans).astype(F32)
+            centered = x - jnp.mean(x, axis=1, keepdims=True)
+            var = jnp.mean(centered * centered, axis=1, keepdims=True)
+            y = (centered * lax.rsqrt(var + LN_EPS) * gamma_ref[...] + beta_ref[...]).astype(BF16)
+            z = lax.dot_general(w_ref[...], y, NT, preferred_element_type=F32) + bias_ref[...]
+            z_v[n] = z * mask_ref[pl.ds(n, 1), :]
+        return carry
+
+    lax.fori_loop(0, seqs // 4, body, 0)
+    for q in range(hid):
+        out_ref[q] = z_v[:, q, :].astype(BF16)
+
+
+def main_late(moved, mask, gamma, beta, w_right, b_right, block=16):
+    srcs, seqs, rows, chans = moved.shape
+    hid = w_right.shape[1]
+    res = srcs * rows
+    whole = lambda v: pl.BlockSpec(v.shape, lambda s: (0,) * v.ndim)
+    row = lambda v: v.astype(F32)[None]
+    bias = jnp.broadcast_to(b_right.astype(F32)[:, None], (hid, res))
+    args = (row(gamma), row(beta), w_right.T, bias)
+    return pl.pallas_call(
+        main_late_kernel,
+        grid=(seqs // block,),
+        in_specs=[
+            pl.BlockSpec((srcs, block, rows, chans), lambda s: (0, s, 0, 0)),
+            pl.BlockSpec((block, res), lambda s: (s, 0)),
+        ] + [whole(v) for v in args],
+        out_specs=pl.BlockSpec((hid, block, res), lambda s: (0, s, 0)),
+        out_shape=jax.ShapeDtypeStruct((hid, seqs, res), BF16),
+        scratch_shapes=[pltpu.VMEM((block, hid, res), F32)],
+        compiler_params=pltpu.CompilerParams(vmem_limit_bytes=32 << 20),
+        cost_estimate=pl.CostEstimate(flops=4 << 30, bytes_accessed=10 << 20, transcendentals=0),
+        name='main_late',
+    )(moved, mask, *args)
+
+
+HID = 32
+OWN_X = ((0, HID, 0, 0, 3), (HID, HID, 0, 0, 2))
+OWN_Y = ((HID, HID, 0, 0, 1),)
+FROM_X = ((0, HID, XBIT, 0, 2), (HID, HID, XBIT, 0, 3), (2 * HID, HID, XBIT, 0, 1))
+FROM_Y = ((0, HID, YBIT, 0, 2), (HID, HID, YBIT, 0, 3), (2 * HID, HID, YBIT, 0, 1))
+FAR_Y = ((0, HID, XBIT | YBIT, 0, 1), (HID, HID // 2, XBIT | YBIT, 0, 3))
+FAR_X = ((0, HID // 2, XBIT | YBIT, HID // 2, 3), (HID // 2, HID, XBIT | YBIT, 0, 2))
+
+
+def main_kernel(tables, qu, iu, idx_ref, a_ref, *refs):
+    b_refs, late_refs = refs[:len(tables)], refs[len(tables):len(tables) + 2]
+    w_ref, bias_ref, inv_ref, z_ref, out_ref, a_v, c_v, b_v, l_v, o_v, sa, sb = refs[len(tables) + 2:]
+    me = idx_ref[0]
+    chip, core = me // 2, lax.rem(me, 2)
     copies = []
-    for t, (ref, (k, first)) in enumerate(zip(b_refs, places)):
-        count, width = ref.shape[:2]
-        at = pl.multiple_of((idx_ref[0] ^ k) * width, width)
-        copies.append(pltpu.make_async_copy(ref, b_v.at[pl.ds(first, count), pl.ds(at, width), :], sb.at[t]))
+    lanes = lambda n: pl.ds(pl.multiple_of(n * LANES, LANES), LANES)
+    for r in range(4):
+        target = c_v if r == 0 else a_v.at[:, lanes(r - 1)]
+        copies.append(pltpu.make_async_copy(a_ref.at[:, lanes(chip ^ r)], target, sa.at[r]))
+    for n, ref in enumerate(late_refs):
+        seqs = ref.shape[1]
+        at = pl.ds(pl.multiple_of((core ^ n) * seqs, seqs), seqs)
+        copies.append(pltpu.make_async_copy(ref, l_v.at[:, at, :], sa.at[4 + n]))
+    count = 0
+    for ref, (core_bit, table) in zip(b_refs, tables):
+        for first, rows, k, q, r in table:
+            width = ref.shape[1]
+            js = pl.ds(pl.multiple_of((me ^ k ^ core_bit) * width, width), width)
+            copies.append(pltpu.make_async_copy(ref.at[pl.ds(first, rows)], b_v.at[pl.ds(q, rows), js, lanes(r - 1)], sb.at[count]))
+            count += 1
     for c in copies:
         c.start()
     for c in copies:
         c.wait()
-    outer_rows(a_ref, b_v, o_v, qu)
+    outer_rows(a_v, b_v, o_v, qu, more=(c_v, l_v))
 
     def store(i, r):
         out_ref[i] = z_ref[i] + ((r + bias_ref[...]) * inv_ref[pl.ds(i, 1), :]).T
@@ -349,28 +420,33 @@
     weigh_rows(w_ref, o_v, iu, store)
 
 
-def main_rows(me, a, b_parts, places, w_t, bias, inv, z, qu=8, iu=8):
-    hid, _, depth = b_parts[0].shape
+def main_rows(me, a, b_parts, tables, late, w_t, bias, inv, z, qu=8, iu=8):
     rows, cols, _ = z.shape
+    hid = a.shape[0] // rows
+    count = sum(len(table) for _, table in tables)
     whole = lambda v: pl.BlockSpec(v.shape, lambda s, i: (0,) * v.ndim)
     return pl.pallas_call(
-        functools.partial(main_kernel, places, qu, iu),
+        functools.partial(main_kernel, tables, qu, iu),
         grid_spec=pltpu.PrefetchScalarGridSpec(
             num_scalar_prefetch=1,
             grid=(1,),
-            in_specs=[whole(a)] + [ANY] * len(b_parts) + [whole(w_t), whole(bias), whole(inv), whole(z)],
+            in_specs=[ANY] * (len(b_parts) + 3) + [whole(w_t), whole(bias), whole(inv), whole(z)],
             out_specs=whole(z),
             scratch_shapes=[
-                pltpu.VMEM((hid, cols, depth), BF16),
+                pltpu.VMEM((rows * hid, 3 * LANES), BF16),
+                pltpu.VMEM((rows * hid, LANES), BF16),
+                pltpu.VMEM((hid, cols, 3 * LANES), BF16),
+                pltpu.VMEM((hid, LANES, cols), BF16),
                 pltpu.VMEM((rows, hid, hid, cols), BF16),
-                pltpu.SemaphoreType.DMA((len(b_parts),)),
+                pltpu.SemaphoreType.DMA((6,)),
+                pltpu.SemaphoreType.DMA((count,)),
             ],
         ),
         out_shape=jax.ShapeDtypeStruct(z.shape, F32),
         compiler_params=pltpu.CompilerParams(vmem_limit_bytes=60 << 20),
         cost_estimate=pl.CostEstimate(flops=12 << 30, bytes_accessed=20 << 20, transcendentals=0),
         name='main_outer',
-    )(me, a, *b_parts, w_t, bias, inv, z)
+    )(me, a, *b_parts, *late, w_t, bias, inv, z)
 
 
 def combine_kernel(base_ref, inv_ref, lower_ref, upper_ref, *refs):
@@ -459,6 +535,7 @@
 
     def local_program(extra_block, extra_mask, main_block, main_mask, pair_rows, eg, eb, ewl, ebl, ewr, ebr, ewo, ebo, mg, mb, mwl, mbl, mwr, mbr, mwo, mbo):
         me = lax.axis_index('dap')
+        chip = me // 2
         rows = extra_block.shape[1]
         hid = ewl.shape[1]
 
@@ -475,43 +552,49 @@
         for k in NEAR[2:]:
             blocks[k] = swap(turned[k], k, size)
         blocks[1] = swap(turned[1], CORE, size)
-        near, far = lax.optimization_barrier(([blocks[k] for k in NEAR[:2]], [turned[6], turned[7]]))
-        blocks.update(zip(NEAR[:2], near))
+        near, far = lax.optimization_barrier(([blocks[k] for k in NEAR], [turned[6], turned[7]]))
+        blocks.update(zip(NEAR, near))
         for k, value in zip((6, 7), far):
             blocks[k] = swap(value, k, size)
 
         mask_rows_m = lax.dynamic_slice_in_dim(main_mask, me * rows, rows, axis=1)
-        mask_rows_e = lax.dynamic_slice_in_dim(extra_mask, me * rows, rows, axis=1)
-        inv_m = inverse_norms(main_mask, mask_rows_m)
-        inv_e = inverse_norms(extra_mask, mask_rows_e)
         normed = layer_norm(main_block, mg, mb)
         mask_m = mask_rows_m.astype(F32).T
-        a_m = jnp.einsum('sim,mp->ips', normed, mwl, preferred_element_type=F32) + mbl.astype(F32)[None, :, None]
-        a_m = (a_m * mask_m[:, None, :]).astype(BF16).reshape(rows * hid, -1)
-        b_m = jnp.einsum('sim,mq->qis', normed, mwr, preferred_element_type=F32) + mbr.astype(F32)[:, None, None]
-        b_m = (b_m * mask_m[None]).astype(BF16)
 
         wide = lambda v, n: jnp.broadcast_to(v.astype(F32)[:, None], (v.shape[0], n))
         mask_seq = lax.dynamic_slice_in_dim(extra_mask, me * seqs, seqs, axis=0).astype(F32).T
         w_both, bias = project_weights(ewl, ebl, ewr, ebr, seqs)
         gamma, beta = wide(eg, seqs), wide(eb, seqs)
         idx_a, idx_b = [(me ^ jnp.array(ks, jnp.int32)).astype(jnp.int32) for ks in (SET_A, SET_B)]
+        a_m = jnp.einsum('sim,mp->ips', normed, mwl, preferred_element_type=F32) + mbl.astype(F32)[None, :, None]
+        a_m = (a_m * mask_m[:, None, :]).astype(BF16).reshape(rows * hid, -1)
+        b_m = jnp.einsum('sim,mq->qis', normed, mwr, preferred_element_type=F32) + mbr.astype(F32)[:, None, None]
+        b_m = (b_m * mask_m[None]).astype(BF16)
+        pick = lambda r: lax.dynamic_slice_in_dim(b_m, (chip ^ r) * LANES, LANES, axis=2)
+        b_0, b_1, b_2, b_3 = [pick(r) for r in range(4)]
+        b_to_x, b_to_y = jnp.concatenate([b_3, b_2, b_0]), jnp.concatenate([b_0, b_1, b_3])
+        mask_rows_e = lax.dynamic_slice_in_dim(extra_mask, me * rows, rows, axis=1)
+        inv_m = inverse_norms(main_mask, mask_rows_m)
+        inv_e = inverse_norms(extra_mask, mask_rows_e)
         w_e, w_m = turn_weights(ewo, hid), turn_weights(mwo, hid)
         bias_e, bias_m = wide(ebo, cols), wide(mbo, cols)
+        count = main_mask.shape[0] // size
+        mask_late = lax.dynamic_slice_in_dim(main_mask, me * count, count, axis=0).astype(F32)
 
         a_a, a_a_give, b_a = project(idx_a, [blocks[k] for k in SET_A], mask_seq, gamma, beta, w_both, bias, hid)
         a_a_sib, b_a_sib = swap(a_a_give, CORE, size), swap(b_a, CORE, size)
 
         blocks[6], blocks[7], main_moved = lax.optimization_barrier((blocks[6], blocks[7], main_block))
         main_moved = lax.all_to_all(main_moved, 'dap', 0, 0, tiled=True).reshape(size, -1, rows, main_block.shape[2])
-        b_x, b_y = swap(b_m, XBIT, size), swap(b_m, YBIT, size)
-        mid = hid // 2
-        b_d = [swap(b_x[:mid], YBIT, size), swap(b_y[mid:], XBIT, size)]
-        b_parts = [b_m, b_x, b_y]
+        b_x, b_y = swap(b_to_x, XBIT, size), swap(b_to_y, YBIT, size)
+        b_dx, b_dy = swap(b_y[hid // 2:2 * hid], XBIT, size), swap(b_x[hid:2 * hid + hid // 2], YBIT, size)
+        b_parts = [b_to_x, b_to_y, b_x, b_y]
         b_parts = b_parts + [swap(part, CORE, size) for part in b_parts]
-        b_parts = b_parts + b_d + [swap(part, CORE, size) for part in b_d]
-        places = ((0, 0), (XBIT, 0), (YBIT, 0), (CORE, 0), (CORE | XBIT, 0), (CORE | YBIT, 0))
-        places = places + ((XBIT | YBIT, 0), (XBIT | YBIT, mid), (CORE | XBIT | YBIT, 0), (CORE | XBIT | YBIT, mid))
+        b_parts = b_parts + [b_dx, b_dy, swap(b_dx, CORE, size), swap(b_dy, CORE, size)]
+        near_tables, far_tables = (OWN_X, OWN_Y, FROM_X, FROM_Y), (FAR_X, FAR_Y)
+        tables = tuple((bit, t) for ts in (near_tables, far_tables) for bit in (0, CORE) for t in ts)
+        late = main_late(main_moved, mask_late, mg, mb, mwr, mbr)
+        late_sib = swap(late, CORE, size)
 
         a_b, a_b_give, b_b = project(idx_b, [blocks[k] for k in SET_B], mask_seq, gamma, beta, w_both, bias, hid)
         a_b_sib, b_b_sib = swap(a_b_give, CORE, size), swap(b_b, CORE, size)
@@ -522,9 +605,10 @@
         ky = (ky.astype(F32) + fx.astype(F32)).astype(BF16)
         kx, ky = swap(kx, XBIT, size), swap(ky, YBIT, size)
 
-        base = main_rows(me1, a_m, b_parts, places, w_m, bias_m, inv_m, pair_rows)
+        base = main_rows(me1, a_m, b_parts, tables, (late, late_sib), w_m, bias_m, inv_m, pair_rows)
         main_out = assemble(main_moved)
-        extra_out = turn_out(me1, blocks).transpose(0, 2, 1)
+        extra_out = turn_out(me1, blocks, (0, 1, 2, 3), size)
+        extra_out = turn_out(me1, blocks, (4, 5, 6, 7), size, extra_out).transpose(0, 2, 1)
         base = combine(base, inv_e, nx, ny, own, bias_e)
         pair_out = combine(base, inv_e, ky, kx)
         return pair_out, extra_out, main_out

time: 423 us -> 427 us (level)
  Pallas kernels: 171 us -> 196 us
  waiting for transfers between devices: 149 us -> 129 us
    ppermute x26 -> x28, waiting for transfers between devices: 149 us -> 129 us  [swap(): return lax.ppermute(value, 'dap', [(d, d ^ bit) for d in range(size)])]
    pallas_call x1 -> x2, Pallas kernels: 20.9 us -> 38.5 us  [the longest x1 25.4 us: main_rows(): pl.pallas_call(functools.partial(main_kernel, tables, qu, iu), grid_spec=...]
    pallas_call x1 -> x2, Pallas kernels: 28.4 us -> 36.3 us  [turn_out(): pl.pallas_call(functools.partial(turn_out_kernel, ks), grid_spec=pltpu.Pr...]
    ppermute x26 -> x28, starting transfers between devices: 21.3 us -> 22 us  [swap(): return lax.ppermute(value, 'dap', [(d, d ^ bit) for d in range(size)])]
  transfers between devices with their start and end apart: 27 -> 29, of which waited for: 10 -> 10; matrix products, arithmetic and copies ran while one was open for 16% -> 16% of each run, Pallas kernels for 34% -> 41%
where the time goes in v4:
time: 427 us; the launch traced here: 425 us
  Pallas kernels  196 us (46%)
  waiting for transfers between devices  129 us (30%)
  local copies, waits for them, and re-layouts  27 us (6%)
  starting transfers between devices  25.9 us (6%)
  other arithmetic  23.6 us (6%)
  matrix products  22.6 us (5%)
    ppermute x28, waiting for transfers between devices, swap(): return lax.ppermute(value, 'dap', [(d, d ^ bit) for d in range(size)])  129 us
    pallas_call x1, Pallas kernels, extra_parts(): pl.pallas_call(functools.partial(extra_kernel, qu, iu), grid_spec=pltpu.P...  72.4 us
    pallas_call x2, Pallas kernels, turn_out(): pl.pallas_call(functools.partial(turn_out_kernel, ks), grid_spec=pltpu.Pr...  36.3 us
    pallas_call x1, Pallas kernels, main_rows(): pl.pallas_call(functools.partial(main_kernel, tables, qu, iu), grid_spec=...  25.4 us
    ppermute x28, starting transfers between devices, swap(): return lax.ppermute(value, 'dap', [(d, d ^ bit) for d in range(size)])  22 us
    pallas_call x2, Pallas kernels, project(): pl.pallas_call(functools.partial(project_kernel, group), grid_spec=pltpu....  21 us
    pallas_call x1, Pallas kernels, main_late(): pl.pallas_call(main_late_kernel, grid=(seqs // block,), in_specs=[pl.Bloc...  13.1 us
    pallas_call x3, Pallas kernels, turn(): pl.pallas_call(functools.partial(turn_kernel, ks), grid_spec=pltpu.Prefet...  11.6 us
  transfers between devices with their start and end apart: 29, of which 10 were waited for; matrix products, arithmetic and copies ran while one was open for 16% of the time, Pallas kernels for 41%

profile of v4, /device:TPU:0, one launch (start us, length us, event | category | flops | bytes accessed | tf_op | source)
XLA Modules:
  0.0 425.3 jit_solution(10320735274746336253)
XLA Ops:
  12.1 5.4 %turn.5 = (bf16[32,64,384]{2,1,0:T(8,128)(2,1)}, bf16[32,64,384]{2,1,0:T(8,128)(2,1)}, bf16[32,64,384]{2,1,0:T(8,128)(2,1)}, bf16[32,64,384]{2,1,0:T(8,128)(2,1)}) custom-call(s32[1]{0:T(128)} %bitcast.me_ref.idx_ref, bf16[32,64,3072]{2,1,0:T(8,128)(2,1)} %bitcast.47), custom_call_target="tpu_custom_call" | custom-call | flops 16777216 | bytes 4194304 | tf_op jit(solution)/shard_map/turn/pallas_call | solution.py:46
  20.5 5.7 %convert_reduce_fusion = f32[512,32]{1,0:T(8,128)S(1)} fusion(bf16[512,32,256]{2,1,0:T(8,128)(2,1)} %param.25), kind=kLoop, calls=%fused_computation.1 | loop fusion | flops 8372224 | bytes 8454144 | tf_op jit(solution)/shard_map/reduce_sum | solution.py:519
  26.2 16.3 %collective-permute-done.10.refs_1_.refs_2_ = bf16[32,64,384]{2,1,0:T(8,128)(2,1)S(1)} collective-permute-done((bf16[32,64,384]{2,1,0:T(8,128)(2,1)}, bf16[32,64,384]{2,1,0:T(8,128)(2,1)S(1)}, u32[]{:S(2)}, u32[]{:S(2)}) %collective-permute-start.10) | collective-permute-done | bytes 1572896 | tf_op jit(solution)/shard_map/ppermute | solution.py:23
  44.7 30.1 %collective-permute-done.12.refs_4_.refs_3_ = bf16[32,64,384]{2,1,0:T(8,128)(2,1)} collective-permute-done((bf16[32,64,384]{2,1,0:T(8,128)(2,1)}, bf16[32,64,384]{2,1,0:T(8,128)(2,1)}, u32[]{:S(2)}, u32[]{:S(2)}) %collective-permute-start.12) | collective-permute-done | bytes 1572896 | tf_op jit(solution)/shard_map/ppermute | solution.py:23
  76.4 14.9 %project.2 = (bf16[3,1024,384]{2,1,0:T(8,128)(2,1)}, bf16[3,1024,384]{2,1,0:T(8,128)(2,1)}, bf16[6,32,32,384]{3,2,1,0:T(8,128)(2,1)}) custom-call(s32[6]{0:T(128)S(1)} %broadcast_xor_fusion.1.idx_ref, bf16[32,64,384]{2,1,0:T(8,128)(2,1)S(1)} %copy-done.5, bf16[32,64,384]{2,1,0:T(8,128)(2,1)S(1)} %collective-permute-done.10.refs_1_.refs_2_, ...), custom_call_target="tpu_custom_call" | custom-call | flops 6442450944 | bytes 13631488 | tf_op jit(solution)/shard_map/project/pallas_call | solution.py:164
  94.4 6.8 %fusion.2 = f32[512,32]{1,0:T(8,128)S(1)} fusion(bf16[512,32,256]{2,1,0:T(8,128)(2,1)} %param.25, f32[512,32]{1,0:T(8,128)S(1)} %broadcast_multiply_fusion), kind=kLoop, calls=%fused_computation.4 | loop fusion | flops 16760832 | bytes 8519680 | tf_op jit(solution)/shard_map/reduce_sum | solution.py:521
  101.4 10.4 %fusion.8 = f32[512,32,32]{2,1,0:T(8,128)} fusion(bf16[512,32,256]{2,1,0:T(8,128)(2,1)} %param.25, f32[256]{0:T(256)S(1)} %convert_element_type.88, f32[256]{0:T(256)S(1)} %convert_element_type.87, f32[512,32]{1,0:T(8,128)S(1)} %add_rsqrt_fusion, f32[512,32]{1,0:T(8,128)S(1)} %broadcast_multiply_fusion, bf16[256,32]{0,1:T(8,128)(2,1)S(1)} %copy-done), kind=kOutput, calls=%fused_computation.9 | convolution fusion | flops 293601280 | bytes 10635264 | tf_op jit(solution)/shard_map/sim,mp->ips/dot_general | solution.py:569
  112.6 17.8 %collective-permute-done.14.refs_0_.refs_2_ = bf16[32,64,384]{2,1,0:T(8,128)(2,1)S(1)} collective-permute-done((bf16[32,64,384]{2,1,0:T(8,128)(2,1)S(1)}, bf16[32,64,384]{2,1,0:T(8,128)(2,1)S(1)}, u32[]{:S(2)}, u32[]{:S(2)}) %collective-permute-start.14) | collective-permute-done | bytes 1572896 | tf_op jit(solution)/shard_map/ppermute | solution.py:23
  130.3 31.8 %collective-permute-done.15.refs_1_.refs_3_ = bf16[32,64,384]{2,1,0:T(8,128)(2,1)S(1)} collective-permute-done((bf16[32,64,384]{2,1,0:T(8,128)(2,1)S(1)}, bf16[32,64,384]{2,1,0:T(8,128)(2,1)S(1)}, u32[]{:S(2)}, u32[]{:S(2)}) %collective-permute-start.15) | collective-permute-done | bytes 1572896 | tf_op jit(solution)/shard_map/ppermute | solution.py:23
  163.3 6.2 %project.3 = (bf16[1,1024,384]{2,1,0:T(8,128)(2,1)S(1)}, bf16[1,1024,384]{2,1,0:T(8,128)(2,1)S(1)}, bf16[2,32,32,384]{3,2,1,0:T(8,128)(2,1)S(1)}) custom-call(s32[2]{0:T(128)S(1)} %broadcast_xor_fusion.idx_ref, bf16[32,64,384]{2,1,0:T(8,128)(2,1)} %copy-done.11, bf16[32,64,384]{2,1,0:T(8,128)(2,1)} %copy-done.12, ...), custom_call_target="tpu_custom_call" | custom-call | flops 6442450944 | bytes 13631488 | tf_op jit(solution)/shard_map/project/pallas_call | solution.py:164
  171.5 3.9 all-to-all-start
  175.4 10.5 %fusion.6 = f32[512,32,32]{2,1,0:T(8,128)} fusion(bf16[512,32,256]{2,1,0:T(8,128)(2,1)} %param.25, f32[256]{0:T(256)S(1)} %convert_element_type.88, f32[256]{0:T(256)S(1)} %convert_element_type.87, f32[512,32]{1,0:T(8,128)S(1)} %add_rsqrt_fusion, f32[512,32]{1,0:T(8,128)S(1)} %broadcast_multiply_fusion, bf16[256,32]{0,1:T(8,128)(2,1)S(1)} %copy-done.8), kind=kOutput, calls=%fused_computation.8 | convolution fusion | flops 293601280 | bytes 10635264 | tf_op jit(solution)/shard_map/sim,mq->qis/dot_general | solution.py:571
  186.8 6.3 %copy.54 = f32[512,32,32]{0,2,1:T(8,128)} copy(f32[512,32,32]{2,1,0:T(8,128)} %fusion.8) | data formatting | bytes 4194304 | tf_op jit(solution)/shard_map/sim,mp->ips/dot_general | solution.py:569
  193.2 6.6 %copy.56 = f32[512,32,32]{0,1,2:T(8,128)} copy(f32[512,32,32]{2,1,0:T(8,128)} %fusion.6) | data formatting | bytes 4194304 | tf_op jit(solution)/shard_map/sim,mq->qis/dot_general | solution.py:571
  199.8 3.9 fusion.10
  211.1 72.4 %extra_outer.1 = (bf16[16,128,256]{2,1,0:T(8,128)(2,1)}, bf16[16,128,256]{2,1,0:T(8,128)(2,1)}, bf16[16,128,256]{2,1,0:T(8,128)(2,1)}, bf16[16,128,256]{2,1,0:T(...) custom-call(s32[1]{0:T(128)} %bitcast.me_ref.idx_ref, ...), custom_call_target="tpu_custom_call" | custom-call | flops 64424509440 | bytes 33554432 | tf_op jit(solution)/shard_map/extra_outer/pallas_call | solution.py:313
  290.2 13.1 %main_late.1.refs_12_ = bf16[32,64,256]{2,1,0:T(8,128)(2,1)S(1)} custom-call(bf16[8,64,32,256]{3,2,1,0:T(8,128)(2,1)} %bitcast.8.x_ref.ref, f32[64,256]{1,0:T(8,128)S(1)} %dynamic-slice_convert_fusion.4.mask_ref, f32[1,256]{1,0:T(1,128)S(1)} %bitcast.44, f32[1,256]{1,0:T(1,128)S(1)} %bitcast.43, bf16[32,256]{1,0:T(8,128)(2,1)S(1)} %bitcast.42, ...), custom_call_target="tpu_custom_call" | custom-call | flops 4294967296 | bytes 10485760 | tf_op jit(solution)/shard_map/main_late/pallas_call | solution.py:365
  304.2 14.8 %collective-permute-done.6.refs_8_ = bf16[48,32,128]{2,1,0:T(8,128)(2,1)S(1)} collective-permute-done((bf16[48,32,128]{2,1,0:T(8,128)(2,1)S(1)}, bf16[48,32,128]{2,1,0:T(8,128)(2,1)S(1)}, u32[]{:S(2)}, u32[]{:S(2)}) %collective-permute-start.6) | collective-permute-done | bytes 393248 | tf_op jit(solution)/shard_map/ppermute | solution.py:23
  320.4 18.0 %turn_out.2.refs_4_ = bf16[384,64,256]{2,1,0:T(8,128)(2,1)} custom-call(s32[1]{0:T(128)} %bitcast.me_ref.idx_ref, bf16[32,64,384]{2,1,0:T(8,128)(2,1)} %get-tuple-element.42.refs_0_, bf16[32,64,384]{2,1,0:T(8,128)(2,1)} %collective-permute-done.17.refs_3_.refs_1_, bf16[32,64,384]{2,1,0:T(8,128)(2,1)} %copy-done.4, ...), custom_call_target="tpu_custom_call" | custom-call | flops 16777216 | bytes 13631488 | tf_op jit(solution)/shard_map/turn_out/pallas_call | solution.py:81
  338.4 18.4 %turn_out.3 = bf16[384,64,256]{2,1,0:T(8,128)(2,1)} custom-call(s32[1]{0:T(128)} %bitcast.me_ref.idx_ref, bf16[32,64,384]{2,1,0:T(8,128)(2,1)} %collective-permute-done.11.refs_2_.refs_0_, bf16[32,64,384]{2,1,0:T(8,128)(2,1)} %collective-permute-done.13.refs_5_.refs_1_, bf16[32,64,384]{2,1,0:T(8,128)(2,1)} %copy-done.11, ...), custom_call_target="tpu_custom_call", output_to_operand_aliasing={{}: (5, {})} | custom-call | flops 16777216 | bytes 13631488 | tf_op jit(solution)/shard_map/turn_out/pallas_call | solution.py:81
  362.6 9.0 %assemble.1 = bf16[64,256,256]{2,1,0:T(8,128)(2,1)} custom-call(bf16[8,64,32,256]{3,2,1,0:T(8,128)(2,1)} %bitcast.8.x_ref.ref), custom_call_target="tpu_custom_call" | custom-call | flops 16777216 | bytes 16777216 | tf_op jit(solution)/shard_map/assemble/pallas_call | solution.py:506
  377.2 25.4 %main_outer.1.base_ref = f32[32,256,128]{2,1,0:T(8,128)} custom-call(s32[1]{0:T(128)} %bitcast.me_ref.idx_ref, bf16[1024,512]{1,0:T(8,128)(2,1)} %bitcast.51, bf16[96,32,128]{2,1,0:T(8,128)(2,1)} %get-tuple-element.68.refs_0_, bf16[96,32,128]{2,1,0:T(8,128)(2,1)} %get-tuple-element.67.refs_1_, bf16[96,32,128]{2,1,0:T(8,128)(2,1)} %collective-permute-done.refs_2_, ...), custom_call_target="tpu_custom_call" | custom-call | flops 12884901888 | bytes 20971520 | tf_op jit(solution)/shard_map/main_outer/pallas_call | solution.py:428
  407.4 12.8 %collective-permute-done.27.upper_ref = bf16[16,128,256]{2,1,0:T(8,128)(2,1)} collective-permute-done((bf16[16,128,256]{2,1,0:T(8,128)(2,1)}, bf16[16,128,256]{2,1,0:T(8,128)(2,1)}, u32[]{:S(2)}, u32[]{:S(2)}) %collective-permute-start.27) | collective-permute-done | bytes 1048608 | tf_op jit(solution)/shard_map/ppermute | solution.py:23
  421.1 4.2 combine.3
  (168 shorter events, 59.4 us)
Async XLA Ops:
  3.8 38.8 %collective-permute-start.10 = (bf16[32,64,384]{2,1,0:T(8,128)(2,1)}, bf16[32,64,384]{2,1,0:T(8,128)(2,1)S(1)}, u32[]{:S(2)}, u32[]{:S(2)}) collective-permute-start(bf16[32,64,384]{2,1,0:T(8,128)(2,1)} %get-tuple-element.33), channel_id=1, source_target_pairs={{0,2},{1,3},{2,0},{3,1},{4,6},{5,7},{6,4},{7,5}} | collective-permute-start | bytes 4718600 | tf_op jit(solution)/shard_map/ppermute | solution.py:23
  7.1 37.6 %collective-permute-start.11 = (bf16[32,64,384]{2,1,0:T(8,128)(2,1)}, bf16[32,64,384]{2,1,0:T(8,128)(2,1)}, u32[]{:S(2)}, u32[]{:S(2)}) collective-permute-start(bf16[32,64,384]{2,1,0:T(8,128)(2,1)} %get-tuple-element.34), channel_id=1, source_target_pairs={{0,4},{1,5},{2,6},{3,7},{4,0},{5,1},{6,2},{7,3}} | collective-permute-start | bytes 4718600 | tf_op jit(solution)/shard_map/ppermute | solution.py:23
  11.8 63.0 %collective-permute-start.12 = (bf16[32,64,384]{2,1,0:T(8,128)(2,1)}, bf16[32,64,384]{2,1,0:T(8,128)(2,1)}, u32[]{:S(2)}, u32[]{:S(2)}) collective-permute-start(bf16[32,64,384]{2,1,0:T(8,128)(2,1)} %get-tuple-element.35), channel_id=1, source_target_pairs={{0,3},{1,2},{2,1},{3,0},{4,7},{5,6},{6,5},{7,4}} | collective-permute-start | bytes 4718600 | tf_op jit(solution)/shard_map/ppermute | solution.py:23
  11.8 64.2 %collective-permute-start.13 = (bf16[32,64,384]{2,1,0:T(8,128)(2,1)}, bf16[32,64,384]{2,1,0:T(8,128)(2,1)}, u32[]{:S(2)}, u32[]{:S(2)}) collective-permute-start(bf16[32,64,384]{2,1,0:T(8,128)(2,1)} %get-tuple-element.36), channel_id=1, source_target_pairs={{0,5},{1,4},{2,7},{3,6},{4,1},{5,0},{6,3},{7,2}} | collective-permute-start | bytes 4718600 | tf_op jit(solution)/shard_map/ppermute | solution.py:23
  17.5 58.6 %collective-permute-start.17 = (bf16[32,64,384]{2,1,0:T(8,128)(2,1)}, bf16[32,64,384]{2,1,0:T(8,128)(2,1)}, u32[]{:S(2)}, u32[]{:S(2)}) collective-permute-start(bf16[32,64,384]{2,1,0:T(8,128)(2,1)} %get-tuple-element.45), channel_id=1, source_target_pairs={{0,1},{1,0},{2,3},{3,2},{4,5},{5,4},{6,7},{7,6}} | collective-permute-start | bytes 4718600 | tf_op jit(solution)/shard_map/ppermute | solution.py:23
  91.3 119.8 %collective-permute-start.20 = (bf16[6,32,32,384]{3,2,1,0:T(8,128)(2,1)}, bf16[6,32,32,384]{3,2,1,0:T(8,128)(2,1)}, u32[]{:S(2)}, u32[]{:S(2)}) collective-permute-start(bf16[6,32,32,384]{3,2,1,0:T(8,128)(2,1)} %get-tuple-element.54.refs_4_), channel_id=1, source_target_pairs={{0,1},{1,0},{2,3},{3,2},{4,5},{5,4},{6,7},{7,6}} | collective-permute-start | bytes 14155784 | tf_op jit(solution)/shard_map/ppermute | solution.py:23
  92.1 38.2 %collective-permute-start.14 = (bf16[32,64,384]{2,1,0:T(8,128)(2,1)S(1)}, bf16[32,64,384]{2,1,0:T(8,128)(2,1)S(1)}, u32[]{:S(2)}, u32[]{:S(2)}) collective-permute-start(bf16[32,64,384]{2,1,0:T(8,128)(2,1)S(1)} %copy-done.26), channel_id=1, source_target_pairs={{0,6},{1,7},{2,4},{3,5},{4,2},{5,3},{6,0},{7,1}} | collective-permute-start | bytes 4718600 | tf_op jit(solution)/shard_map/ppermute | solution.py:23
  93.7 68.5 %collective-permute-start.15 = (bf16[32,64,384]{2,1,0:T(8,128)(2,1)S(1)}, bf16[32,64,384]{2,1,0:T(8,128)(2,1)S(1)}, u32[]{:S(2)}, u32[]{:S(2)}) collective-permute-start(bf16[32,64,384]{2,1,0:T(8,128)(2,1)S(1)} %copy-done.25), channel_id=1, source_target_pairs={{0,7},{1,6},{2,5},{3,4},{4,3},{5,2},{6,1},{7,0}} | collective-permute-start | bytes 4718600 | tf_op jit(solution)/shard_map/ppermute | solution.py:23
  111.8 97.6 %collective-permute-start.18 = (bf16[3,1024,384]{2,1,0:T(8,128)(2,1)}, bf16[3,1024,384]{2,1,0:T(8,128)(2,1)}, u32[]{:S(2)}, u32[]{:S(2)}) collective-permute-start(bf16[3,1024,384]{2,1,0:T(8,128)(2,1)} %get-tuple-element.49), channel_id=1, source_target_pairs={{0,1},{1,0},{2,3},{3,2},{4,5},{5,4},{6,7},{7,6}} | collective-permute-start | bytes 7077896 | tf_op jit(solution)/shard_map/ppermute | solution.py:23
  170.4 40.6 %collective-permute-start.21 = (bf16[2,32,32,384]{3,2,1,0:T(8,128)(2,1)S(1)}, bf16[2,32,32,384]{3,2,1,0:T(8,128)(2,1)}, u32[]{:S(2)}, u32[]{:S(2)}) collective-permute-start(bf16[2,32,32,384]{3,2,1,0:T(8,128)(2,1)S(1)} %get-tuple-element.55.refs_6_), channel_id=1, source_target_pairs={{0,1},{1,0},{2,3},{3,2},{4,5},{5,4},{6,7},{7,6}} | collective-permute-start | bytes 4718600 | tf_op jit(solution)/shard_map/ppermute | solution.py:23
  171.5 118.6 %all-to-all-start = ((bf16[512,32,256]{2,1,0:T(8,128)(2,1)}), bf16[512,32,256]{2,1,0:T(8,128)(2,1)}, u32[]{:S(2)}, u32[]{:S(2)}) async-start(bf16[512,32,256]{2,1,0:T(8,128)(2,1)} %param.25), calls=%async_computation | async-start | bytes 16777216 | tf_op jit(solution)/shard_map/all_to_all | solution.py:588
  205.3 82.4 %collective-permute-start = (bf16[96,32,128]{2,1,0:T(8,128)(2,1)}, bf16[96,32,128]{2,1,0:T(8,128)(2,1)}, u32[]{:S(2)}, u32[]{:S(2)}) collective-permute-start(bf16[96,32,128]{2,1,0:T(8,128)(2,1)} %get-tuple-element.68.refs_0_), channel_id=1, source_target_pairs={{0,2},{1,3},{2,0},{3,1},{4,6},{5,7},{6,4},{7,5}} | collective-permute-start | bytes 2359304 | tf_op jit(solution)/shard_map/ppermute | solution.py:23
  209.3 80.2 %collective-permute-start.2 = (bf16[96,32,128]{2,1,0:T(8,128)(2,1)}, bf16[96,32,128]{2,1,0:T(8,128)(2,1)}, u32[]{:S(2)}, u32[]{:S(2)}) collective-permute-start(bf16[96,32,128]{2,1,0:T(8,128)(2,1)} %get-tuple-element.68.refs_0_), channel_id=1, source_target_pairs={{0,1},{1,0},{2,3},{3,2},{4,5},{5,4},{6,7},{7,6}} | collective-permute-start | bytes 2359304 | tf_op jit(solution)/shard_map/ppermute | solution.py:23
  209.4 76.0 %collective-permute-start.1 = (bf16[96,32,128]{2,1,0:T(8,128)(2,1)}, bf16[96,32,128]{2,1,0:T(8,128)(2,1)}, u32[]{:S(2)}, u32[]{:S(2)}) collective-permute-start(bf16[96,32,128]{2,1,0:T(8,128)(2,1)} %get-tuple-element.67.refs_1_), channel_id=1, source_target_pairs={{0,4},{1,5},{2,6},{3,7},{4,0},{5,1},{6,2},{7,3}} | collective-permute-start | bytes 2359304 | tf_op jit(solution)/shard_map/ppermute | solution.py:23
  210.9 92.4 %collective-permute-start.3 = (bf16[96,32,128]{2,1,0:T(8,128)(2,1)}, bf16[96,32,128]{2,1,0:T(8,128)(2,1)}, u32[]{:S(2)}, u32[]{:S(2)}) collective-permute-start(bf16[96,32,128]{2,1,0:T(8,128)(2,1)} %get-tuple-element.67.refs_1_), channel_id=1, source_target_pairs={{0,1},{1,0},{2,3},{3,2},{4,5},{5,4},{6,7},{7,6}} | collective-permute-start | bytes 2359304 | tf_op jit(solution)/shard_map/ppermute | solution.py:23
  283.4 73.3 %collective-permute-start.26 = (bf16[16,128,256]{2,1,0:T(8,128)(2,1)}, bf16[16,128,256]{2,1,0:T(8,128)(2,1)}, u32[]{:S(2)}, u32[]{:S(2)}) collective-permute-start(bf16[16,128,256]{2,1,0:T(8,128)(2,1)} %get-tuple-element.62), channel_id=1, source_target_pairs={{0,4},{1,5},{2,6},{3,7},{4,0},{5,1},{6,2},{7,3}} | collective-permute-start | bytes 3145736 | tf_op jit(solution)/shard_map/ppermute | solution.py:23
  285.5 71.4 %collective-permute-start.24 = (bf16[16,128,256]{2,1,0:T(8,128)(2,1)}, bf16[16,128,256]{2,1,0:T(8,128)(2,1)}, u32[]{:S(2)}, u32[]{:S(2)}) collective-permute-start(bf16[16,128,256]{2,1,0:T(8,128)(2,1)} %get-tuple-element.60), channel_id=1, source_target_pairs={{0,2},{1,3},{2,0},{3,1},{4,6},{5,7},{6,4},{7,5}} | collective-permute-start | bytes 3145736 | tf_op jit(solution)/shard_map/ppermute | solution.py:23
  287.7 31.3 %collective-permute-start.6 = (bf16[48,32,128]{2,1,0:T(8,128)(2,1)S(1)}, bf16[48,32,128]{2,1,0:T(8,128)(2,1)S(1)}, u32[]{:S(2)}, u32[]{:S(2)}) collective-permute-start(bf16[48,32,128]{2,1,0:T(8,128)(2,1)S(1)} %slice.8), channel_id=1, source_target_pairs={{0,2},{1,3},{2,0},{3,1},{4,6},{5,7},{6,4},{7,5}} | collective-permute-start | bytes 1179656 | tf_op jit(solution)/shard_map/ppermute | solution.py:23
  303.3 73.1 %collective-permute-start.16 = (bf16[32,64,256]{2,1,0:T(8,128)(2,1)S(1)}, bf16[32,64,256]{2,1,0:T(8,128)(2,1)}, u32[]{:S(2)}, u32[]{:S(2)}) collective-permute-start(bf16[32,64,256]{2,1,0:T(8,128)(2,1)S(1)} %main_late.1.refs_12_), channel_id=1, source_target_pairs={{0,1},{1,0},{2,3},{3,2},{4,5},{5,4},{6,7},{7,6}} | collective-permute-start | bytes 3145736 | tf_op jit(solution)/shard_map/ppermute | solution.py:23
  319.0 55.1 %collective-permute-start.4 = (bf16[96,32,128]{2,1,0:T(8,128)(2,1)}, bf16[96,32,128]{2,1,0:T(8,128)(2,1)}, u32[]{:S(2)}, u32[]{:S(2)}) collective-permute-start(bf16[96,32,128]{2,1,0:T(8,128)(2,1)} %collective-permute-done.refs_2_), channel_id=1, source_target_pairs={{0,1},{1,0},{2,3},{3,2},{4,5},{5,4},{6,7},{7,6}} | collective-permute-start | bytes 2359304 | tf_op jit(solution)/shard_map/ppermute | solution.py:23
  319.0 56.2 %collective-permute-start.5 = (bf16[96,32,128]{2,1,0:T(8,128)(2,1)}, bf16[96,32,128]{2,1,0:T(8,128)(2,1)}, u32[]{:S(2)}, u32[]{:S(2)}) collective-permute-start(bf16[96,32,128]{2,1,0:T(8,128)(2,1)} %collective-permute-done.1.refs_3_), channel_id=1, source_target_pairs={{0,1},{1,0},{2,3},{3,2},{4,5},{5,4},{6,7},{7,6}} | collective-permute-start | bytes 2359304 | tf_op jit(solution)/shard_map/ppermute | solution.py:23
  372.4 30.2 %collective-permute-start.22 = (bf16[16,128,256]{2,1,0:T(8,128)(2,1)}, bf16[16,128,256]{2,1,0:T(8,128)(2,1)S(1)}, u32[]{:S(2)}, u32[]{:S(2)}) collective-permute-start(bf16[16,128,256]{2,1,0:T(8,128)(2,1)} %get-tuple-element.56), channel_id=1, source_target_pairs={{0,2},{1,3},{2,0},{3,1},{4,6},{5,7},{6,4},{7,5}} | collective-permute-start | bytes 3145736 | tf_op jit(solution)/shard_map/ppermute | solution.py:23
  374.1 46.2 %collective-permute-start.27 = (bf16[16,128,256]{2,1,0:T(8,128)(2,1)}, bf16[16,128,256]{2,1,0:T(8,128)(2,1)}, u32[]{:S(2)}, u32[]{:S(2)}) collective-permute-start(bf16[16,128,256]{2,1,0:T(8,128)(2,1)} %add_convert_fusion), channel_id=1, source_target_pairs={{0,2},{1,3},{2,0},{3,1},{4,6},{5,7},{6,4},{7,5}} | collective-permute-start | bytes 3145736 | tf_op jit(solution)/shard_map/ppermute | solution.py:23
  375.1 46.0 %collective-permute-start.25 = (bf16[16,128,256]{2,1,0:T(8,128)(2,1)}, bf16[16,128,256]{2,1,0:T(8,128)(2,1)}, u32[]{:S(2)}, u32[]{:S(2)}) collective-permute-start(bf16[16,128,256]{2,1,0:T(8,128)(2,1)} %add_convert_fusion.1), channel_id=1, source_target_pairs={{0,4},{1,5},{2,6},{3,7},{4,0},{5,1},{6,2},{7,3}} | collective-permute-start | bytes 3145736 | tf_op jit(solution)/shard_map/ppermute | solution.py:23
  (40 other events, 762.7 us)

commit v5 on v4

--- a/solution.py
+++ b/solution.py
@@ -392,27 +392,38 @@
     w_ref, bias_ref, inv_ref, z_ref, out_ref, a_v, c_v, b_v, l_v, o_v, sa, sb = refs[len(tables) + 2:]
     me = idx_ref[0]
     chip, core = me // 2, lax.rem(me, 2)
-    copies = []
     lanes = lambda n: pl.ds(pl.multiple_of(n * LANES, LANES), LANES)
+    first_copies = []
     for r in range(4):
         target = c_v if r == 0 else a_v.at[:, lanes(r - 1)]
-        copies.append(pltpu.make_async_copy(a_ref.at[:, lanes(chip ^ r)], target, sa.at[r]))
+        first_copies.append(pltpu.make_async_copy(a_ref.at[:, lanes(chip ^ r)], target, sa.at[r]))
     for n, ref in enumerate(late_refs):
         seqs = ref.shape[1]
         at = pl.ds(pl.multiple_of((core ^ n) * seqs, seqs), seqs)
-        copies.append(pltpu.make_async_copy(ref, l_v.at[:, at, :], sa.at[4 + n]))
-    count = 0
+        first_copies.append(pltpu.make_async_copy(ref, l_v.at[:, at, :], sa.at[4 + n]))
+    width = b_refs[0].shape[1]
+    groups = b_v.shape[0] // qu
+    b_copies = [[] for _ in range(groups)]
     for ref, (core_bit, table) in zip(b_refs, tables):
         for first, rows, k, q, r in table:
-            width = ref.shape[1]
             js = pl.ds(pl.multiple_of((me ^ k ^ core_bit) * width, width), width)
-            copies.append(pltpu.make_async_copy(ref.at[pl.ds(first, rows)], b_v.at[pl.ds(q, rows), js, lanes(r - 1)], sb.at[count]))
-            count += 1
-    for c in copies:
+            for part in range(rows // qu):
+                src = ref.at[pl.ds(first + part * qu, qu)]
+                g = q // qu + part
+                b_copies[g].append(pltpu.make_async_copy(src, b_v.at[pl.ds(g * qu, qu), js, lanes(r - 1)], sb.at[g, len(b_copies[g])]))
+    for c in first_copies + [c for group in b_copies for c in group]:
         c.start()
-    for c in copies:
+    for c in first_copies:
         c.wait()
-    outer_rows(a_v, b_v, o_v, qu, more=(c_v, l_v))
+
+    def ready(g):
+        for n in range(groups):
+            @pl.when(g == n)
+            def _(n=n):
+                for c in b_copies[n]:
+                    c.wait()
+
+    outer_rows(a_v, b_v, o_v, qu, ready=ready, more=(c_v, l_v))
 
     def store(i, r):
         out_ref[i] = z_ref[i] + ((r + bias_ref[...]) * inv_ref[pl.ds(i, 1), :]).T
@@ -423,7 +434,7 @@
 def main_rows(me, a, b_parts, tables, late, w_t, bias, inv, z, qu=8, iu=8):
     rows, cols, _ = z.shape
     hid = a.shape[0] // rows
-    count = sum(len(table) for _, table in tables)
+    pieces = sum(piece[1] for _, table in tables for piece in table) // hid
     whole = lambda v: pl.BlockSpec(v.shape, lambda s, i: (0,) * v.ndim)
     return pl.pallas_call(
         functools.partial(main_kernel, tables, qu, iu),
@@ -439,11 +450,11 @@
                 pltpu.VMEM((hid, LANES, cols), BF16),
                 pltpu.VMEM((rows, hid, hid, cols), BF16),
                 pltpu.SemaphoreType.DMA((6,)),
-                pltpu.SemaphoreType.DMA((count,)),
+                pltpu.SemaphoreType.DMA((hid // qu, pieces)),
             ],
         ),
         out_shape=jax.ShapeDtypeStruct(z.shape, F32),
-        compiler_params=pltpu.CompilerParams(vmem_limit_bytes=60 << 20),
+        compiler_params=pltpu.CompilerParams(vmem_limit_bytes=48 << 20),
         cost_estimate=pl.CostEstimate(flops=12 << 30, bytes_accessed=20 << 20, transcendentals=0),
         name='main_outer',
     )(me, a, *b_parts, *late, w_t, bias, inv, z)

time: 427 us -> 421 us (0.986)
  other arithmetic: 23.6 us -> 29.8 us
    reduce_sum x1, other arithmetic: 6.82 us -> 13.7 us  [layer_norm(): var = jnp.mean(centered * centered, axis=-1, keepdims=True)]
  transfers between devices with their start and end apart: 29 -> 29, of which waited for: 10 -> 10; matrix products, arithmetic and copies ran while one was open for 16% -> 17% of each run, Pallas kernels for 41% -> 41%
where the time goes in v5:
time: 421 us; the launch traced here: 420 us
  Pallas kernels  193 us (46%)
  waiting for transfers between devices  128 us (30%)
  other arithmetic  29.8 us (7%)
  starting transfers between devices  25.8 us (6%)
  local copies, waits for them, and re-layouts  23.6 us (6%)
  matrix products  19.3 us (5%)
    ppermute x28, waiting for transfers between devices, swap(): return lax.ppermute(value, 'dap', [(d, d ^ bit) for d in range(size)])  128 us
    pallas_call x1, Pallas kernels, extra_parts(): pl.pallas_call(functools.partial(extra_kernel, qu, iu), grid_spec=pltpu.P...  72.3 us
    pallas_call x2, Pallas kernels, turn_out(): pl.pallas_call(functools.partial(turn_out_kernel, ks), grid_spec=pltpu.Pr...  36.2 us
    pallas_call x1, Pallas kernels, main_rows(): pl.pallas_call(functools.partial(main_kernel, tables, qu, iu), grid_spec=...  24.8 us
    ppermute x28, starting transfers between devices, swap(): return lax.ppermute(value, 'dap', [(d, d ^ bit) for d in range(size)])  21.9 us
    pallas_call x2, Pallas kernels, project(): pl.pallas_call(functools.partial(project_kernel, group), grid_spec=pltpu....  20.9 us
    pallas_call x1, Pallas kernels, main_late(): pl.pallas_call(main_late_kernel, grid=(seqs // block,), in_specs=[pl.Bloc...  13.8 us
    reduce_sum x1, other arithmetic, layer_norm(): var = jnp.mean(centered * centered, axis=-1, keepdims=True)  13.7 us
  transfers between devices with their start and end apart: 29, of which 10 were waited for; matrix products, arithmetic and copies ran while one was open for 17% of the time, Pallas kernels for 41%

profile of v5, /device:TPU:0, one launch (start us, length us, event | category | flops | bytes accessed | tf_op | source)
XLA Modules:
  0.0 420.4 jit_solution(4539233554797845633)
XLA Ops:
  3.8 3.3 collective-permute-start.10
  12.1 5.4 %turn.5 = (bf16[32,64,384]{2,1,0:T(8,128)(2,1)}, bf16[32,64,384]{2,1,0:T(8,128)(2,1)}, bf16[32,64,384]{2,1,0:T(8,128)(2,1)}, bf16[32,64,384]{2,1,0:T(8,128)(2,1)}) custom-call(s32[1]{0:T(128)} %bitcast.me_ref.idx_ref, bf16[32,64,3072]{2,1,0:T(8,128)(2,1)} %bitcast.47), custom_call_target="tpu_custom_call" | custom-call | flops 16777216 | bytes 4194304 | tf_op jit(solution)/shard_map/turn/pallas_call | solution.py:46
  20.5 5.7 %convert_reduce_fusion = f32[512,32]{1,0:T(8,128)S(1)} fusion(bf16[512,32,256]{2,1,0:T(8,128)(2,1)} %param.25), kind=kLoop, calls=%fused_computation.1 | loop fusion | flops 8372224 | bytes 8454144 | tf_op jit(solution)/shard_map/reduce_sum | solution.py:530
  26.2 16.3 %collective-permute-done.10.refs_1_.refs_2_ = bf16[32,64,384]{2,1,0:T(8,128)(2,1)S(1)} collective-permute-done((bf16[32,64,384]{2,1,0:T(8,128)(2,1)}, bf16[32,64,384]{2,1,0:T(8,128)(2,1)S(1)}, u32[]{:S(2)}, u32[]{:S(2)}) %collective-permute-start.10) | collective-permute-done | bytes 1572896 | tf_op jit(solution)/shard_map/ppermute | solution.py:23
  44.7 30.1 %collective-permute-done.12.refs_4_.refs_3_ = bf16[32,64,384]{2,1,0:T(8,128)(2,1)} collective-permute-done((bf16[32,64,384]{2,1,0:T(8,128)(2,1)}, bf16[32,64,384]{2,1,0:T(8,128)(2,1)}, u32[]{:S(2)}, u32[]{:S(2)}) %collective-permute-start.12) | collective-permute-done | bytes 1572896 | tf_op jit(solution)/shard_map/ppermute | solution.py:23
  76.4 14.1 %project.2 = (bf16[3,1024,384]{2,1,0:T(8,128)(2,1)}, bf16[3,1024,384]{2,1,0:T(8,128)(2,1)}, bf16[6,32,32,384]{3,2,1,0:T(8,128)(2,1)}) custom-call(s32[6]{0:T(128)S(1)} %broadcast_xor_fusion.1.idx_ref, bf16[32,64,384]{2,1,0:T(8,128)(2,1)S(1)} %copy-done.5, bf16[32,64,384]{2,1,0:T(8,128)(2,1)S(1)} %collective-permute-done.10.refs_1_.refs_2_, ...), custom_call_target="tpu_custom_call" | custom-call | flops 6442450944 | bytes 13631488 | tf_op jit(solution)/shard_map/project/pallas_call | solution.py:164
  93.7 13.7 %fusion.2 = f32[512,32]{1,0:T(8,128)S(1)} fusion(bf16[512,32,256]{2,1,0:T(8,128)(2,1)S(1)} %bitcast.49, f32[512,32]{1,0:T(8,128)S(1)} %broadcast_multiply_fusion), kind=kLoop, calls=%fused_computation.4 | loop fusion | flops 16760832 | bytes 8519680 | tf_op jit(solution)/shard_map/reduce_sum | solution.py:532
  107.5 7.7 %fusion.8 = f32[512,32,32]{2,1,0:T(8,128)} fusion(bf16[512,32,256]{2,1,0:T(8,128)(2,1)S(1)} %bitcast.49, f32[256]{0:T(256)S(1)} %convert_element_type.88, f32[256]{0:T(256)S(1)} %convert_element_type.87, f32[512,32]{1,0:T(8,128)S(1)} %add_rsqrt_fusion, f32[512,32]{1,0:T(8,128)S(1)} %broadcast_multiply_fusion, bf16[256,32]{0,1:T(8,128)(2,1)S(1)} %copy-done), kind=kOutput, calls=%fused_computation.9 | convolution fusion | flops 293601280 | bytes 10635264 | tf_op jit(solution)/shard_map/sim,mp->ips/dot_general | solution.py:580
  116.0 13.9 %collective-permute-done.14.refs_0_.refs_2_ = bf16[32,64,384]{2,1,0:T(8,128)(2,1)S(1)} collective-permute-done((bf16[32,64,384]{2,1,0:T(8,128)(2,1)}, bf16[32,64,384]{2,1,0:T(8,128)(2,1)S(1)}, u32[]{:S(2)}, u32[]{:S(2)}) %collective-permute-start.14) | collective-permute-done | bytes 1572896 | tf_op jit(solution)/shard_map/ppermute | solution.py:23
  129.8 31.9 %collective-permute-done.15.refs_1_.refs_3_ = bf16[32,64,384]{2,1,0:T(8,128)(2,1)} collective-permute-done((bf16[32,64,384]{2,1,0:T(8,128)(2,1)}, bf16[32,64,384]{2,1,0:T(8,128)(2,1)}, u32[]{:S(2)}, u32[]{:S(2)}) %collective-permute-start.15) | collective-permute-done | bytes 1572896 | tf_op jit(solution)/shard_map/ppermute | solution.py:23
  161.7 6.8 %project.3 = (bf16[1,1024,384]{2,1,0:T(8,128)(2,1)S(1)}, bf16[1,1024,384]{2,1,0:T(8,128)(2,1)S(1)}, bf16[2,32,32,384]{3,2,1,0:T(8,128)(2,1)}) custom-call(s32[2]{0:T(128)S(1)} %broadcast_xor_fusion.idx_ref, bf16[32,64,384]{2,1,0:T(8,128)(2,1)} %copy-done.9, bf16[32,64,384]{2,1,0:T(8,128)(2,1)} %collective-permute-done.15.refs_1_.refs_3_, ...), custom_call_target="tpu_custom_call" | custom-call | flops 6442450944 | bytes 13631488 | tf_op jit(solution)/shard_map/project/pallas_call | solution.py:164
  169.4 3.9 all-to-all-start
  173.4 10.5 %fusion.6 = f32[512,32,32]{2,1,0:T(8,128)} fusion(bf16[512,32,256]{2,1,0:T(8,128)(2,1)} %param.25, f32[256]{0:T(256)S(1)} %convert_element_type.88, f32[256]{0:T(256)S(1)} %convert_element_type.87, f32[512,32]{1,0:T(8,128)S(1)} %add_rsqrt_fusion, f32[512,32]{1,0:T(8,128)S(1)} %broadcast_multiply_fusion, bf16[256,32]{0,1:T(8,128)(2,1)S(1)} %copy-done.6), kind=kOutput, calls=%fused_computation.8 | convolution fusion | flops 293601280 | bytes 10635264 | tf_op jit(solution)/shard_map/sim,mq->qis/dot_general | solution.py:582
  184.8 5.3 %copy.54 = f32[512,32,32]{0,2,1:T(8,128)S(1)} copy(f32[512,32,32]{2,1,0:T(8,128)} %fusion.8) | data formatting | bytes 4194304 | tf_op jit(solution)/shard_map/sim,mp->ips/dot_general | solution.py:580
  190.1 6.6 %copy.56 = f32[512,32,32]{0,1,2:T(8,128)} copy(f32[512,32,32]{2,1,0:T(8,128)} %fusion.6) | data formatting | bytes 4194304 | tf_op jit(solution)/shard_map/sim,mq->qis/dot_general | solution.py:582
  196.7 3.2 fusion.10
  208.0 72.3 %extra_outer.1 = (bf16[16,128,256]{2,1,0:T(8,128)(2,1)}, bf16[16,128,256]{2,1,0:T(8,128)(2,1)}, bf16[16,128,256]{2,1,0:T(8,128)(2,1)}, bf16[16,128,256]{2,1,0:T(...) custom-call(s32[1]{0:T(128)} %bitcast.me_ref.idx_ref, ...), custom_call_target="tpu_custom_call" | custom-call | flops 64424509440 | bytes 33554432 | tf_op jit(solution)/shard_map/extra_outer/pallas_call | solution.py:313
  288.3 13.8 %main_late.1.refs_12_ = bf16[32,64,256]{2,1,0:T(8,128)(2,1)} custom-call(bf16[8,64,32,256]{3,2,1,0:T(8,128)(2,1)} %bitcast.8.x_ref.ref, f32[64,256]{1,0:T(8,128)S(1)} %dynamic-slice_convert_fusion.4.mask_ref, f32[1,256]{1,0:T(1,128)S(1)} %bitcast.44, f32[1,256]{1,0:T(1,128)S(1)} %bitcast.43, bf16[32,256]{1,0:T(8,128)(2,1)S(1)} %bitcast.42, ...), custom_call_target="tpu_custom_call" | custom-call | flops 4294967296 | bytes 10485760 | tf_op jit(solution)/shard_map/main_late/pallas_call | solution.py:365
  303.0 14.0 %collective-permute-done.6.refs_8_ = bf16[48,32,128]{2,1,0:T(8,128)(2,1)} collective-permute-done((bf16[48,32,128]{2,1,0:T(8,128)(2,1)}, bf16[48,32,128]{2,1,0:T(8,128)(2,1)}, u32[]{:S(2)}, u32[]{:S(2)}) %collective-permute-start.6) | collective-permute-done | bytes 393248 | tf_op jit(solution)/shard_map/ppermute | solution.py:23
  317.8 18.0 %turn_out.2.refs_4_ = bf16[384,64,256]{2,1,0:T(8,128)(2,1)} custom-call(s32[1]{0:T(128)} %bitcast.me_ref.idx_ref, bf16[32,64,384]{2,1,0:T(8,128)(2,1)} %get-tuple-element.42.refs_0_, bf16[32,64,384]{2,1,0:T(8,128)(2,1)} %collective-permute-done.17.refs_3_.refs_1_, bf16[32,64,384]{2,1,0:T(8,128)(2,1)} %copy-done.4, ...), custom_call_target="tpu_custom_call" | custom-call | flops 16777216 | bytes 13631488 | tf_op jit(solution)/shard_map/turn_out/pallas_call | solution.py:81
  335.8 18.2 %turn_out.3 = bf16[384,64,256]{2,1,0:T(8,128)(2,1)} custom-call(s32[1]{0:T(128)} %bitcast.me_ref.idx_ref, bf16[32,64,384]{2,1,0:T(8,128)(2,1)} %collective-permute-done.11.refs_2_.refs_0_, bf16[32,64,384]{2,1,0:T(8,128)(2,1)} %collective-permute-done.13.refs_5_.refs_1_, bf16[32,64,384]{2,1,0:T(8,128)(2,1)} %copy-done.9, ...), custom_call_target="tpu_custom_call", output_to_operand_aliasing={{}: (5, {})} | custom-call | flops 16777216 | bytes 13631488 | tf_op jit(solution)/shard_map/turn_out/pallas_call | solution.py:81
  360.2 9.0 %assemble.1 = bf16[64,256,256]{2,1,0:T(8,128)(2,1)} custom-call(bf16[8,64,32,256]{3,2,1,0:T(8,128)(2,1)} %bitcast.8.x_ref.ref), custom_call_target="tpu_custom_call" | custom-call | flops 16777216 | bytes 16777216 | tf_op jit(solution)/shard_map/assemble/pallas_call | solution.py:517
  373.4 24.8 %main_outer.1.base_ref = f32[32,256,128]{2,1,0:T(8,128)} custom-call(s32[1]{0:T(128)} %bitcast.me_ref.idx_ref, bf16[1024,512]{1,0:T(8,128)(2,1)} %bitcast.53, bf16[96,32,128]{2,1,0:T(8,128)(2,1)S(1)} %get-tuple-element.68.refs_0_, bf16[96,32,128]{2,1,0:T(8,128)(2,1)S(1)} %get-tuple-element.67.refs_1_, bf16[96,32,128]{2,1,0:T(8,128)(2,1)S(1)} %collective-permute-done.refs_2_, ...), custom_call_target="tpu_custom_call" | custom-call | flops 12884901888 | bytes 20971520 | tf_op jit(solution)/shard_map/main_outer/pallas_call | solution.py:439
  401.8 15.2 %collective-permute-done.27.upper_ref = bf16[16,128,256]{2,1,0:T(8,128)(2,1)S(1)} collective-permute-done((bf16[16,128,256]{2,1,0:T(8,128)(2,1)}, bf16[16,128,256]{2,1,0:T(8,128)(2,1)S(1)}, u32[]{:S(2)}, u32[]{:S(2)}) %collective-permute-start.27) | collective-permute-done | bytes 1048608 | tf_op jit(solution)/shard_map/ppermute | solution.py:23
  (155 shorter events, 55.4 us)
Async XLA Ops:
  3.8 38.8 %collective-permute-start.10 = (bf16[32,64,384]{2,1,0:T(8,128)(2,1)}, bf16[32,64,384]{2,1,0:T(8,128)(2,1)S(1)}, u32[]{:S(2)}, u32[]{:S(2)}) collective-permute-start(bf16[32,64,384]{2,1,0:T(8,128)(2,1)} %get-tuple-element.33), channel_id=1, source_target_pairs={{0,2},{1,3},{2,0},{3,1},{4,6},{5,7},{6,4},{7,5}} | collective-permute-start | bytes 4718600 | tf_op jit(solution)/shard_map/ppermute | solution.py:23
  7.1 37.6 %collective-permute-start.11 = (bf16[32,64,384]{2,1,0:T(8,128)(2,1)}, bf16[32,64,384]{2,1,0:T(8,128)(2,1)}, u32[]{:S(2)}, u32[]{:S(2)}) collective-permute-start(bf16[32,64,384]{2,1,0:T(8,128)(2,1)} %get-tuple-element.34), channel_id=1, source_target_pairs={{0,4},{1,5},{2,6},{3,7},{4,0},{5,1},{6,2},{7,3}} | collective-permute-start | bytes 4718600 | tf_op jit(solution)/shard_map/ppermute | solution.py:23
  11.8 63.0 %collective-permute-start.12 = (bf16[32,64,384]{2,1,0:T(8,128)(2,1)}, bf16[32,64,384]{2,1,0:T(8,128)(2,1)}, u32[]{:S(2)}, u32[]{:S(2)}) collective-permute-start(bf16[32,64,384]{2,1,0:T(8,128)(2,1)} %get-tuple-element.35), channel_id=1, source_target_pairs={{0,3},{1,2},{2,1},{3,0},{4,7},{5,6},{6,5},{7,4}} | collective-permute-start | bytes 4718600 | tf_op jit(solution)/shard_map/ppermute | solution.py:23
  11.9 64.2 %collective-permute-start.13 = (bf16[32,64,384]{2,1,0:T(8,128)(2,1)}, bf16[32,64,384]{2,1,0:T(8,128)(2,1)}, u32[]{:S(2)}, u32[]{:S(2)}) collective-permute-start(bf16[32,64,384]{2,1,0:T(8,128)(2,1)} %get-tuple-element.36), channel_id=1, source_target_pairs={{0,5},{1,4},{2,7},{3,6},{4,1},{5,0},{6,3},{7,2}} | collective-permute-start | bytes 4718600 | tf_op jit(solution)/shard_map/ppermute | solution.py:23
  17.5 58.6 %collective-permute-start.17 = (bf16[32,64,384]{2,1,0:T(8,128)(2,1)}, bf16[32,64,384]{2,1,0:T(8,128)(2,1)}, u32[]{:S(2)}, u32[]{:S(2)}) collective-permute-start(bf16[32,64,384]{2,1,0:T(8,128)(2,1)} %get-tuple-element.45), channel_id=1, source_target_pairs={{0,1},{1,0},{2,3},{3,2},{4,5},{5,4},{6,7},{7,6}} | collective-permute-start | bytes 4718600 | tf_op jit(solution)/shard_map/ppermute | solution.py:23
  90.6 117.4 %collective-permute-start.20 = (bf16[6,32,32,384]{3,2,1,0:T(8,128)(2,1)}, bf16[6,32,32,384]{3,2,1,0:T(8,128)(2,1)}, u32[]{:S(2)}, u32[]{:S(2)}) collective-permute-start(bf16[6,32,32,384]{3,2,1,0:T(8,128)(2,1)} %get-tuple-element.54.refs_4_), channel_id=1, source_target_pairs={{0,1},{1,0},{2,3},{3,2},{4,5},{5,4},{6,7},{7,6}} | collective-permute-start | bytes 14155784 | tf_op jit(solution)/shard_map/ppermute | solution.py:23
  91.4 38.4 %collective-permute-start.14 = (bf16[32,64,384]{2,1,0:T(8,128)(2,1)}, bf16[32,64,384]{2,1,0:T(8,128)(2,1)S(1)}, u32[]{:S(2)}, u32[]{:S(2)}) collective-permute-start(bf16[32,64,384]{2,1,0:T(8,128)(2,1)} %get-tuple-element.39), channel_id=1, source_target_pairs={{0,6},{1,7},{2,4},{3,5},{4,2},{5,3},{6,0},{7,1}} | collective-permute-start | bytes 4718600 | tf_op jit(solution)/shard_map/ppermute | solution.py:23
  92.9 68.8 %collective-permute-start.15 = (bf16[32,64,384]{2,1,0:T(8,128)(2,1)}, bf16[32,64,384]{2,1,0:T(8,128)(2,1)}, u32[]{:S(2)}, u32[]{:S(2)}) collective-permute-start(bf16[32,64,384]{2,1,0:T(8,128)(2,1)} %get-tuple-element.40), channel_id=1, source_target_pairs={{0,7},{1,6},{2,5},{3,4},{4,3},{5,2},{6,1},{7,0}} | collective-permute-start | bytes 4718600 | tf_op jit(solution)/shard_map/ppermute | solution.py:23
  115.2 91.2 %collective-permute-start.18 = (bf16[3,1024,384]{2,1,0:T(8,128)(2,1)}, bf16[3,1024,384]{2,1,0:T(8,128)(2,1)}, u32[]{:S(2)}, u32[]{:S(2)}) collective-permute-start(bf16[3,1024,384]{2,1,0:T(8,128)(2,1)} %get-tuple-element.49), channel_id=1, source_target_pairs={{0,1},{1,0},{2,3},{3,2},{4,5},{5,4},{6,7},{7,6}} | collective-permute-start | bytes 7077896 | tf_op jit(solution)/shard_map/ppermute | solution.py:23
  168.5 39.3 %collective-permute-start.21 = (bf16[2,32,32,384]{3,2,1,0:T(8,128)(2,1)}, bf16[2,32,32,384]{3,2,1,0:T(8,128)(2,1)}, u32[]{:S(2)}, u32[]{:S(2)}) collective-permute-start(bf16[2,32,32,384]{3,2,1,0:T(8,128)(2,1)} %get-tuple-element.55.refs_6_), channel_id=1, source_target_pairs={{0,1},{1,0},{2,3},{3,2},{4,5},{5,4},{6,7},{7,6}} | collective-permute-start | bytes 4718600 | tf_op jit(solution)/shard_map/ppermute | solution.py:23
  169.4 118.8 %all-to-all-start = ((bf16[512,32,256]{2,1,0:T(8,128)(2,1)}), bf16[512,32,256]{2,1,0:T(8,128)(2,1)}, u32[]{:S(2)}, u32[]{:S(2)}) async-start(bf16[512,32,256]{2,1,0:T(8,128)(2,1)} %param.25), calls=%async_computation | async-start | bytes 16777216 | tf_op jit(solution)/shard_map/all_to_all | solution.py:599
  200.3 85.8 %collective-permute-start = (bf16[96,32,128]{2,1,0:T(8,128)(2,1)S(1)}, bf16[96,32,128]{2,1,0:T(8,128)(2,1)S(1)}, u32[]{:S(2)}, u32[]{:S(2)}) collective-permute-start(bf16[96,32,128]{2,1,0:T(8,128)(2,1)S(1)} %get-tuple-element.68.refs_0_), channel_id=1, source_target_pairs={{0,2},{1,3},{2,0},{3,1},{4,6},{5,7},{6,4},{7,5}} | collective-permute-start | bytes 2359304 | tf_op jit(solution)/shard_map/ppermute | solution.py:23
  206.2 81.5 %collective-permute-start.2 = (bf16[96,32,128]{2,1,0:T(8,128)(2,1)S(1)}, bf16[96,32,128]{2,1,0:T(8,128)(2,1)}, u32[]{:S(2)}, u32[]{:S(2)}) collective-permute-start(bf16[96,32,128]{2,1,0:T(8,128)(2,1)S(1)} %get-tuple-element.68.refs_0_), channel_id=1, source_target_pairs={{0,1},{1,0},{2,3},{3,2},{4,5},{5,4},{6,7},{7,6}} | collective-permute-start | bytes 2359304 | tf_op jit(solution)/shard_map/ppermute | solution.py:23
  206.4 76.9 %collective-permute-start.1 = (bf16[96,32,128]{2,1,0:T(8,128)(2,1)S(1)}, bf16[96,32,128]{2,1,0:T(8,128)(2,1)S(1)}, u32[]{:S(2)}, u32[]{:S(2)}) collective-permute-start(bf16[96,32,128]{2,1,0:T(8,128)(2,1)S(1)} %get-tuple-element.67.refs_1_), channel_id=1, source_target_pairs={{0,4},{1,5},{2,6},{3,7},{4,0},{5,1},{6,2},{7,3}} | collective-permute-start | bytes 2359304 | tf_op jit(solution)/shard_map/ppermute | solution.py:23
  207.9 94.3 %collective-permute-start.3 = (bf16[96,32,128]{2,1,0:T(8,128)(2,1)S(1)}, bf16[96,32,128]{2,1,0:T(8,128)(2,1)}, u32[]{:S(2)}, u32[]{:S(2)}) collective-permute-start(bf16[96,32,128]{2,1,0:T(8,128)(2,1)S(1)} %get-tuple-element.67.refs_1_), channel_id=1, source_target_pairs={{0,1},{1,0},{2,3},{3,2},{4,5},{5,4},{6,7},{7,6}} | collective-permute-start | bytes 2359304 | tf_op jit(solution)/shard_map/ppermute | solution.py:23
  280.3 73.7 %collective-permute-start.26 = (bf16[16,128,256]{2,1,0:T(8,128)(2,1)}, bf16[16,128,256]{2,1,0:T(8,128)(2,1)}, u32[]{:S(2)}, u32[]{:S(2)}) collective-permute-start(bf16[16,128,256]{2,1,0:T(8,128)(2,1)} %get-tuple-element.62), channel_id=1, source_target_pairs={{0,4},{1,5},{2,6},{3,7},{4,0},{5,1},{6,2},{7,3}} | collective-permute-start | bytes 3145736 | tf_op jit(solution)/shard_map/ppermute | solution.py:23
  283.3 70.7 %collective-permute-start.24 = (bf16[16,128,256]{2,1,0:T(8,128)(2,1)}, bf16[16,128,256]{2,1,0:T(8,128)(2,1)}, u32[]{:S(2)}, u32[]{:S(2)}) collective-permute-start(bf16[16,128,256]{2,1,0:T(8,128)(2,1)} %get-tuple-element.60), channel_id=1, source_target_pairs={{0,2},{1,3},{2,0},{3,1},{4,6},{5,7},{6,4},{7,5}} | collective-permute-start | bytes 3145736 | tf_op jit(solution)/shard_map/ppermute | solution.py:23
  286.1 30.8 %collective-permute-start.6 = (bf16[48,32,128]{2,1,0:T(8,128)(2,1)}, bf16[48,32,128]{2,1,0:T(8,128)(2,1)}, u32[]{:S(2)}, u32[]{:S(2)}) collective-permute-start(bf16[48,32,128]{2,1,0:T(8,128)(2,1)} %slice.8), channel_id=1, source_target_pairs={{0,2},{1,3},{2,0},{3,1},{4,6},{5,7},{6,4},{7,5}} | collective-permute-start | bytes 1179656 | tf_op jit(solution)/shard_map/ppermute | solution.py:23
  287.7 29.2 %collective-permute-start.7 = (bf16[48,32,128]{2,1,0:T(8,128)(2,1)}, bf16[48,32,128]{2,1,0:T(8,128)(2,1)}, u32[]{:S(2)}, u32[]{:S(2)}) collective-permute-start(bf16[48,32,128]{2,1,0:T(8,128)(2,1)} %slice.9), channel_id=1, source_target_pairs={{0,4},{1,5},{2,6},{3,7},{4,0},{5,1},{6,2},{7,3}} | collective-permute-start | bytes 1179656 | tf_op jit(solution)/shard_map/ppermute | solution.py:23
  302.1 71.2 %collective-permute-start.16 = (bf16[32,64,256]{2,1,0:T(8,128)(2,1)}, bf16[32,64,256]{2,1,0:T(8,128)(2,1)}, u32[]{:S(2)}, u32[]{:S(2)}) collective-permute-start(bf16[32,64,256]{2,1,0:T(8,128)(2,1)} %main_late.1.refs_12_), channel_id=1, source_target_pairs={{0,1},{1,0},{2,3},{3,2},{4,5},{5,4},{6,7},{7,6}} | collective-permute-start | bytes 3145736 | tf_op jit(solution)/shard_map/ppermute | solution.py:23
  316.9 53.9 %collective-permute-start.4 = (bf16[96,32,128]{2,1,0:T(8,128)(2,1)S(1)}, bf16[96,32,128]{2,1,0:T(8,128)(2,1)}, u32[]{:S(2)}, u32[]{:S(2)}) collective-permute-start(bf16[96,32,128]{2,1,0:T(8,128)(2,1)S(1)} %collective-permute-done.refs_2_), channel_id=1, source_target_pairs={{0,1},{1,0},{2,3},{3,2},{4,5},{5,4},{6,7},{7,6}} | collective-permute-start | bytes 2359304 | tf_op jit(solution)/shard_map/ppermute | solution.py:23
  317.0 55.0 %collective-permute-start.5 = (bf16[96,32,128]{2,1,0:T(8,128)(2,1)S(1)}, bf16[96,32,128]{2,1,0:T(8,128)(2,1)}, u32[]{:S(2)}, u32[]{:S(2)}) collective-permute-start(bf16[96,32,128]{2,1,0:T(8,128)(2,1)S(1)} %collective-permute-done.1.refs_3_), channel_id=1, source_target_pairs={{0,1},{1,0},{2,3},{3,2},{4,5},{5,4},{6,7},{7,6}} | collective-permute-start | bytes 2359304 | tf_op jit(solution)/shard_map/ppermute | solution.py:23
  370.8 46.2 %collective-permute-start.27 = (bf16[16,128,256]{2,1,0:T(8,128)(2,1)}, bf16[16,128,256]{2,1,0:T(8,128)(2,1)S(1)}, u32[]{:S(2)}, u32[]{:S(2)}) collective-permute-start(bf16[16,128,256]{2,1,0:T(8,128)(2,1)} %add_convert_fusion), channel_id=1, source_target_pairs={{0,2},{1,3},{2,0},{3,1},{4,6},{5,7},{6,4},{7,5}} | collective-permute-start | bytes 3145736 | tf_op jit(solution)/shard_map/ppermute | solution.py:23
  371.9 45.8 %collective-permute-start.25 = (bf16[16,128,256]{2,1,0:T(8,128)(2,1)}, bf16[16,128,256]{2,1,0:T(8,128)(2,1)S(1)}, u32[]{:S(2)}, u32[]{:S(2)}) collective-permute-start(bf16[16,128,256]{2,1,0:T(8,128)(2,1)} %add_convert_fusion.1), channel_id=1, source_target_pairs={{0,4},{1,5},{2,6},{3,7},{4,0},{5,1},{6,2},{7,3}} | collective-permute-start | bytes 3145736 | tf_op jit(solution)/shard_map/ppermute | solution.py:23
  (33 other events, 728.9 us)

commit v6 on v5

--- a/solution.py
+++ b/solution.py
@@ -16,6 +16,7 @@
 ANY = pl.BlockSpec(memory_space=pl.ANY)
 CORE, XBIT, YBIT = 1, 2, 4
 LANES = 128
+PIECES = 4
 NEAR, REST = (2, 4, 3, 5), (6, 7, 1, 0)
 
 
@@ -26,11 +27,14 @@
 def turn_kernel(ks, me_ref, x_ref, *refs):
     outs, (v, s_in, s_out) = refs[:len(ks)], refs[len(ks):]
     seqs = v.shape[3]
-    loads = [
-        pltpu.make_async_copy(x_ref.at[:, :, pl.ds(pl.multiple_of((me_ref[0] ^ k) * seqs, LANES), seqs)], v.at[t], s_in.at[t])
-        for t, k in enumerate(ks)
-    ]
-    stores = [pltpu.make_async_copy(v.at[t], out, s_out.at[t]) for t, out in enumerate(outs)]
+    rows = v.shape[1] // PIECES
+    loads, stores = [], []
+    for n in range(len(ks) * PIECES):
+        t, piece = divmod(n, PIECES)
+        at = pl.ds(piece * rows, rows)
+        lanes = pl.ds(pl.multiple_of((me_ref[0] ^ ks[t]) * seqs, LANES), seqs)
+        loads.append(pltpu.make_async_copy(x_ref.at[at, :, lanes], v.at[t, at], s_in.at[n]))
+        stores.append(pltpu.make_async_copy(v.at[t, at], outs[t].at[at], s_out.at[n]))
     for c in loads:
         c.start()
     for load, save in zip(loads, stores):
@@ -52,8 +56,8 @@
             out_specs=[ANY] * len(ks),
             scratch_shapes=[
                 pltpu.VMEM((len(ks), rows, chans, seqs), x.dtype),
-                pltpu.SemaphoreType.DMA((len(ks),)),
-                pltpu.SemaphoreType.DMA((len(ks),)),
+                pltpu.SemaphoreType.DMA((len(ks) * PIECES,)),
+                pltpu.SemaphoreType.DMA((len(ks) * PIECES,)),
             ],
         ),
         out_shape=[jax.ShapeDtypeStruct((rows, chans, seqs), x.dtype) for _ in ks],

time: 421 us -> 421 us (level)
  no operation moved by 1% of the time
where the time goes in v6:
time: 421 us; the launch traced here: 420 us
  Pallas kernels  192 us (46%)
  waiting for transfers between devices  128 us (30%)
  other arithmetic  29.8 us (7%)
  starting transfers between devices  25.8 us (6%)
  local copies, waits for them, and re-layouts  23.6 us (6%)
  matrix products  19.3 us (5%)
    ppermute x28, waiting for transfers between devices, swap(): return lax.ppermute(value, 'dap', [(d, d ^ bit) for d in range(size)])  128 us
    pallas_call x1, Pallas kernels, extra_parts(): pl.pallas_call(functools.partial(extra_kernel, qu, iu), grid_spec=pltpu.P...  72.3 us
    pallas_call x2, Pallas kernels, turn_out(): pl.pallas_call(functools.partial(turn_out_kernel, ks), grid_spec=pltpu.Pr...  36.2 us
    pallas_call x1, Pallas kernels, main_rows(): pl.pallas_call(functools.partial(main_kernel, tables, qu, iu), grid_spec=...  24.9 us
    ppermute x28, starting transfers between devices, swap(): return lax.ppermute(value, 'dap', [(d, d ^ bit) for d in range(size)])  21.9 us
    pallas_call x2, Pallas kernels, project(): pl.pallas_call(functools.partial(project_kernel, group), grid_spec=pltpu....  20.9 us
    pallas_call x1, Pallas kernels, main_late(): pl.pallas_call(main_late_kernel, grid=(seqs // block,), in_specs=[pl.Bloc...  13.8 us
    reduce_sum x1, other arithmetic, layer_norm(): var = jnp.mean(centered * centered, axis=-1, keepdims=True)  13.7 us
  transfers between devices with their start and end apart: 29, of which 10 were waited for; matrix products, arithmetic and copies ran while one was open for 17% of the time, Pallas kernels for 41%

profile of v6, /device:TPU:0, one launch (start us, length us, event | category | flops | bytes accessed | tf_op | source)
XLA Modules:
  0.0 420.0 jit_solution(5368449710436773356)
XLA Ops:
  3.5 3.3 collective-permute-start.10
  11.4 5.4 %turn.5 = (bf16[32,64,384]{2,1,0:T(8,128)(2,1)}, bf16[32,64,384]{2,1,0:T(8,128)(2,1)}, bf16[32,64,384]{2,1,0:T(8,128)(2,1)}, bf16[32,64,384]{2,1,0:T(8,128)(2,1)}) custom-call(s32[1]{0:T(128)} %bitcast.me_ref.idx_ref, bf16[32,64,3072]{2,1,0:T(8,128)(2,1)} %bitcast.47), custom_call_target="tpu_custom_call" | custom-call | flops 16777216 | bytes 4194304 | tf_op jit(solution)/shard_map/turn/pallas_call | solution.py:50
  19.9 5.7 %convert_reduce_fusion = f32[512,32]{1,0:T(8,128)S(1)} fusion(bf16[512,32,256]{2,1,0:T(8,128)(2,1)} %param.25), kind=kLoop, calls=%fused_computation.1 | loop fusion | flops 8372224 | bytes 8454144 | tf_op jit(solution)/shard_map/reduce_sum | solution.py:534
  25.7 16.6 %collective-permute-done.10.refs_1_.refs_2_ = bf16[32,64,384]{2,1,0:T(8,128)(2,1)S(1)} collective-permute-done((bf16[32,64,384]{2,1,0:T(8,128)(2,1)}, bf16[32,64,384]{2,1,0:T(8,128)(2,1)S(1)}, u32[]{:S(2)}, u32[]{:S(2)}) %collective-permute-start.10) | collective-permute-done | bytes 1572896 | tf_op jit(solution)/shard_map/ppermute | solution.py:24
  44.4 30.1 %collective-permute-done.12.refs_4_.refs_3_ = bf16[32,64,384]{2,1,0:T(8,128)(2,1)} collective-permute-done((bf16[32,64,384]{2,1,0:T(8,128)(2,1)}, bf16[32,64,384]{2,1,0:T(8,128)(2,1)}, u32[]{:S(2)}, u32[]{:S(2)}) %collective-permute-start.12) | collective-permute-done | bytes 1572896 | tf_op jit(solution)/shard_map/ppermute | solution.py:24
  76.1 14.1 %project.2 = (bf16[3,1024,384]{2,1,0:T(8,128)(2,1)}, bf16[3,1024,384]{2,1,0:T(8,128)(2,1)}, bf16[6,32,32,384]{3,2,1,0:T(8,128)(2,1)}) custom-call(s32[6]{0:T(128)S(1)} %broadcast_xor_fusion.1.idx_ref, bf16[32,64,384]{2,1,0:T(8,128)(2,1)S(1)} %copy-done.5, bf16[32,64,384]{2,1,0:T(8,128)(2,1)S(1)} %collective-permute-done.10.refs_1_.refs_2_, ...), custom_call_target="tpu_custom_call" | custom-call | flops 6442450944 | bytes 13631488 | tf_op jit(solution)/shard_map/project/pallas_call | solution.py:168
  93.4 13.7 %fusion.2 = f32[512,32]{1,0:T(8,128)S(1)} fusion(bf16[512,32,256]{2,1,0:T(8,128)(2,1)S(1)} %bitcast.49, f32[512,32]{1,0:T(8,128)S(1)} %broadcast_multiply_fusion), kind=kLoop, calls=%fused_computation.4 | loop fusion | flops 16760832 | bytes 8519680 | tf_op jit(solution)/shard_map/reduce_sum | solution.py:536
  107.2 7.7 %fusion.8 = f32[512,32,32]{2,1,0:T(8,128)} fusion(bf16[512,32,256]{2,1,0:T(8,128)(2,1)S(1)} %bitcast.49, f32[256]{0:T(256)S(1)} %convert_element_type.88, f32[256]{0:T(256)S(1)} %convert_element_type.87, f32[512,32]{1,0:T(8,128)S(1)} %add_rsqrt_fusion, f32[512,32]{1,0:T(8,128)S(1)} %broadcast_multiply_fusion, bf16[256,32]{0,1:T(8,128)(2,1)S(1)} %copy-done), kind=kOutput, calls=%fused_computation.9 | convolution fusion | flops 293601280 | bytes 10635264 | tf_op jit(solution)/shard_map/sim,mp->ips/dot_general | solution.py:584
  115.6 13.9 %collective-permute-done.14.refs_0_.refs_2_ = bf16[32,64,384]{2,1,0:T(8,128)(2,1)S(1)} collective-permute-done((bf16[32,64,384]{2,1,0:T(8,128)(2,1)}, bf16[32,64,384]{2,1,0:T(8,128)(2,1)S(1)}, u32[]{:S(2)}, u32[]{:S(2)}) %collective-permute-start.14) | collective-permute-done | bytes 1572896 | tf_op jit(solution)/shard_map/ppermute | solution.py:24
  129.5 31.9 %collective-permute-done.15.refs_1_.refs_3_ = bf16[32,64,384]{2,1,0:T(8,128)(2,1)} collective-permute-done((bf16[32,64,384]{2,1,0:T(8,128)(2,1)}, bf16[32,64,384]{2,1,0:T(8,128)(2,1)}, u32[]{:S(2)}, u32[]{:S(2)}) %collective-permute-start.15) | collective-permute-done | bytes 1572896 | tf_op jit(solution)/shard_map/ppermute | solution.py:24
  161.4 6.8 %project.3 = (bf16[1,1024,384]{2,1,0:T(8,128)(2,1)S(1)}, bf16[1,1024,384]{2,1,0:T(8,128)(2,1)S(1)}, bf16[2,32,32,384]{3,2,1,0:T(8,128)(2,1)}) custom-call(s32[2]{0:T(128)S(1)} %broadcast_xor_fusion.idx_ref, bf16[32,64,384]{2,1,0:T(8,128)(2,1)} %copy-done.9, bf16[32,64,384]{2,1,0:T(8,128)(2,1)} %collective-permute-done.15.refs_1_.refs_3_, ...), custom_call_target="tpu_custom_call" | custom-call | flops 6442450944 | bytes 13631488 | tf_op jit(solution)/shard_map/project/pallas_call | solution.py:168
  169.1 3.9 all-to-all-start
  173.0 10.5 %fusion.6 = f32[512,32,32]{2,1,0:T(8,128)} fusion(bf16[512,32,256]{2,1,0:T(8,128)(2,1)} %param.25, f32[256]{0:T(256)S(1)} %convert_element_type.88, f32[256]{0:T(256)S(1)} %convert_element_type.87, f32[512,32]{1,0:T(8,128)S(1)} %add_rsqrt_fusion, f32[512,32]{1,0:T(8,128)S(1)} %broadcast_multiply_fusion, bf16[256,32]{0,1:T(8,128)(2,1)S(1)} %copy-done.6), kind=kOutput, calls=%fused_computation.8 | convolution fusion | flops 293601280 | bytes 10635264 | tf_op jit(solution)/shard_map/sim,mq->qis/dot_general | solution.py:586
  184.4 5.3 %copy.54 = f32[512,32,32]{0,2,1:T(8,128)S(1)} copy(f32[512,32,32]{2,1,0:T(8,128)} %fusion.8) | data formatting | bytes 4194304 | tf_op jit(solution)/shard_map/sim,mp->ips/dot_general | solution.py:584
  189.7 6.6 %copy.56 = f32[512,32,32]{0,1,2:T(8,128)} copy(f32[512,32,32]{2,1,0:T(8,128)} %fusion.6) | data formatting | bytes 4194304 | tf_op jit(solution)/shard_map/sim,mq->qis/dot_general | solution.py:586
  196.3 3.2 fusion.10
  207.6 72.3 %extra_outer.1 = (bf16[16,128,256]{2,1,0:T(8,128)(2,1)}, bf16[16,128,256]{2,1,0:T(8,128)(2,1)}, bf16[16,128,256]{2,1,0:T(8,128)(2,1)}, bf16[16,128,256]{2,1,0:T(...) custom-call(s32[1]{0:T(128)} %bitcast.me_ref.idx_ref, ...), custom_call_target="tpu_custom_call" | custom-call | flops 64424509440 | bytes 33554432 | tf_op jit(solution)/shard_map/extra_outer/pallas_call | solution.py:317
  287.9 13.8 %main_late.1.refs_12_ = bf16[32,64,256]{2,1,0:T(8,128)(2,1)} custom-call(bf16[8,64,32,256]{3,2,1,0:T(8,128)(2,1)} %bitcast.8.x_ref.ref, f32[64,256]{1,0:T(8,128)S(1)} %dynamic-slice_convert_fusion.4.mask_ref, f32[1,256]{1,0:T(1,128)S(1)} %bitcast.44, f32[1,256]{1,0:T(1,128)S(1)} %bitcast.43, bf16[32,256]{1,0:T(8,128)(2,1)S(1)} %bitcast.42, ...), custom_call_target="tpu_custom_call" | custom-call | flops 4294967296 | bytes 10485760 | tf_op jit(solution)/shard_map/main_late/pallas_call | solution.py:369
  302.6 14.0 %collective-permute-done.6.refs_8_ = bf16[48,32,128]{2,1,0:T(8,128)(2,1)} collective-permute-done((bf16[48,32,128]{2,1,0:T(8,128)(2,1)}, bf16[48,32,128]{2,1,0:T(8,128)(2,1)}, u32[]{:S(2)}, u32[]{:S(2)}) %collective-permute-start.6) | collective-permute-done | bytes 393248 | tf_op jit(solution)/shard_map/ppermute | solution.py:24
  317.4 18.0 %turn_out.2.refs_4_ = bf16[384,64,256]{2,1,0:T(8,128)(2,1)} custom-call(s32[1]{0:T(128)} %bitcast.me_ref.idx_ref, bf16[32,64,384]{2,1,0:T(8,128)(2,1)} %get-tuple-element.42.refs_0_, bf16[32,64,384]{2,1,0:T(8,128)(2,1)} %collective-permute-done.17.refs_3_.refs_1_, bf16[32,64,384]{2,1,0:T(8,128)(2,1)} %copy-done.4, ...), custom_call_target="tpu_custom_call" | custom-call | flops 16777216 | bytes 13631488 | tf_op jit(solution)/shard_map/turn_out/pallas_call | solution.py:85
  335.4 18.2 %turn_out.3 = bf16[384,64,256]{2,1,0:T(8,128)(2,1)} custom-call(s32[1]{0:T(128)} %bitcast.me_ref.idx_ref, bf16[32,64,384]{2,1,0:T(8,128)(2,1)} %collective-permute-done.11.refs_2_.refs_0_, bf16[32,64,384]{2,1,0:T(8,128)(2,1)} %collective-permute-done.13.refs_5_.refs_1_, bf16[32,64,384]{2,1,0:T(8,128)(2,1)} %copy-done.9, ...), custom_call_target="tpu_custom_call", output_to_operand_aliasing={{}: (5, {})} | custom-call | flops 16777216 | bytes 13631488 | tf_op jit(solution)/shard_map/turn_out/pallas_call | solution.py:85
  359.9 9.0 %assemble.1 = bf16[64,256,256]{2,1,0:T(8,128)(2,1)} custom-call(bf16[8,64,32,256]{3,2,1,0:T(8,128)(2,1)} %bitcast.8.x_ref.ref), custom_call_target="tpu_custom_call" | custom-call | flops 16777216 | bytes 16777216 | tf_op jit(solution)/shard_map/assemble/pallas_call | solution.py:521
  373.0 24.9 %main_outer.1.base_ref = f32[32,256,128]{2,1,0:T(8,128)} custom-call(s32[1]{0:T(128)} %bitcast.me_ref.idx_ref, bf16[1024,512]{1,0:T(8,128)(2,1)} %bitcast.53, bf16[96,32,128]{2,1,0:T(8,128)(2,1)S(1)} %get-tuple-element.68.refs_0_, bf16[96,32,128]{2,1,0:T(8,128)(2,1)S(1)} %get-tuple-element.67.refs_1_, bf16[96,32,128]{2,1,0:T(8,128)(2,1)S(1)} %collective-permute-done.refs_2_, ...), custom_call_target="tpu_custom_call" | custom-call | flops 12884901888 | bytes 20971520 | tf_op jit(solution)/shard_map/main_outer/pallas_call | solution.py:443
  401.5 15.2 %collective-permute-done.27.upper_ref = bf16[16,128,256]{2,1,0:T(8,128)(2,1)S(1)} collective-permute-done((bf16[16,128,256]{2,1,0:T(8,128)(2,1)}, bf16[16,128,256]{2,1,0:T(8,128)(2,1)S(1)}, u32[]{:S(2)}, u32[]{:S(2)}) %collective-permute-start.27) | collective-permute-done | bytes 1048608 | tf_op jit(solution)/shard_map/ppermute | solution.py:24
  (155 shorter events, 54.7 us)
Async XLA Ops:
  3.5 38.8 %collective-permute-start.10 = (bf16[32,64,384]{2,1,0:T(8,128)(2,1)}, bf16[32,64,384]{2,1,0:T(8,128)(2,1)S(1)}, u32[]{:S(2)}, u32[]{:S(2)}) collective-permute-start(bf16[32,64,384]{2,1,0:T(8,128)(2,1)} %get-tuple-element.33), channel_id=1, source_target_pairs={{0,2},{1,3},{2,0},{3,1},{4,6},{5,7},{6,4},{7,5}} | collective-permute-start | bytes 4718600 | tf_op jit(solution)/shard_map/ppermute | solution.py:24
  6.8 37.6 %collective-permute-start.11 = (bf16[32,64,384]{2,1,0:T(8,128)(2,1)}, bf16[32,64,384]{2,1,0:T(8,128)(2,1)}, u32[]{:S(2)}, u32[]{:S(2)}) collective-permute-start(bf16[32,64,384]{2,1,0:T(8,128)(2,1)} %get-tuple-element.34), channel_id=1, source_target_pairs={{0,4},{1,5},{2,6},{3,7},{4,0},{5,1},{6,2},{7,3}} | collective-permute-start | bytes 4718600 | tf_op jit(solution)/shard_map/ppermute | solution.py:24
  11.2 63.3 %collective-permute-start.12 = (bf16[32,64,384]{2,1,0:T(8,128)(2,1)}, bf16[32,64,384]{2,1,0:T(8,128)(2,1)}, u32[]{:S(2)}, u32[]{:S(2)}) collective-permute-start(bf16[32,64,384]{2,1,0:T(8,128)(2,1)} %get-tuple-element.35), channel_id=1, source_target_pairs={{0,3},{1,2},{2,1},{3,0},{4,7},{5,6},{6,5},{7,4}} | collective-permute-start | bytes 4718600 | tf_op jit(solution)/shard_map/ppermute | solution.py:24
  11.2 64.5 %collective-permute-start.13 = (bf16[32,64,384]{2,1,0:T(8,128)(2,1)}, bf16[32,64,384]{2,1,0:T(8,128)(2,1)}, u32[]{:S(2)}, u32[]{:S(2)}) collective-permute-start(bf16[32,64,384]{2,1,0:T(8,128)(2,1)} %get-tuple-element.36), channel_id=1, source_target_pairs={{0,5},{1,4},{2,7},{3,6},{4,1},{5,0},{6,3},{7,2}} | collective-permute-start | bytes 4718600 | tf_op jit(solution)/shard_map/ppermute | solution.py:24
  16.9 58.8 %collective-permute-start.17 = (bf16[32,64,384]{2,1,0:T(8,128)(2,1)}, bf16[32,64,384]{2,1,0:T(8,128)(2,1)}, u32[]{:S(2)}, u32[]{:S(2)}) collective-permute-start(bf16[32,64,384]{2,1,0:T(8,128)(2,1)} %get-tuple-element.45), channel_id=1, source_target_pairs={{0,1},{1,0},{2,3},{3,2},{4,5},{5,4},{6,7},{7,6}} | collective-permute-start | bytes 4718600 | tf_op jit(solution)/shard_map/ppermute | solution.py:24
  90.2 117.4 %collective-permute-start.20 = (bf16[6,32,32,384]{3,2,1,0:T(8,128)(2,1)}, bf16[6,32,32,384]{3,2,1,0:T(8,128)(2,1)}, u32[]{:S(2)}, u32[]{:S(2)}) collective-permute-start(bf16[6,32,32,384]{3,2,1,0:T(8,128)(2,1)} %get-tuple-element.54.refs_4_), channel_id=1, source_target_pairs={{0,1},{1,0},{2,3},{3,2},{4,5},{5,4},{6,7},{7,6}} | collective-permute-start | bytes 14155784 | tf_op jit(solution)/shard_map/ppermute | solution.py:24
  91.1 38.4 %collective-permute-start.14 = (bf16[32,64,384]{2,1,0:T(8,128)(2,1)}, bf16[32,64,384]{2,1,0:T(8,128)(2,1)S(1)}, u32[]{:S(2)}, u32[]{:S(2)}) collective-permute-start(bf16[32,64,384]{2,1,0:T(8,128)(2,1)} %get-tuple-element.39), channel_id=1, source_target_pairs={{0,6},{1,7},{2,4},{3,5},{4,2},{5,3},{6,0},{7,1}} | collective-permute-start | bytes 4718600 | tf_op jit(solution)/shard_map/ppermute | solution.py:24
  92.6 68.8 %collective-permute-start.15 = (bf16[32,64,384]{2,1,0:T(8,128)(2,1)}, bf16[32,64,384]{2,1,0:T(8,128)(2,1)}, u32[]{:S(2)}, u32[]{:S(2)}) collective-permute-start(bf16[32,64,384]{2,1,0:T(8,128)(2,1)} %get-tuple-element.40), channel_id=1, source_target_pairs={{0,7},{1,6},{2,5},{3,4},{4,3},{5,2},{6,1},{7,0}} | collective-permute-start | bytes 4718600 | tf_op jit(solution)/shard_map/ppermute | solution.py:24
  114.9 91.2 %collective-permute-start.18 = (bf16[3,1024,384]{2,1,0:T(8,128)(2,1)}, bf16[3,1024,384]{2,1,0:T(8,128)(2,1)}, u32[]{:S(2)}, u32[]{:S(2)}) collective-permute-start(bf16[3,1024,384]{2,1,0:T(8,128)(2,1)} %get-tuple-element.49), channel_id=1, source_target_pairs={{0,1},{1,0},{2,3},{3,2},{4,5},{5,4},{6,7},{7,6}} | collective-permute-start | bytes 7077896 | tf_op jit(solution)/shard_map/ppermute | solution.py:24
  168.2 39.3 %collective-permute-start.21 = (bf16[2,32,32,384]{3,2,1,0:T(8,128)(2,1)}, bf16[2,32,32,384]{3,2,1,0:T(8,128)(2,1)}, u32[]{:S(2)}, u32[]{:S(2)}) collective-permute-start(bf16[2,32,32,384]{3,2,1,0:T(8,128)(2,1)} %get-tuple-element.55.refs_6_), channel_id=1, source_target_pairs={{0,1},{1,0},{2,3},{3,2},{4,5},{5,4},{6,7},{7,6}} | collective-permute-start | bytes 4718600 | tf_op jit(solution)/shard_map/ppermute | solution.py:24
  169.1 118.8 %all-to-all-start = ((bf16[512,32,256]{2,1,0:T(8,128)(2,1)}), bf16[512,32,256]{2,1,0:T(8,128)(2,1)}, u32[]{:S(2)}, u32[]{:S(2)}) async-start(bf16[512,32,256]{2,1,0:T(8,128)(2,1)} %param.25), calls=%async_computation | async-start | bytes 16777216 | tf_op jit(solution)/shard_map/all_to_all | solution.py:603
  200.0 85.8 %collective-permute-start = (bf16[96,32,128]{2,1,0:T(8,128)(2,1)S(1)}, bf16[96,32,128]{2,1,0:T(8,128)(2,1)S(1)}, u32[]{:S(2)}, u32[]{:S(2)}) collective-permute-start(bf16[96,32,128]{2,1,0:T(8,128)(2,1)S(1)} %get-tuple-element.68.refs_0_), channel_id=1, source_target_pairs={{0,2},{1,3},{2,0},{3,1},{4,6},{5,7},{6,4},{7,5}} | collective-permute-start | bytes 2359304 | tf_op jit(solution)/shard_map/ppermute | solution.py:24
  205.9 81.5 %collective-permute-start.2 = (bf16[96,32,128]{2,1,0:T(8,128)(2,1)S(1)}, bf16[96,32,128]{2,1,0:T(8,128)(2,1)}, u32[]{:S(2)}, u32[]{:S(2)}) collective-permute-start(bf16[96,32,128]{2,1,0:T(8,128)(2,1)S(1)} %get-tuple-element.68.refs_0_), channel_id=1, source_target_pairs={{0,1},{1,0},{2,3},{3,2},{4,5},{5,4},{6,7},{7,6}} | collective-permute-start | bytes 2359304 | tf_op jit(solution)/shard_map/ppermute | solution.py:24
  206.0 76.9 %collective-permute-start.1 = (bf16[96,32,128]{2,1,0:T(8,128)(2,1)S(1)}, bf16[96,32,128]{2,1,0:T(8,128)(2,1)S(1)}, u32[]{:S(2)}, u32[]{:S(2)}) collective-permute-start(bf16[96,32,128]{2,1,0:T(8,128)(2,1)S(1)} %get-tuple-element.67.refs_1_), channel_id=1, source_target_pairs={{0,4},{1,5},{2,6},{3,7},{4,0},{5,1},{6,2},{7,3}} | collective-permute-start | bytes 2359304 | tf_op jit(solution)/shard_map/ppermute | solution.py:24
  207.5 94.2 %collective-permute-start.3 = (bf16[96,32,128]{2,1,0:T(8,128)(2,1)S(1)}, bf16[96,32,128]{2,1,0:T(8,128)(2,1)}, u32[]{:S(2)}, u32[]{:S(2)}) collective-permute-start(bf16[96,32,128]{2,1,0:T(8,128)(2,1)S(1)} %get-tuple-element.67.refs_1_), channel_id=1, source_target_pairs={{0,1},{1,0},{2,3},{3,2},{4,5},{5,4},{6,7},{7,6}} | collective-permute-start | bytes 2359304 | tf_op jit(solution)/shard_map/ppermute | solution.py:24
  280.0 73.7 %collective-permute-start.26 = (bf16[16,128,256]{2,1,0:T(8,128)(2,1)}, bf16[16,128,256]{2,1,0:T(8,128)(2,1)}, u32[]{:S(2)}, u32[]{:S(2)}) collective-permute-start(bf16[16,128,256]{2,1,0:T(8,128)(2,1)} %get-tuple-element.62), channel_id=1, source_target_pairs={{0,4},{1,5},{2,6},{3,7},{4,0},{5,1},{6,2},{7,3}} | collective-permute-start | bytes 3145736 | tf_op jit(solution)/shard_map/ppermute | solution.py:24
  283.0 70.7 %collective-permute-start.24 = (bf16[16,128,256]{2,1,0:T(8,128)(2,1)}, bf16[16,128,256]{2,1,0:T(8,128)(2,1)}, u32[]{:S(2)}, u32[]{:S(2)}) collective-permute-start(bf16[16,128,256]{2,1,0:T(8,128)(2,1)} %get-tuple-element.60), channel_id=1, source_target_pairs={{0,2},{1,3},{2,0},{3,1},{4,6},{5,7},{6,4},{7,5}} | collective-permute-start | bytes 3145736 | tf_op jit(solution)/shard_map/ppermute | solution.py:24
  285.8 30.8 %collective-permute-start.6 = (bf16[48,32,128]{2,1,0:T(8,128)(2,1)}, bf16[48,32,128]{2,1,0:T(8,128)(2,1)}, u32[]{:S(2)}, u32[]{:S(2)}) collective-permute-start(bf16[48,32,128]{2,1,0:T(8,128)(2,1)} %slice.8), channel_id=1, source_target_pairs={{0,2},{1,3},{2,0},{3,1},{4,6},{5,7},{6,4},{7,5}} | collective-permute-start | bytes 1179656 | tf_op jit(solution)/shard_map/ppermute | solution.py:24
  287.4 29.2 %collective-permute-start.7 = (bf16[48,32,128]{2,1,0:T(8,128)(2,1)}, bf16[48,32,128]{2,1,0:T(8,128)(2,1)}, u32[]{:S(2)}, u32[]{:S(2)}) collective-permute-start(bf16[48,32,128]{2,1,0:T(8,128)(2,1)} %slice.9), channel_id=1, source_target_pairs={{0,4},{1,5},{2,6},{3,7},{4,0},{5,1},{6,2},{7,3}} | collective-permute-start | bytes 1179656 | tf_op jit(solution)/shard_map/ppermute | solution.py:24
  301.8 71.2 %collective-permute-start.16 = (bf16[32,64,256]{2,1,0:T(8,128)(2,1)}, bf16[32,64,256]{2,1,0:T(8,128)(2,1)}, u32[]{:S(2)}, u32[]{:S(2)}) collective-permute-start(bf16[32,64,256]{2,1,0:T(8,128)(2,1)} %main_late.1.refs_12_), channel_id=1, source_target_pairs={{0,1},{1,0},{2,3},{3,2},{4,5},{5,4},{6,7},{7,6}} | collective-permute-start | bytes 3145736 | tf_op jit(solution)/shard_map/ppermute | solution.py:24
  316.6 53.9 %collective-permute-start.4 = (bf16[96,32,128]{2,1,0:T(8,128)(2,1)S(1)}, bf16[96,32,128]{2,1,0:T(8,128)(2,1)}, u32[]{:S(2)}, u32[]{:S(2)}) collective-permute-start(bf16[96,32,128]{2,1,0:T(8,128)(2,1)S(1)} %collective-permute-done.refs_2_), channel_id=1, source_target_pairs={{0,1},{1,0},{2,3},{3,2},{4,5},{5,4},{6,7},{7,6}} | collective-permute-start | bytes 2359304 | tf_op jit(solution)/shard_map/ppermute | solution.py:24
  316.6 55.0 %collective-permute-start.5 = (bf16[96,32,128]{2,1,0:T(8,128)(2,1)S(1)}, bf16[96,32,128]{2,1,0:T(8,128)(2,1)}, u32[]{:S(2)}, u32[]{:S(2)}) collective-permute-start(bf16[96,32,128]{2,1,0:T(8,128)(2,1)S(1)} %collective-permute-done.1.refs_3_), channel_id=1, source_target_pairs={{0,1},{1,0},{2,3},{3,2},{4,5},{5,4},{6,7},{7,6}} | collective-permute-start | bytes 2359304 | tf_op jit(solution)/shard_map/ppermute | solution.py:24
  370.5 46.2 %collective-permute-start.27 = (bf16[16,128,256]{2,1,0:T(8,128)(2,1)}, bf16[16,128,256]{2,1,0:T(8,128)(2,1)S(1)}, u32[]{:S(2)}, u32[]{:S(2)}) collective-permute-start(bf16[16,128,256]{2,1,0:T(8,128)(2,1)} %add_convert_fusion), channel_id=1, source_target_pairs={{0,2},{1,3},{2,0},{3,1},{4,6},{5,7},{6,4},{7,5}} | collective-permute-start | bytes 3145736 | tf_op jit(solution)/shard_map/ppermute | solution.py:24
  371.6 45.8 %collective-permute-start.25 = (bf16[16,128,256]{2,1,0:T(8,128)(2,1)}, bf16[16,128,256]{2,1,0:T(8,128)(2,1)S(1)}, u32[]{:S(2)}, u32[]{:S(2)}) collective-permute-start(bf16[16,128,256]{2,1,0:T(8,128)(2,1)} %add_convert_fusion.1), channel_id=1, source_target_pairs={{0,4},{1,5},{2,6},{3,7},{4,0},{5,1},{6,2},{7,3}} | collective-permute-start | bytes 3145736 | tf_op jit(solution)/shard_map/ppermute | solution.py:24
  (33 other events, 729.4 us)
